TPU v7x, 32 devices: a whole 2x2x4 slice. The times are simulated.
32 devices in a mesh: sec: 8 (over y, x, core), env: 4 (over z).
Axes of the slice: x: 2, y: 2, z: 4, core: 2. Of those that a mesh axis runs over, the one named last changes fastest.
Arguments:
- wavefunction: float32 [8, 512, 512], P('sec', 'env'), may hold values from -14 to 14
- left_env: bfloat16 [34, 512, 512], P(None, 'env'), may hold values from -0.176776695 to 0.176776695
- right_env: bfloat16 [34, 512, 512], P(None, 'env'), may hold values from -0.25 to 0.25
- task_in: int32 [32], replicated, may hold values from 0 to 7
- task_out: int32 [32, 1], replicated, may hold values from 0 to 7; in each aligned block of 32 rows (0 to 31, 32 to 63, ...) at most 16 rows name the same one
- task_term: int32 [32], replicated, may hold values from 0 to 33
Outputs:
- sigma: float32 [8, 512, 512], P('sec', 'env')
Inputs may be any that keep to these rules, and one draw needn't show every extreme that they name: `task_out`: no sector is the target of more than 16 tasks, and in every draw some sector is the target of exactly 16.
All inputs are finite; a program needn't handle non-finite values.
Results may differ from a plain program's by a relative error of at most 0.00045.
Values may be sent and summed in bfloat16 or wider, within the bound.
No kernel may reach another device: no remote copies, remote signals or barrier semaphores. Data moves between devices by JAX's collectives and lax.ppermute only.
A program may use at most 64 MiB of HBM per device.

v0:
```python
import functools

import jax
import jax.numpy as jnp
from jax import lax
from jax.experimental import pallas as pl
from jax.experimental.pallas import tpu as pltpu
from jax.sharding import PartitionSpec as P


VMEM_BYTES = 16 * 1024 * 1024
VMEM = pl.BlockSpec(memory_space=pltpu.VMEM)
SMEM = pl.BlockSpec(memory_space=pltpu.SMEM)
HBM = pl.BlockSpec(memory_space=pltpu.HBM)


def call(kernel, out_shape, in_specs, scratch=(), flops=1, moved=1):
    return pl.pallas_call(
        kernel,
        out_shape=out_shape,
        in_specs=in_specs,
        out_specs=jax.tree.map(lambda _: VMEM, out_shape),
        scratch_shapes=list(scratch),
        cost_estimate=pl.CostEstimate(flops=flops, bytes_accessed=moved, transcendentals=0),
        compiler_params=pltpu.CompilerParams(vmem_limit_bytes=VMEM_BYTES),
    )


def pick_terms_kernel(base, me, count, term_ref, left_ref, right_ref, *rest):
    outs, sem = rest[:count], rest[count]
    copies = []
    start, mine = base(), me()
    for step in range(count):
        term = term_ref[start + lax.rem(mine + step, count)]
        copies.append(pltpu.make_async_copy(left_ref.at[term], outs[step].at[0], sem.at[2 * step]))
        copies.append(pltpu.make_async_copy(right_ref.at[term], outs[step].at[1], sem.at[2 * step + 1]))
    for copy in copies:
        copy.start()
    for copy in copies:
        copy.wait()


def partner_psi_kernel(base, sec, count, chips, in_ref, *rest):
    held, out = rest[:chips], rest[chips]
    start = base()
    chip, core = sec() // 2, lax.rem(sec(), 2)
    for slot in range(count):
        source = in_ref[start + slot]
        for step in range(chips):
            @pl.when((source // 2 == chip ^ step) & (lax.rem(source, 2) == core))
            def _():
                out[slot] = held[step][...]


def own_psi_kernel(base, sec, me, count, chips, in_ref, *rest):
    held, paired, outs = rest[:chips], rest[chips], rest[chips + 1 :]
    start, mine = base(), me()
    chip, core = sec() // 2, lax.rem(sec(), 2)
    for step in range(count):
        slot = lax.rem(mine + step, count)
        source = in_ref[start + slot]
        same = lax.rem(source, 2) == core
        for hop in range(chips):
            @pl.when((source // 2 == chip ^ hop) & same)
            def _():
                outs[step][...] = held[hop][...]

        @pl.when(jnp.logical_not(same))
        def _():
            outs[step][...] = paired[slot]


def task_kernel(me, count, *refs):
    envs, psis, outs = refs[:count], refs[count : 2 * count], refs[2 * count : 3 * count]
    high, low, right = refs[3 * count :]
    rows = psis[0].shape[0]
    mine = me()
    for step in range(count):
        place = pl.ds(pl.multiple_of(lax.rem(mine + count - step, count) * rows, rows), rows)
        right[place, :] = envs[step][1]
        psi = psis[step][...]
        top = psi.astype(jnp.bfloat16)
        high[place, :] = top
        low[place, :] = (psi - top.astype(jnp.float32)).astype(jnp.bfloat16)
    mixed = jnp.dot(high[...], right[...], preferred_element_type=jnp.float32) + jnp.dot(
        low[...], right[...], preferred_element_type=jnp.float32
    )
    top = mixed.astype(jnp.bfloat16)
    high[...] = top
    low[...] = (mixed - top.astype(jnp.float32)).astype(jnp.bfloat16)
    for step in range(count):
        left = envs[(count - step) % count][0]
        outs[step][...] = jnp.dot(left, high[...], preferred_element_type=jnp.float32) + jnp.dot(
            left, low[...], preferred_element_type=jnp.float32
        )


def combine_kernel(base, sec, me, count, chips, target_ref, *rest):
    parts, keeps, send = rest[:count], rest[count : count + chips], rest[count + chips]
    start, mine = base(), me()
    chip, core = sec() // 2, lax.rem(sec(), 2)
    targets = [target_ref[start + lax.rem(mine + count - step, count)] for step in range(count)]
    for hop in range(chips):
        for out, owner in ((keeps[hop], core), (send.at[hop], 1 - core)):
            wanted = (chip ^ hop) * 2 + owner
            total = jnp.zeros(parts[0].shape, jnp.float32)
            for step in range(count):
                total = total + jnp.where(targets[step] == wanted, parts[step][...], 0.0)
            out[...] = total


def body(wavefunction, left_env, right_env, task_in, task_out, task_term):
    groups, count = lax.axis_size("sec"), lax.axis_size("env")
    chips = groups // 2
    _, rows, cols = wavefunction.shape
    per_device = task_in.shape[0] // (groups * count)
    targets = task_out[:, 0]
    f32, bf16 = jnp.float32, jnp.bfloat16
    block = jax.ShapeDtypeStruct((rows, cols), f32)
    sec = lambda: lax.axis_index("sec")
    me = lambda: lax.axis_index("env")

    def along(shift):
        return [(i, (i + shift) % count) for i in range(count)]

    def across(hop):
        return [(i, i ^ (2 * hop)) for i in range(groups)]

    pair = [(i, i ^ 1) for i in range(groups)]
    psi = wavefunction[0]
    held = [psi] + [lax.ppermute(psi, "sec", across(hop)) for hop in range(1, chips)]

    keeps, sends = None, None
    for turn in range(per_device):
        base = lambda: (sec() * per_device + turn) * count
        partner_base = lambda: ((sec() ^ 1) * per_device + turn) * count
        env_block = jax.ShapeDtypeStruct((2, rows, cols), bf16)
        envs = call(
            functools.partial(pick_terms_kernel, base, me, count),
            [env_block] * count,
            [SMEM, HBM, HBM],
            [pltpu.SemaphoreType.DMA((2 * count,))],
        )(task_term, left_env, right_env)
        envs = [envs[0]] + [lax.ppermute(envs[s], "env", along(s)) for s in range(1, count)]
        sent = call(
            functools.partial(partner_psi_kernel, partner_base, sec, count, chips),
            jax.ShapeDtypeStruct((count, rows, cols), f32),
            [SMEM] + [VMEM] * chips,
        )(task_in, *held)
        paired = lax.ppermute(sent, "sec", pair)
        psis = call(
            functools.partial(own_psi_kernel, base, sec, me, count, chips),
            [block] * count,
            [SMEM] + [VMEM] * (chips + 1),
        )(task_in, *held, paired)
        psis = [psis[0]] + [lax.ppermute(psis[s], "env", along(s)) for s in range(1, count)]
        full = count * rows
        parts = call(
            functools.partial(task_kernel, me, count),
            [block] * count,
            [VMEM] * (2 * count),
            [pltpu.VMEM((full, cols), bf16)] * 3,
            flops=8 * full * full * cols,
        )(*envs, *psis)
        parts = [parts[0]] + [lax.ppermute(parts[s], "env", along(s)) for s in range(1, count)]
        *kept, send = call(
            functools.partial(combine_kernel, base, sec, me, count, chips),
            [block] * chips + [jax.ShapeDtypeStruct((chips, rows, cols), f32)],
            [SMEM] + [VMEM] * count,
        )(targets, *parts)
        keeps = kept if keeps is None else [a + b for a, b in zip(keeps, kept)]
        sends = send if sends is None else sends + send
    other = lax.ppermute(sends, "sec", pair)
    sums = [keeps[hop] + other[hop] for hop in range(chips)]
    total = sums[0]
    for hop in range(1, chips):
        total = total + lax.ppermute(sums[hop], "sec", across(hop))
    return total[None]


def solution(mesh):
    placed = (P("sec", "env", None), P(None, "env", None), P(None, "env", None), P(), P(), P())
    return jax.shard_map(
        body, mesh=mesh, in_specs=placed, out_specs=P("sec", "env", None), check_vma=False
    )
```

profile of v0, /device:TPU:8, one launch (start us, length us, event | category | flops | bytes accessed | tf_op | source)
XLA Modules:
  0.0 119.8 jit_solution(16609008648055100905)
XLA Ops:
  0.0 1.5 %collective-permute-start.3 = (f32[128,512]{1,0:T(8,128)}, f32[128,512]{1,0:T(8,128)S(1)}, u32[]{:S(2)}, u32[]{:S(2)}) collective-permute-start(f32[128,512]{1,0:T(8,128)} %bitcast.28), channel_id=1, source_target_pairs={{0,8},{4,12},{8,0},{12,4},{16,24},{20,28},{24,16},{28,20},{1,9},{5... | collective-permute-start | bytes 786440 | tf_op jit(solution)/shard_map/ppermute | solution.py:131
  1.5 1.5 %collective-permute-start.4 = (f32[128,512]{1,0:T(8,128)}, f32[128,512]{1,0:T(8,128)S(1)}, u32[]{:S(2)}, u32[]{:S(2)}) collective-permute-start(f32[128,512]{1,0:T(8,128)} %bitcast.29), channel_id=1, source_target_pairs={{0,16},{4,20},{8,24},{12,28},{16,0},{20,4},{24,8},{28,12},{1,17},{... | collective-permute-start | bytes 786440 | tf_op jit(solution)/shard_map/ppermute | solution.py:131
  3.0 0.5 collective-permute-start.5
  3.5 5.9 %collective-permute-done.3.rest_1_ = f32[128,512]{1,0:T(8,128)S(1)} collective-permute-done((f32[128,512]{1,0:T(8,128)}, f32[128,512]{1,0:T(8,128)S(1)}, u32[]{:S(2)}, u32[]{:S(2)}) %collective-permute-start.3) | collective-permute-done | bytes 262176 | tf_op jit(solution)/shard_map/ppermute | solution.py:131
  9.4 5.7 %collective-permute-done.4.rest_2_ = f32[128,512]{1,0:T(8,128)S(1)} collective-permute-done((f32[128,512]{1,0:T(8,128)}, f32[128,512]{1,0:T(8,128)S(1)}, u32[]{:S(2)}, u32[]{:S(2)}) %collective-permute-start.4) | collective-permute-done | bytes 262176 | tf_op jit(solution)/shard_map/ppermute | solution.py:131
  15.1 0.0 collective-permute-done.5.rest_3_
  15.1 0.9 copy-done.2
  16.0 0.7 copy-done.4
  16.7 0.7 shard_map.65
  17.4 0.1 collective-permute-start.6
  17.5 0.0 copy-start
  17.5 2.3 %copy-done = bf16[34,128,512]{2,1,0:T(8,128)(2,1)S(1)} copy-done((bf16[34,128,512]{2,1,0:T(8,128)(2,1)S(1)}, bf16[34,128,512]{2,1,0:T(8,128)(2,1)}, u32[]{:S(2)}) %copy-start) | copy-done | bytes 4456472
  19.8 2.3 %copy-done.1 = bf16[34,128,512]{2,1,0:T(8,128)(2,1)S(1)} copy-done((bf16[34,128,512]{2,1,0:T(8,128)(2,1)S(1)}, bf16[34,128,512]{2,1,0:T(8,128)(2,1)}, u32[]{:S(2)}) %copy-start.1) | copy-done | bytes 4456472
  22.0 0.7 copy-done.6
  22.7 2.0 %shard_map.64 = (bf16[2,128,512]{2,1,0:T(8,128)(2,1)S(1)}, bf16[2,128,512]{2,1,0:T(8,128)(2,1)S(1)}, bf16[2,128,512]{2,1,0:T(8,128)(2,1)S(1)}, bf16[2,128,512]{2,1,0:T(8,128)(2,1)S(1)}) custom-call(s32[32]{0:T(128)S(1)} %copy-done.6, bf16[34,128,512]{2,1,0:T(8,128)(2,1)S(1)} %copy-done, bf16[34,128,512]{2,1,0:T(8,128)(2,1)S(1)} %copy-done.1), custom_call_target="tpu_custom_call" | custom-call | flops 1 | bytes 1 | tf_op jit(solution)/shard_map/pallas_call | solution.py:138
  24.7 0.0 copy-start.7
  24.7 1.6 %collective-permute-start = (bf16[2,128,512]{2,1,0:T(8,128)(2,1)S(1)}, bf16[2,128,512]{2,1,0:T(8,128)(2,1)S(1)}, u32[]{:S(2)}, u32[]{:S(2)}) collective-permute-start(bf16[2,128,512]{2,1,0:T(8,128)(2,1)S(1)} %get-tuple-element.23), channel_id=1, source_target_pairs={{0,1},{1,2},{2,3},{3,0},{4,5},{5,6},{6,7},{7,4},{8,9},{9,10},{10,1... | collective-permute-start | bytes 786440 | tf_op jit(solution)/shard_map/ppermute | solution.py:144
  26.3 1.2 %collective-permute-start.1 = (bf16[2,128,512]{2,1,0:T(8,128)(2,1)S(1)}, bf16[2,128,512]{2,1,0:T(8,128)(2,1)S(1)}, u32[]{:S(2)}, u32[]{:S(2)}) collective-permute-start(bf16[2,128,512]{2,1,0:T(8,128)(2,1)S(1)} %get-tuple-element.24), channel_id=1, source_target_pairs={{0,2},{1,3},{2,0},{3,1},{4,6},{5,7},{6,4},{7,5},{8,10},{9,11},{10,... | collective-permute-start | bytes 786440 | tf_op jit(solution)/shard_map/ppermute | solution.py:144
  27.6 1.8 %collective-permute-start.2 = (bf16[2,128,512]{2,1,0:T(8,128)(2,1)S(1)}, bf16[2,128,512]{2,1,0:T(8,128)(2,1)S(1)}, u32[]{:S(2)}, u32[]{:S(2)}) collective-permute-start(bf16[2,128,512]{2,1,0:T(8,128)(2,1)S(1)} %get-tuple-element.25), channel_id=1, source_target_pairs={{0,3},{1,0},{2,1},{3,2},{4,7},{5,4},{6,5},{7,6},{8,11},{9,8},{10,9... | collective-permute-start | bytes 786440 | tf_op jit(solution)/shard_map/ppermute | solution.py:144
  29.4 0.0 collective-permute-done.6.rest_4_
  29.4 0.8 shard_map.66
  30.1 0.3 collective-permute-start.7
  30.4 3.5 %collective-permute-start.8 = (f32[128,512]{1,0:T(8,128)S(1)}, f32[128,512]{1,0:T(8,128)S(1)}, u32[]{:S(2)}, u32[]{:S(2)}) collective-permute-start(f32[128,512]{1,0:T(8,128)S(1)} %get-tuple-element.28), channel_id=1, source_target_pairs={{0,2},{1,3},{2,0},{3,1},{4,6},{5,7},{6,4},{7,5},{8,10},{9,11},{10,... | collective-permute-start | bytes 786440 | tf_op jit(solution)/shard_map/ppermute | solution.py:156
  33.9 10.0 %collective-permute-done.refs_1_ = bf16[2,128,512]{2,1,0:T(8,128)(2,1)S(1)} collective-permute-done((bf16[2,128,512]{2,1,0:T(8,128)(2,1)S(1)}, bf16[2,128,512]{2,1,0:T(8,128)(2,1)S(1)}, u32[]{:S(2)}, u32[]{:S(2)}) %collective-permute-start) | collective-permute-done | bytes 262176 | tf_op jit(solution)/shard_map/ppermute | solution.py:144
  43.9 0.0 collective-permute-start.9
  43.9 17.1 %collective-permute-done.1.refs_2_ = bf16[2,128,512]{2,1,0:T(8,128)(2,1)S(1)} collective-permute-done((bf16[2,128,512]{2,1,0:T(8,128)(2,1)S(1)}, bf16[2,128,512]{2,1,0:T(8,128)(2,1)S(1)}, u32[]{:S(2)}, u32[]{:S(2)}) %collective-permute-start.1) | collective-permute-done | bytes 262176 | tf_op jit(solution)/shard_map/ppermute | solution.py:144
  61.0 1.5 %collective-permute-done.2.refs_3_ = bf16[2,128,512]{2,1,0:T(8,128)(2,1)S(1)} collective-permute-done((bf16[2,128,512]{2,1,0:T(8,128)(2,1)S(1)}, bf16[2,128,512]{2,1,0:T(8,128)(2,1)S(1)}, u32[]{:S(2)}, u32[]{:S(2)}) %collective-permute-start.2) | collective-permute-done | bytes 262176 | tf_op jit(solution)/shard_map/ppermute | solution.py:144
  62.5 4.2 %collective-permute-done.7.refs_5_ = f32[128,512]{1,0:T(8,128)S(1)} collective-permute-done((f32[128,512]{1,0:T(8,128)S(1)}, f32[128,512]{1,0:T(8,128)S(1)}, u32[]{:S(2)}, u32[]{:S(2)}) %collective-permute-start.7) | collective-permute-done | bytes 262176 | tf_op jit(solution)/shard_map/ppermute | solution.py:156
  66.8 5.1 %collective-permute-done.8.refs_6_ = f32[128,512]{1,0:T(8,128)S(1)} collective-permute-done((f32[128,512]{1,0:T(8,128)S(1)}, f32[128,512]{1,0:T(8,128)S(1)}, u32[]{:S(2)}, u32[]{:S(2)}) %collective-permute-start.8) | collective-permute-done | bytes 262176 | tf_op jit(solution)/shard_map/ppermute | solution.py:156
  71.9 1.8 %collective-permute-done.9.refs_7_ = f32[128,512]{1,0:T(8,128)S(1)} collective-permute-done((f32[128,512]{1,0:T(8,128)S(1)}, f32[128,512]{1,0:T(8,128)S(1)}, u32[]{:S(2)}, u32[]{:S(2)}) %collective-permute-start.9) | collective-permute-done | bytes 262176 | tf_op jit(solution)/shard_map/ppermute | solution.py:156
  73.7 1.5 %shard_map.67 = (f32[128,512]{1,0:T(8,128)S(1)}, f32[128,512]{1,0:T(8,128)S(1)}, f32[128,512]{1,0:T(8,128)S(1)}, f32[128,512]{1,0:T(8,128)S(1)}) custom-call(bf16[2,128,512]{2,1,0:T(8,128)(2,1)S(1)} %get-tuple-element.22.refs_0_, bf16[2,128,512]{2,1,0:T(8,128)(2,1)S(1)} %collective-permute-done.refs_1_, ...), custom_call_target="tpu_custom_call" | custom-call | flops 1073741824 | bytes 1 | tf_op jit(solution)/shard_map/pallas_call | solution.py:158
  75.2 0.1 collective-permute-start.10
  75.3 1.7 %collective-permute-start.11 = (f32[128,512]{1,0:T(8,128)S(1)}, f32[128,512]{1,0:T(8,128)S(1)}, u32[]{:S(2)}, u32[]{:S(2)}) collective-permute-start(f32[128,512]{1,0:T(8,128)S(1)} %get-tuple-element.32), channel_id=1, source_target_pairs={{0,2},{1,3},{2,0},{3,1},{4,6},{5,7},{6,4},{7,5},{8,10},{9,11},{10,... | collective-permute-start | bytes 786440 | tf_op jit(solution)/shard_map/ppermute | solution.py:165
  76.9 1.9 %collective-permute-start.12 = (f32[128,512]{1,0:T(8,128)S(1)}, f32[128,512]{1,0:T(8,128)S(1)}, u32[]{:S(2)}, u32[]{:S(2)}) collective-permute-start(f32[128,512]{1,0:T(8,128)S(1)} %get-tuple-element.33), channel_id=1, source_target_pairs={{0,3},{1,0},{2,1},{3,2},{4,7},{5,4},{6,5},{7,6},{8,11},{9,8},{10,9... | collective-permute-start | bytes 786440 | tf_op jit(solution)/shard_map/ppermute | solution.py:165
  78.9 5.6 %collective-permute-done.10.rest_1_ = f32[128,512]{1,0:T(8,128)S(1)} collective-permute-done((f32[128,512]{1,0:T(8,128)S(1)}, f32[128,512]{1,0:T(8,128)S(1)}, u32[]{:S(2)}, u32[]{:S(2)}) %collective-permute-start.10) | collective-permute-done | bytes 262176 | tf_op jit(solution)/shard_map/ppermute | solution.py:165
  84.4 13.8 %collective-permute-done.11.rest_2_ = f32[128,512]{1,0:T(8,128)S(1)} collective-permute-done((f32[128,512]{1,0:T(8,128)S(1)}, f32[128,512]{1,0:T(8,128)S(1)}, u32[]{:S(2)}, u32[]{:S(2)}) %collective-permute-start.11) | collective-permute-done | bytes 262176 | tf_op jit(solution)/shard_map/ppermute | solution.py:165
  98.2 1.7 %collective-permute-done.12.rest_3_ = f32[128,512]{1,0:T(8,128)S(1)} collective-permute-done((f32[128,512]{1,0:T(8,128)S(1)}, f32[128,512]{1,0:T(8,128)S(1)}, u32[]{:S(2)}, u32[]{:S(2)}) %collective-permute-start.12) | collective-permute-done | bytes 262176 | tf_op jit(solution)/shard_map/ppermute | solution.py:165
  99.9 1.2 %shard_map.68 = (f32[128,512]{1,0:T(8,128)S(1)}, f32[128,512]{1,0:T(8,128)S(1)}, f32[128,512]{1,0:T(8,128)S(1)}, f32[128,512]{1,0:T(8,128)S(1)}, f32[4,128,512]{2,1,0:T(8,128)S(1)}) custom-call(s32[32]{0:T(128)S(1)} %bitcast.33, f32[128,512]{1,0:T(8,128)S(1)} %get-tuple-element.30.rest_0_, f32[128,512]{1,0:T(8,128)S(1)} %collective-permute-done.10.rest_1_, ...), custom_call_target="tpu_custom_call" | custom-call | flops 1 | bytes 1 | tf_op jit(solution)/shard_map/pallas_call | solution.py:166
  101.1 0.1 collective-permute-start.13
  101.2 2.6 %collective-permute-done.13 = f32[4,128,512]{2,1,0:T(8,128)S(1)} collective-permute-done((f32[4,128,512]{2,1,0:T(8,128)S(1)}, f32[4,128,512]{2,1,0:T(8,128)S(1)}, u32[]{:S(2)}, u32[]{:S(2)}) %collective-permute-start.13) | collective-permute-done | bytes 1048608 | tf_op jit(solution)/shard_map/ppermute | solution.py:173
  103.8 0.1 fusion.2
  104.0 1.3 %collective-permute-start.14 = (f32[128,512]{1,0:T(8,128)S(1)}, f32[128,512]{1,0:T(8,128)S(1)}, u32[]{:S(2)}, u32[]{:S(2)}) collective-permute-start(f32[128,512]{1,0:T(8,128)S(1)} %get-tuple-element.39), channel_id=1, source_target_pairs={{0,8},{4,12},{8,0},{12,4},{16,24},{20,28},{24,16},{28,20},{1,9},{5... | collective-permute-start | bytes 786440 | tf_op jit(solution)/shard_map/ppermute | solution.py:177
  105.2 0.8 collective-permute-start.15
  106.0 1.5 %collective-permute-start.16 = (f32[128,512]{1,0:T(8,128)S(1)}, f32[128,512]{1,0:T(8,128)S(1)}, u32[]{:S(2)}, u32[]{:S(2)}) collective-permute-start(f32[128,512]{1,0:T(8,128)S(1)} %get-tuple-element.40), channel_id=1, source_target_pairs={{0,24},{4,28},{8,16},{12,20},{16,8},{20,12},{24,0},{28,4},{1,25},{... | collective-permute-start | bytes 786440 | tf_op jit(solution)/shard_map/ppermute | solution.py:177
  107.5 5.7 %collective-permute-done.14 = f32[128,512]{1,0:T(8,128)S(1)} collective-permute-done((f32[128,512]{1,0:T(8,128)S(1)}, f32[128,512]{1,0:T(8,128)S(1)}, u32[]{:S(2)}, u32[]{:S(2)}) %collective-permute-start.14) | collective-permute-done | bytes 262176 | tf_op jit(solution)/shard_map/ppermute | solution.py:177
  113.2 0.9 collective-permute-done.15
  114.1 4.8 %collective-permute-done.16 = f32[128,512]{1,0:T(8,128)S(1)} collective-permute-done((f32[128,512]{1,0:T(8,128)S(1)}, f32[128,512]{1,0:T(8,128)S(1)}, u32[]{:S(2)}, u32[]{:S(2)}) %collective-permute-start.16) | collective-permute-done | bytes 262176 | tf_op jit(solution)/shard_map/ppermute | solution.py:177
  118.9 0.8 fusion.7
  (9 shorter events, 0.0 us)
Async XLA Ops:
  0.0 9.4 %collective-permute-start.3 = (f32[128,512]{1,0:T(8,128)}, f32[128,512]{1,0:T(8,128)S(1)}, u32[]{:S(2)}, u32[]{:S(2)}) collective-permute-start(f32[128,512]{1,0:T(8,128)} %bitcast.28), channel_id=1, source_target_pairs={{0,8},{4,12},{8,0},{12,4},{16,24},{20,28},{24,16},{28,20},{1,9},{5... | collective-permute-start | bytes 786440 | tf_op jit(solution)/shard_map/ppermute | solution.py:131
  1.5 13.6 %collective-permute-start.4 = (f32[128,512]{1,0:T(8,128)}, f32[128,512]{1,0:T(8,128)S(1)}, u32[]{:S(2)}, u32[]{:S(2)}) collective-permute-start(f32[128,512]{1,0:T(8,128)} %bitcast.29), channel_id=1, source_target_pairs={{0,16},{4,20},{8,24},{12,28},{16,0},{20,4},{24,8},{28,12},{1,17},{... | collective-permute-start | bytes 786440 | tf_op jit(solution)/shard_map/ppermute | solution.py:131
  3.0 12.1 %collective-permute-start.5 = (f32[128,512]{1,0:T(8,128)}, f32[128,512]{1,0:T(8,128)S(1)}, u32[]{:S(2)}, u32[]{:S(2)}) collective-permute-start(f32[128,512]{1,0:T(8,128)} %bitcast.30), channel_id=1, source_target_pairs={{0,24},{4,28},{8,16},{12,20},{16,8},{20,12},{24,0},{28,4},{1,25},{... | collective-permute-start | bytes 786440 | tf_op jit(solution)/shard_map/ppermute | solution.py:131
  15.1 1.0 copy-start.2
  16.0 0.7 copy-start.4
  17.4 11.9 %collective-permute-start.6 = (f32[4,128,512]{2,1,0:T(8,128)S(1)}, f32[4,128,512]{2,1,0:T(8,128)S(1)}, u32[]{:S(2)}, u32[]{:S(2)}) collective-permute-start(f32[4,128,512]{2,1,0:T(8,128)S(1)} %shard_map.65), channel_id=1, source_target_pairs={{0,4},{4,0},{8,12},{12,8},{16,20},{20,16},{24,28},{28,24},{1,5},{5... | collective-permute-start | bytes 3145736 | tf_op jit(solution)/shard_map/ppermute | solution.py:150
  17.5 2.3 %copy-start = (bf16[34,128,512]{2,1,0:T(8,128)(2,1)S(1)}, bf16[34,128,512]{2,1,0:T(8,128)(2,1)}, u32[]{:S(2)}) copy-start(bf16[34,128,512]{2,1,0:T(8,128)(2,1)} %left_ref.1) | copy-start | bytes 13369348
  19.8 2.3 %copy-start.1 = (bf16[34,128,512]{2,1,0:T(8,128)(2,1)S(1)}, bf16[34,128,512]{2,1,0:T(8,128)(2,1)}, u32[]{:S(2)}) copy-start(bf16[34,128,512]{2,1,0:T(8,128)(2,1)} %right_ref.1) | copy-start | bytes 13369348
  22.0 0.7 copy-start.6
  22.7 6.7 %copy-start.3 = (f32[1,128,512]{2,1,0:T(8,128)S(1)}, f32[1,128,512]{2,1,0:T(8,128)}, u32[]{:S(2)}) copy-start(f32[1,128,512]{2,1,0:T(8,128)} %param.6) | copy-start | bytes 786436
  22.7 6.7 %copy-start.5 = (s32[32]{0:T(128)S(1)}, s32[32]{0:T(128)}, u32[]{:S(2)}) copy-start(s32[32]{0:T(128)} %in_ref.3) | copy-start | bytes 388
  24.7 75.2 %copy-start.7 = (s32[32,1]{0,1:T(1,128)S(1)}, s32[32,1]{0,1:T(1,128)}, u32[]{:S(2)}) copy-start(s32[32,1]{0,1:T(1,128)} %param.10) | copy-start | bytes 388
  24.7 19.2 %collective-permute-start = (bf16[2,128,512]{2,1,0:T(8,128)(2,1)S(1)}, bf16[2,128,512]{2,1,0:T(8,128)(2,1)S(1)}, u32[]{:S(2)}, u32[]{:S(2)}) collective-permute-start(bf16[2,128,512]{2,1,0:T(8,128)(2,1)S(1)} %get-tuple-element.23), channel_id=1, source_target_pairs={{0,1},{1,2},{2,3},{3,0},{4,5},{5,6},{6,7},{7,4},{8,9},{9,10},{10,1... | collective-permute-start | bytes 786440 | tf_op jit(solution)/shard_map/ppermute | solution.py:144
  26.3 34.7 %collective-permute-start.1 = (bf16[2,128,512]{2,1,0:T(8,128)(2,1)S(1)}, bf16[2,128,512]{2,1,0:T(8,128)(2,1)S(1)}, u32[]{:S(2)}, u32[]{:S(2)}) collective-permute-start(bf16[2,128,512]{2,1,0:T(8,128)(2,1)S(1)} %get-tuple-element.24), channel_id=1, source_target_pairs={{0,2},{1,3},{2,0},{3,1},{4,6},{5,7},{6,4},{7,5},{8,10},{9,11},{10,... | collective-permute-start | bytes 786440 | tf_op jit(solution)/shard_map/ppermute | solution.py:144
  27.6 35.0 %collective-permute-start.2 = (bf16[2,128,512]{2,1,0:T(8,128)(2,1)S(1)}, bf16[2,128,512]{2,1,0:T(8,128)(2,1)S(1)}, u32[]{:S(2)}, u32[]{:S(2)}) collective-permute-start(bf16[2,128,512]{2,1,0:T(8,128)(2,1)S(1)} %get-tuple-element.25), channel_id=1, source_target_pairs={{0,3},{1,0},{2,1},{3,2},{4,7},{5,4},{6,5},{7,6},{8,11},{9,8},{10,9... | collective-permute-start | bytes 786440 | tf_op jit(solution)/shard_map/ppermute | solution.py:144
  30.1 36.6 %collective-permute-start.7 = (f32[128,512]{1,0:T(8,128)S(1)}, f32[128,512]{1,0:T(8,128)S(1)}, u32[]{:S(2)}, u32[]{:S(2)}) collective-permute-start(f32[128,512]{1,0:T(8,128)S(1)} %get-tuple-element.27), channel_id=1, source_target_pairs={{0,1},{1,2},{2,3},{3,0},{4,5},{5,6},{6,7},{7,4},{8,9},{9,10},{10,1... | collective-permute-start | bytes 786440 | tf_op jit(solution)/shard_map/ppermute | solution.py:156
  30.4 41.5 %collective-permute-start.8 = (f32[128,512]{1,0:T(8,128)S(1)}, f32[128,512]{1,0:T(8,128)S(1)}, u32[]{:S(2)}, u32[]{:S(2)}) collective-permute-start(f32[128,512]{1,0:T(8,128)S(1)} %get-tuple-element.28), channel_id=1, source_target_pairs={{0,2},{1,3},{2,0},{3,1},{4,6},{5,7},{6,4},{7,5},{8,10},{9,11},{10,... | collective-permute-start | bytes 786440 | tf_op jit(solution)/shard_map/ppermute | solution.py:156
  43.9 29.8 %collective-permute-start.9 = (f32[128,512]{1,0:T(8,128)S(1)}, f32[128,512]{1,0:T(8,128)S(1)}, u32[]{:S(2)}, u32[]{:S(2)}) collective-permute-start(f32[128,512]{1,0:T(8,128)S(1)} %get-tuple-element.29), channel_id=1, source_target_pairs={{0,3},{1,0},{2,1},{3,2},{4,7},{5,4},{6,5},{7,6},{8,11},{9,8},{10,9... | collective-permute-start | bytes 786440 | tf_op jit(solution)/shard_map/ppermute | solution.py:156
  75.2 9.2 %collective-permute-start.10 = (f32[128,512]{1,0:T(8,128)S(1)}, f32[128,512]{1,0:T(8,128)S(1)}, u32[]{:S(2)}, u32[]{:S(2)}) collective-permute-start(f32[128,512]{1,0:T(8,128)S(1)} %get-tuple-element.31), channel_id=1, source_target_pairs={{0,1},{1,2},{2,3},{3,0},{4,5},{5,6},{6,7},{7,4},{8,9},{9,10},{10,1... | collective-permute-start | bytes 786440 | tf_op jit(solution)/shard_map/ppermute | solution.py:165
  75.3 22.9 %collective-permute-start.11 = (f32[128,512]{1,0:T(8,128)S(1)}, f32[128,512]{1,0:T(8,128)S(1)}, u32[]{:S(2)}, u32[]{:S(2)}) collective-permute-start(f32[128,512]{1,0:T(8,128)S(1)} %get-tuple-element.32), channel_id=1, source_target_pairs={{0,2},{1,3},{2,0},{3,1},{4,6},{5,7},{6,4},{7,5},{8,10},{9,11},{10,... | collective-permute-start | bytes 786440 | tf_op jit(solution)/shard_map/ppermute | solution.py:165
  76.9 22.9 %collective-permute-start.12 = (f32[128,512]{1,0:T(8,128)S(1)}, f32[128,512]{1,0:T(8,128)S(1)}, u32[]{:S(2)}, u32[]{:S(2)}) collective-permute-start(f32[128,512]{1,0:T(8,128)S(1)} %get-tuple-element.33), channel_id=1, source_target_pairs={{0,3},{1,0},{2,1},{3,2},{4,7},{5,4},{6,5},{7,6},{8,11},{9,8},{10,9... | collective-permute-start | bytes 786440 | tf_op jit(solution)/shard_map/ppermute | solution.py:165
  101.1 2.7 %collective-permute-start.13 = (f32[4,128,512]{2,1,0:T(8,128)S(1)}, f32[4,128,512]{2,1,0:T(8,128)S(1)}, u32[]{:S(2)}, u32[]{:S(2)}) collective-permute-start(f32[4,128,512]{2,1,0:T(8,128)S(1)} %get-tuple-element.35), channel_id=1, source_target_pairs={{0,4},{4,0},{8,12},{12,8},{16,20},{20,16},{24,28},{28,24},{1,5},{5... | collective-permute-start | bytes 3145736 | tf_op jit(solution)/shard_map/ppermute | solution.py:173
  104.0 9.2 %collective-permute-start.14 = (f32[128,512]{1,0:T(8,128)S(1)}, f32[128,512]{1,0:T(8,128)S(1)}, u32[]{:S(2)}, u32[]{:S(2)}) collective-permute-start(f32[128,512]{1,0:T(8,128)S(1)} %get-tuple-element.39), channel_id=1, source_target_pairs={{0,8},{4,12},{8,0},{12,4},{16,24},{20,28},{24,16},{28,20},{1,9},{5... | collective-permute-start | bytes 786440 | tf_op jit(solution)/shard_map/ppermute | solution.py:177
  105.2 8.9 %collective-permute-start.15 = (f32[128,512]{1,0:T(8,128)S(1)}, f32[128,512]{1,0:T(8,128)S(1)}, u32[]{:S(2)}, u32[]{:S(2)}) collective-permute-start(f32[128,512]{1,0:T(8,128)S(1)} %get-tuple-element.41), channel_id=1, source_target_pairs={{0,16},{4,20},{8,24},{12,28},{16,0},{20,4},{24,8},{28,12},{1,17},{... | collective-permute-start | bytes 786440 | tf_op jit(solution)/shard_map/ppermute | solution.py:177
  106.0 12.9 %collective-permute-start.16 = (f32[128,512]{1,0:T(8,128)S(1)}, f32[128,512]{1,0:T(8,128)S(1)}, u32[]{:S(2)}, u32[]{:S(2)}) collective-permute-start(f32[128,512]{1,0:T(8,128)S(1)} %get-tuple-element.40), channel_id=1, source_target_pairs={{0,24},{4,28},{8,16},{12,20},{16,8},{20,12},{24,0},{28,4},{1,25},{... | collective-permute-start | bytes 786440 | tf_op jit(solution)/shard_map/ppermute | solution.py:177
where the time goes:
time: 120 us
  waiting for transfers between devices  86.5 us (72%)
  starting transfers between devices  19.3 us (16%)
  local copies, waits for them, and re-layouts  6.79 us (6%)
  Pallas kernels  6.15 us (5%)
    ppermute x3, waiting for transfers between devices, body(): lax.ppermute(envs[s], 'env', along(s))  28.6 us
    ppermute x3, waiting for transfers between devices, body(): lax.ppermute(parts[s], 'env', along(s))  21 us
    ppermute x3, waiting for transfers between devices, body(): lax.ppermute(psi, 'sec', across(hop))  11.6 us
    ppermute x3, waiting for transfers between devices, body(): total = total + lax.ppermute(sums[hop], 'sec', across(hop))  11.4 us
    ppermute x3, waiting for transfers between devices, body(): lax.ppermute(psis[s], 'env', along(s))  11.2 us
    unnamed x16, local copies, waits for them, and re-layouts  6.79 us
    ppermute x3, starting transfers between devices, body(): lax.ppermute(envs[s], 'env', along(s))  4.67 us
    ppermute x3, starting transfers between devices, body(): lax.ppermute(psis[s], 'env', along(s))  3.77 us
  transfers between devices with their start and end apart: 17, of which 15 were waited for; matrix products, arithmetic and copies ran while one was open for 0% of the time, Pallas kernels for 2%

commit v1 on v0

v1 whole, which is shorter than its diff:
```python
import functools

import jax
import jax.numpy as jnp
from jax import lax
from jax.experimental import pallas as pl
from jax.experimental.pallas import tpu as pltpu
from jax.sharding import PartitionSpec as P


GRID, LIMIT, LEVELS, HEAD = 1024.0, 32767.0, 256.0, 16
PREPARE_BYTES = 63_400_000
VMEM_BYTES = 16 * 1024 * 1024
VMEM = pl.BlockSpec(memory_space=pltpu.VMEM)
SMEM = pl.BlockSpec(memory_space=pltpu.SMEM)
HBM = pl.BlockSpec(memory_space=pltpu.HBM)


def call(kernel, out_shape, in_specs, scratch=(), flops=1, vmem=VMEM_BYTES):
    return pl.pallas_call(
        kernel,
        out_shape=out_shape,
        in_specs=in_specs,
        out_specs=jax.tree.map(lambda _: VMEM, out_shape),
        scratch_shapes=list(scratch),
        cost_estimate=pl.CostEstimate(flops=flops, bytes_accessed=1, transcendentals=0),
        compiler_params=pltpu.CompilerParams(vmem_limit_bytes=vmem),
    )


def encode(value, out, centred):
    rows = value.shape[0]
    centre = jnp.zeros_like(value[:1])
    if centred:
        middle = (jnp.max(value, axis=0, keepdims=True) + jnp.min(value, axis=0, keepdims=True)) / 2
        centre = jnp.clip((middle * GRID).astype(jnp.int32), -LIMIT, LIMIT).astype(jnp.float32)
        value = value - centre / GRID
    span = jnp.max(jnp.abs(value), axis=0, keepdims=True)
    level = jnp.log(jnp.maximum(span, 1e-30)) * LEVELS + 1.0
    level = (level + jnp.where(level > 0, 1.0, 0.0)).astype(jnp.int32).astype(jnp.float32)
    scaled = value * (LIMIT / jnp.exp(level / LEVELS))
    scaled = jnp.clip(scaled + jnp.where(scaled > 0, 0.5, -0.5), -LIMIT, LIMIT)
    out[pl.ds(0, rows), :] = scaled.astype(jnp.int32).astype(jnp.int16)
    lines = lax.broadcasted_iota(jnp.int32, (HEAD, value.shape[1]), 0)
    head = jnp.where(lines == 0, level.astype(jnp.int32), centre.astype(jnp.int32))
    out[pl.ds(rows, HEAD), :] = head.astype(jnp.int16)


def decode(code):
    rows = code.shape[0] - HEAD
    head = code[pl.ds(rows, HEAD), :].astype(jnp.int32).astype(jnp.float32)
    step = jnp.exp(head[0:1] / LEVELS) / LIMIT
    value = code[pl.ds(0, rows), :].astype(jnp.int32).astype(jnp.float32)
    return value * step + head[1:2] / GRID


def prepare_kernel(base, me, count, term_ref, psi_ref, left_ref, right_ref, *rest):
    outs, code, sem = rest[:count], rest[count], rest[count + 1]
    copies = []
    start, mine = base(), me()
    for step in range(count):
        term = term_ref[start + lax.rem(mine + step, count)]
        copies.append(pltpu.make_async_copy(left_ref.at[term], outs[step].at[0], sem.at[2 * step]))
        copies.append(pltpu.make_async_copy(right_ref.at[term], outs[step].at[1], sem.at[2 * step + 1]))
    for copy in copies:
        copy.start()
    encode(psi_ref[...], code, True)
    for copy in copies:
        copy.wait()


def partner_psi_kernel(base, sec, count, chips, in_ref, *rest):
    held, out = rest[:chips], rest[chips]
    start = base()
    chip, core = sec() // 2, lax.rem(sec(), 2)
    for slot in range(count):
        source = in_ref[start + slot]
        for step in range(chips):
            @pl.when((source // 2 == chip ^ step) & (lax.rem(source, 2) == core))
            def _():
                out[slot] = held[step][...]


def own_psi_kernel(base, sec, me, count, chips, in_ref, *rest):
    held, paired, outs = rest[:chips], rest[chips], rest[chips + 1 :]
    start, mine = base(), me()
    chip, core = sec() // 2, lax.rem(sec(), 2)
    for step in range(count):
        slot = lax.rem(mine + step, count)
        source = in_ref[start + slot]
        same = lax.rem(source, 2) == core
        for hop in range(chips):
            @pl.when((source // 2 == chip ^ hop) & same)
            def _():
                outs[step][...] = held[hop][...]

        @pl.when(jnp.logical_not(same))
        def _():
            outs[step][...] = paired[slot]


def task_kernel(me, count, *refs):
    envs, psis, outs = refs[:count], refs[count : 2 * count], refs[2 * count : 3 * count]
    high, low, right = refs[3 * count :]
    rows = outs[0].shape[0]
    mine = me()
    for step in range(count):
        place = pl.ds(pl.multiple_of(lax.rem(mine + count - step, count) * rows, rows), rows)
        right[place, :] = envs[step][1]
        psi = decode(psis[step])
        top = psi.astype(jnp.bfloat16)
        high[place, :] = top
        low[place, :] = (psi - top.astype(jnp.float32)).astype(jnp.bfloat16)
    mixed = jnp.dot(high[...], right[...], preferred_element_type=jnp.float32) + jnp.dot(
        low[...], right[...], preferred_element_type=jnp.float32
    )
    top = mixed.astype(jnp.bfloat16)
    high[...] = top
    low[...] = (mixed - top.astype(jnp.float32)).astype(jnp.bfloat16)
    for step in range(count):
        left = envs[(count - step) % count][0]
        part = jnp.dot(left, high[...], preferred_element_type=jnp.float32) + jnp.dot(
            left, low[...], preferred_element_type=jnp.float32
        )
        if step == 0:
            outs[0][...] = part
        else:
            encode(part, outs[step], False)


def combine_kernel(base, sec, me, count, target_ref, *rest):
    parts, keep, send = rest[:count], rest[count], rest[count + 1]
    start, mine = base(), me()
    chip, core = sec() // 2, lax.rem(sec(), 2)
    keep[...] = jnp.zeros(keep.shape, jnp.float32)
    send[...] = jnp.zeros(send.shape, jnp.float32)
    for step in range(count):
        target = target_ref[start + lax.rem(mine + count - step, count)]
        hop = (target // 2) ^ chip
        part = parts[0][...] if step == 0 else decode(parts[step])
        mine_too = lax.rem(target, 2) == core

        @pl.when(mine_too)
        def _():
            keep[hop] = keep[hop] + part

        @pl.when(jnp.logical_not(mine_too))
        def _():
            send[hop] = send[hop] + part


def join_kernel(chips, keep, other, *outs):
    for hop in range(chips):
        total = keep[hop] + other[hop]
        if hop == 0:
            outs[0][...] = total
        else:
            encode(total, outs[hop], False)


def finish_kernel(chips, *refs):
    total = refs[0][...]
    for hop in range(1, chips):
        total = total + decode(refs[hop])
    refs[chips][...] = total


def body(wavefunction, left_env, right_env, task_in, task_out, task_term):
    groups, count = lax.axis_size("sec"), lax.axis_size("env")
    chips = groups // 2
    _, rows, cols = wavefunction.shape
    per_device = task_in.shape[0] // (groups * count)
    targets = task_out[:, 0]
    f32, bf16 = jnp.float32, jnp.bfloat16
    block = jax.ShapeDtypeStruct((rows, cols), f32)
    sec = lambda: lax.axis_index("sec")
    me = lambda: lax.axis_index("env")

    def along(shift):
        return [(i, (i + shift) % count) for i in range(count)]

    def across(hop):
        return [(i, i ^ (2 * hop)) for i in range(groups)]

    pair = [(i, i ^ 1) for i in range(groups)]
    code = jax.ShapeDtypeStruct((rows + HEAD, cols), jnp.int16)
    stack = jax.ShapeDtypeStruct((chips, rows, cols), f32)

    keep, send, held = None, None, None
    for turn in range(per_device):
        base = lambda: (sec() * per_device + turn) * count
        partner_base = lambda: ((sec() ^ 1) * per_device + turn) * count
        env_block = jax.ShapeDtypeStruct((2, rows, cols), bf16)
        *envs, psi = call(
            functools.partial(prepare_kernel, base, me, count),
            [env_block] * count + [code],
            [SMEM, VMEM, HBM, HBM],
            [pltpu.SemaphoreType.DMA((2 * count,))],
            vmem=PREPARE_BYTES,
        )(task_term, wavefunction[0], left_env, right_env)
        envs = [envs[0]] + [lax.ppermute(envs[s], "env", along(s)) for s in range(1, count)]
        if held is None:
            held = [psi] + [lax.ppermute(psi, "sec", across(hop)) for hop in range(1, chips)]
        sent = call(
            functools.partial(partner_psi_kernel, partner_base, sec, count, chips),
            jax.ShapeDtypeStruct((count, *code.shape), code.dtype),
            [SMEM] + [VMEM] * chips,
        )(task_in, *held)
        paired = lax.ppermute(sent, "sec", pair)
        psis = call(
            functools.partial(own_psi_kernel, base, sec, me, count, chips),
            [code] * count,
            [SMEM] + [VMEM] * (chips + 1),
        )(task_in, *held, paired)
        psis = [psis[0]] + [lax.ppermute(psis[s], "env", along(s)) for s in range(1, count)]
        full = count * rows
        parts = call(
            functools.partial(task_kernel, me, count),
            [block] + [code] * (count - 1),
            [VMEM] * (2 * count),
            [pltpu.VMEM((full, cols), bf16)] * 3,
            flops=8 * full * full * cols,
        )(*envs, *psis)
        parts = [parts[0]] + [lax.ppermute(parts[s], "env", along(s)) for s in range(1, count)]
        kept, sends = call(
            functools.partial(combine_kernel, base, sec, me, count),
            [stack, stack],
            [SMEM] + [VMEM] * count,
        )(targets, *parts)
        keep = kept if keep is None else keep + kept
        send = sends if send is None else send + sends
    other = lax.ppermute(send, "sec", pair)
    sums = call(
        functools.partial(join_kernel, chips), [block] + [code] * (chips - 1), [VMEM] * 2
    )(keep, other)
    sums = [sums[0]] + [lax.ppermute(sums[hop], "sec", across(hop)) for hop in range(1, chips)]
    total = call(functools.partial(finish_kernel, chips), block, [VMEM] * chips)(*sums)
    return total[None]


def solution(mesh):
    placed = (P("sec", "env", None), P(None, "env", None), P(None, "env", None), P(), P(), P())
    return jax.shard_map(
        body, mesh=mesh, in_specs=placed, out_specs=P("sec", "env", None), check_vma=False
    )
```

time: 120 us -> 87.2 us (0.73)
  the two profiles are of different devices: /device:TPU:8 before, /device:TPU:0 now
where the time goes in v1:
time: 87.2 us; the launch traced here: 86.5 us
  waiting for transfers between devices  52.8 us (61%)
  starting transfers between devices  23 us (26%)
  Pallas kernels  8.64 us (10%)
  local copies, waits for them, and re-layouts  1.87 us (2%)
    ppermute x3, waiting for transfers between devices, body(): lax.ppermute(psis[s], 'env', along(s))  14.6 us
    ppermute x3, waiting for transfers between devices, body(): lax.ppermute(envs[s], 'env', along(s))  13.4 us
    ppermute x3, waiting for transfers between devices, body(): lax.ppermute(parts[s], 'env', along(s))  8.57 us
    ppermute x3, waiting for transfers between devices, body(): lax.ppermute(psi, 'sec', across(hop))  6.86 us
    ppermute x3, waiting for transfers between devices, body(): lax.ppermute(sums[hop], 'sec', across(hop))  6.8 us
    ppermute x3, starting transfers between devices, body(): lax.ppermute(parts[s], 'env', along(s))  6.14 us
    ppermute x3, starting transfers between devices, body(): lax.ppermute(envs[s], 'env', along(s))  5.57 us
    ppermute x3, starting transfers between devices, body(): lax.ppermute(psi, 'sec', across(hop))  4.63 us
  transfers between devices with their start and end apart: 17, of which 12 were waited for; matrix products, arithmetic and copies ran while one was open for 0% of the time, Pallas kernels for 1%

profile of v1, /device:TPU:0, one launch (start us, length us, event | category | flops | bytes accessed | tf_op | source)
XLA Modules:
  0.0 86.5 jit_solution(11474781859704498430)
XLA Ops:
  0.0 0.0 copy-start.1
  0.0 3.3 %shard_map.64 = (bf16[2,128,512]{2,1,0:T(8,128)(2,1)}, bf16[2,128,512]{2,1,0:T(8,128)(2,1)}, bf16[2,128,512]{2,1,0:T(8,128)(2,1)}, bf16[2,128,512]{2,1,0:T(8,128)(2,1)}, s16[144,512]{1,0:T(8,128)(2,1)}) custom-call(s32[32]{0:T(128)} %term_ref.1, f32[128,512]{1,0:T(8,128)} %bitcast.4, bf16[34,128,512]{2,1,0:T(8,128)(2,1)} %left_ref.1, ...), custom_call_target="tpu_custom_call" | custom-call | flops 1 | bytes 1 | tf_op jit(solution)/shard_map/pallas_call | solution.py:194
  3.3 0.0 copy-start.2
  3.4 4.0 %collective-permute-start.5 = (s16[144,512]{1,0:T(8,128)(2,1)}, s16[144,512]{1,0:T(8,128)(2,1)S(1)}, u32[]{:S(2)}, u32[]{:S(2)}) collective-permute-start(s16[144,512]{1,0:T(8,128)(2,1)} %get-tuple-element.28.rest_0_), channel_id=1, source_target_pairs={{0,24},{4,28},{8,16},{12,20},{16,8},{20,12},{24,0},{28,4},{1,25},{... | collective-permute-start | bytes 442376 | tf_op jit(solution)/shard_map/ppermute | solution.py:203
  7.3 0.5 collective-permute-start.4
  7.9 0.1 collective-permute-start.3
  8.0 3.9 %collective-permute-done.5.rest_3_ = s16[144,512]{1,0:T(8,128)(2,1)S(1)} collective-permute-done((s16[144,512]{1,0:T(8,128)(2,1)}, s16[144,512]{1,0:T(8,128)(2,1)S(1)}, u32[]{:S(2)}, u32[]{:S(2)}) %collective-permute-start.5) | collective-permute-done | bytes 147488 | tf_op jit(solution)/shard_map/ppermute | solution.py:203
  11.9 2.6 %collective-permute-done.4.rest_2_ = s16[144,512]{1,0:T(8,128)(2,1)S(1)} collective-permute-done((s16[144,512]{1,0:T(8,128)(2,1)}, s16[144,512]{1,0:T(8,128)(2,1)S(1)}, u32[]{:S(2)}, u32[]{:S(2)}) %collective-permute-start.4) | collective-permute-done | bytes 147488 | tf_op jit(solution)/shard_map/ppermute | solution.py:203
  14.6 0.3 collective-permute-done.3.rest_1_
  14.8 0.0 copy-done.1
  14.9 0.0 copy-start
  14.9 0.9 %copy-done = s16[144,512]{1,0:T(8,128)(2,1)S(1)} copy-done((s16[144,512]{1,0:T(8,128)(2,1)S(1)}, s16[144,512]{1,0:T(8,128)(2,1)}, u32[]{:S(2)}) %copy-start) | copy-done | bytes 147480
  15.8 0.7 shard_map.65
  16.5 0.1 collective-permute-start.6
  16.5 1.6 %collective-permute-start = (bf16[2,128,512]{2,1,0:T(8,128)(2,1)}, bf16[2,128,512]{2,1,0:T(8,128)(2,1)S(1)}, u32[]{:S(2)}, u32[]{:S(2)}) collective-permute-start(bf16[2,128,512]{2,1,0:T(8,128)(2,1)} %get-tuple-element.25), channel_id=1, source_target_pairs={{0,1},{1,2},{2,3},{3,0},{4,5},{5,6},{6,7},{7,4},{8,9},{9,10},{10,1... | collective-permute-start | bytes 786440 | tf_op jit(solution)/shard_map/ppermute | solution.py:201
  18.2 2.6 %collective-permute-start.1 = (bf16[2,128,512]{2,1,0:T(8,128)(2,1)}, bf16[2,128,512]{2,1,0:T(8,128)(2,1)S(1)}, u32[]{:S(2)}, u32[]{:S(2)}) collective-permute-start(bf16[2,128,512]{2,1,0:T(8,128)(2,1)} %get-tuple-element.26), channel_id=1, source_target_pairs={{0,2},{1,3},{2,0},{3,1},{4,6},{5,7},{6,4},{7,5},{8,10},{9,11},{10,... | collective-permute-start | bytes 786440 | tf_op jit(solution)/shard_map/ppermute | solution.py:201
  20.8 1.3 %collective-permute-start.2 = (bf16[2,128,512]{2,1,0:T(8,128)(2,1)}, bf16[2,128,512]{2,1,0:T(8,128)(2,1)S(1)}, u32[]{:S(2)}, u32[]{:S(2)}) collective-permute-start(bf16[2,128,512]{2,1,0:T(8,128)(2,1)} %get-tuple-element.27), channel_id=1, source_target_pairs={{0,3},{1,0},{2,1},{3,2},{4,7},{5,4},{6,5},{7,6},{8,11},{9,8},{10,9... | collective-permute-start | bytes 786440 | tf_op jit(solution)/shard_map/ppermute | solution.py:201
  22.1 0.0 collective-permute-done.6.rest_4_
  22.1 0.7 shard_map.66
  22.9 0.7 collective-permute-start.7
  23.6 0.3 collective-permute-start.8
  23.9 4.0 %collective-permute-done.refs_1_ = bf16[2,128,512]{2,1,0:T(8,128)(2,1)S(1)} collective-permute-done((bf16[2,128,512]{2,1,0:T(8,128)(2,1)}, bf16[2,128,512]{2,1,0:T(8,128)(2,1)S(1)}, u32[]{:S(2)}, u32[]{:S(2)}) %collective-permute-start) | collective-permute-done | bytes 262176 | tf_op jit(solution)/shard_map/ppermute | solution.py:201
  27.9 1.9 %collective-permute-start.9 = (s16[144,512]{1,0:T(8,128)(2,1)S(1)}, s16[144,512]{1,0:T(8,128)(2,1)S(1)}, u32[]{:S(2)}, u32[]{:S(2)}) collective-permute-start(s16[144,512]{1,0:T(8,128)(2,1)S(1)} %get-tuple-element.32), channel_id=1, source_target_pairs={{0,3},{1,0},{2,1},{3,2},{4,7},{5,4},{6,5},{7,6},{8,11},{9,8},{10,9... | collective-permute-start | bytes 442376 | tf_op jit(solution)/shard_map/ppermute | solution.py:215
  29.8 9.3 %collective-permute-done.1.refs_2_ = bf16[2,128,512]{2,1,0:T(8,128)(2,1)S(1)} collective-permute-done((bf16[2,128,512]{2,1,0:T(8,128)(2,1)}, bf16[2,128,512]{2,1,0:T(8,128)(2,1)S(1)}, u32[]{:S(2)}, u32[]{:S(2)}) %collective-permute-start.1) | collective-permute-done | bytes 262176 | tf_op jit(solution)/shard_map/ppermute | solution.py:201
  39.2 0.0 collective-permute-done.2.refs_3_
  39.2 3.2 %collective-permute-done.7.refs_5_ = s16[144,512]{1,0:T(8,128)(2,1)S(1)} collective-permute-done((s16[144,512]{1,0:T(8,128)(2,1)S(1)}, s16[144,512]{1,0:T(8,128)(2,1)S(1)}, u32[]{:S(2)}, u32[]{:S(2)}) %collective-permute-start.7) | collective-permute-done | bytes 147488 | tf_op jit(solution)/shard_map/ppermute | solution.py:215
  42.4 11.4 %collective-permute-done.8.refs_6_ = s16[144,512]{1,0:T(8,128)(2,1)S(1)} collective-permute-done((s16[144,512]{1,0:T(8,128)(2,1)S(1)}, s16[144,512]{1,0:T(8,128)(2,1)S(1)}, u32[]{:S(2)}, u32[]{:S(2)}) %collective-permute-start.8) | collective-permute-done | bytes 147488 | tf_op jit(solution)/shard_map/ppermute | solution.py:215
  53.8 0.0 collective-permute-done.9.refs_7_
  53.8 0.9 %copy-done.3 = bf16[2,128,512]{2,1,0:T(8,128)(2,1)S(1)} copy-done((bf16[2,128,512]{2,1,0:T(8,128)(2,1)S(1)}, bf16[2,128,512]{2,1,0:T(8,128)(2,1)}, u32[]{:S(2)}) %copy-start.3) | copy-done | bytes 262168
  54.8 1.8 %shard_map.67 = (f32[128,512]{1,0:T(8,128)S(1)}, s16[144,512]{1,0:T(8,128)(2,1)S(1)}, s16[144,512]{1,0:T(8,128)(2,1)S(1)}, s16[144,512]{1,0:T(8,128)(2,1)S(1)}) custom-call(bf16[2,128,512]{2,1,0:T(8,128)(2,1)S(1)} %copy-done.3, bf16[2,128,512]{2,1,0:T(8,128)(2,1)S(1)} %collective-permute-done.refs_1_, ...), custom_call_target="tpu_custom_call" | custom-call | flops 1073741824 | bytes 1 | tf_op jit(solution)/shard_map/pallas_call | solution.py:217
  56.5 3.7 %collective-permute-start.10 = (s16[144,512]{1,0:T(8,128)(2,1)S(1)}, s16[144,512]{1,0:T(8,128)(2,1)S(1)}, u32[]{:S(2)}, u32[]{:S(2)}) collective-permute-start(s16[144,512]{1,0:T(8,128)(2,1)S(1)} %get-tuple-element.34), channel_id=1, source_target_pairs={{0,1},{1,2},{2,3},{3,0},{4,5},{5,6},{6,7},{7,4},{8,9},{9,10},{10,1... | collective-permute-start | bytes 442376 | tf_op jit(solution)/shard_map/ppermute | solution.py:224
  60.2 1.6 %collective-permute-start.11 = (s16[144,512]{1,0:T(8,128)(2,1)S(1)}, s16[144,512]{1,0:T(8,128)(2,1)S(1)}, u32[]{:S(2)}, u32[]{:S(2)}) collective-permute-start(s16[144,512]{1,0:T(8,128)(2,1)S(1)} %get-tuple-element.35), channel_id=1, source_target_pairs={{0,2},{1,3},{2,0},{3,1},{4,6},{5,7},{6,4},{7,5},{8,10},{9,11},{10,... | collective-permute-start | bytes 442376 | tf_op jit(solution)/shard_map/ppermute | solution.py:224
  61.8 0.9 %collective-permute-start.12 = (s16[144,512]{1,0:T(8,128)(2,1)S(1)}, s16[144,512]{1,0:T(8,128)(2,1)S(1)}, u32[]{:S(2)}, u32[]{:S(2)}) collective-permute-start(s16[144,512]{1,0:T(8,128)(2,1)S(1)} %get-tuple-element.36), channel_id=1, source_target_pairs={{0,3},{1,0},{2,1},{3,2},{4,7},{5,4},{6,5},{7,6},{8,11},{9,8},{10,9... | collective-permute-start | bytes 442376 | tf_op jit(solution)/shard_map/ppermute | solution.py:224
  62.7 3.4 %collective-permute-done.10.rest_1_ = s16[144,512]{1,0:T(8,128)(2,1)S(1)} collective-permute-done((s16[144,512]{1,0:T(8,128)(2,1)S(1)}, s16[144,512]{1,0:T(8,128)(2,1)S(1)}, u32[]{:S(2)}, u32[]{:S(2)}) %collective-permute-start.10) | collective-permute-done | bytes 147488 | tf_op jit(solution)/shard_map/ppermute | solution.py:224
  66.0 5.2 %collective-permute-done.11.rest_2_ = s16[144,512]{1,0:T(8,128)(2,1)S(1)} collective-permute-done((s16[144,512]{1,0:T(8,128)(2,1)S(1)}, s16[144,512]{1,0:T(8,128)(2,1)S(1)}, u32[]{:S(2)}, u32[]{:S(2)}) %collective-permute-start.11) | collective-permute-done | bytes 147488 | tf_op jit(solution)/shard_map/ppermute | solution.py:224
  71.2 0.0 collective-permute-done.12.rest_3_
  71.2 0.0 copy-done.2
  71.2 0.9 %shard_map.68 = (f32[4,128,512]{2,1,0:T(8,128)S(1)}, f32[4,128,512]{2,1,0:T(8,128)S(1)}) custom-call(s32[32]{0:T(128)S(1)} %bitcast.3, f32[128,512]{1,0:T(8,128)S(1)} %get-tuple-element.33.rest_0_, s16[144,512]{1,0:T(8,128)(2,1)S(1)} %collective-permute-done.10.rest_1_, s16[144,512]{1,0:T(8,128)(2,1)S(1)} %collective-permute-done.11.rest_2_, ...), custom_call_target="tpu_custom_call" | custom-call | flops 1 | bytes 1 | tf_op jit(solution)/shard_map/pallas_call | solution.py:225
  72.2 0.1 collective-permute-start.13
  72.2 2.6 %collective-permute-done.13.other = f32[4,128,512]{2,1,0:T(8,128)S(1)} collective-permute-done((f32[4,128,512]{2,1,0:T(8,128)S(1)}, f32[4,128,512]{2,1,0:T(8,128)S(1)}, u32[]{:S(2)}, u32[]{:S(2)}) %collective-permute-start.13) | collective-permute-done | bytes 1048608 | tf_op jit(solution)/shard_map/ppermute | solution.py:232
  74.9 0.4 shard_map.69
  75.3 1.6 %collective-permute-start.14 = (s16[144,512]{1,0:T(8,128)(2,1)S(1)}, s16[144,512]{1,0:T(8,128)(2,1)S(1)}, u32[]{:S(2)}, u32[]{:S(2)}) collective-permute-start(s16[144,512]{1,0:T(8,128)(2,1)S(1)} %get-tuple-element.40), channel_id=1, source_target_pairs={{0,8},{4,12},{8,0},{12,4},{16,24},{20,28},{24,16},{28,20},{1,9},{5... | collective-permute-start | bytes 442376 | tf_op jit(solution)/shard_map/ppermute | solution.py:236
  76.8 0.7 collective-permute-start.15
  77.5 1.3 %collective-permute-start.16 = (s16[144,512]{1,0:T(8,128)(2,1)S(1)}, s16[144,512]{1,0:T(8,128)(2,1)S(1)}, u32[]{:S(2)}, u32[]{:S(2)}) collective-permute-start(s16[144,512]{1,0:T(8,128)(2,1)S(1)} %get-tuple-element.42), channel_id=1, source_target_pairs={{0,24},{4,28},{8,16},{12,20},{16,8},{20,12},{24,0},{28,4},{1,25},{... | collective-permute-start | bytes 442376 | tf_op jit(solution)/shard_map/ppermute | solution.py:236
  78.8 3.1 %collective-permute-done.14.refs_1_ = s16[144,512]{1,0:T(8,128)(2,1)S(1)} collective-permute-done((s16[144,512]{1,0:T(8,128)(2,1)S(1)}, s16[144,512]{1,0:T(8,128)(2,1)S(1)}, u32[]{:S(2)}, u32[]{:S(2)}) %collective-permute-start.14) | collective-permute-done | bytes 147488 | tf_op jit(solution)/shard_map/ppermute | solution.py:236
  82.0 3.7 %collective-permute-done.15.refs_2_ = s16[144,512]{1,0:T(8,128)(2,1)S(1)} collective-permute-done((s16[144,512]{1,0:T(8,128)(2,1)S(1)}, s16[144,512]{1,0:T(8,128)(2,1)S(1)}, u32[]{:S(2)}, u32[]{:S(2)}) %collective-permute-start.15) | collective-permute-done | bytes 147488 | tf_op jit(solution)/shard_map/ppermute | solution.py:236
  85.6 0.0 collective-permute-done.16.refs_3_
  85.6 0.8 shard_map.70
  (1 shorter events, 0.0 us)
Async XLA Ops:
  0.0 14.9 %copy-start.1 = (s32[32]{0:T(128)S(1)}, s32[32]{0:T(128)}, u32[]{:S(2)}) copy-start(s32[32]{0:T(128)} %in_ref.3) | copy-start | bytes 388
  3.3 67.9 %copy-start.2 = (s32[32,1]{0,1:T(1,128)S(1)}, s32[32,1]{0,1:T(1,128)}, u32[]{:S(2)}) copy-start(s32[32,1]{0,1:T(1,128)} %param.10) | copy-start | bytes 388
  3.4 8.6 %collective-permute-start.5 = (s16[144,512]{1,0:T(8,128)(2,1)}, s16[144,512]{1,0:T(8,128)(2,1)S(1)}, u32[]{:S(2)}, u32[]{:S(2)}) collective-permute-start(s16[144,512]{1,0:T(8,128)(2,1)} %get-tuple-element.28.rest_0_), channel_id=1, source_target_pairs={{0,24},{4,28},{8,16},{12,20},{16,8},{20,12},{24,0},{28,4},{1,25},{... | collective-permute-start | bytes 442376 | tf_op jit(solution)/shard_map/ppermute | solution.py:203
  7.3 7.2 %collective-permute-start.4 = (s16[144,512]{1,0:T(8,128)(2,1)}, s16[144,512]{1,0:T(8,128)(2,1)S(1)}, u32[]{:S(2)}, u32[]{:S(2)}) collective-permute-start(s16[144,512]{1,0:T(8,128)(2,1)} %get-tuple-element.28.rest_0_), channel_id=1, source_target_pairs={{0,16},{4,20},{8,24},{12,28},{16,0},{20,4},{24,8},{28,12},{1,17},{... | collective-permute-start | bytes 442376 | tf_op jit(solution)/shard_map/ppermute | solution.py:203
  7.9 7.0 %collective-permute-start.3 = (s16[144,512]{1,0:T(8,128)(2,1)}, s16[144,512]{1,0:T(8,128)(2,1)S(1)}, u32[]{:S(2)}, u32[]{:S(2)}) collective-permute-start(s16[144,512]{1,0:T(8,128)(2,1)} %get-tuple-element.28.rest_0_), channel_id=1, source_target_pairs={{0,8},{4,12},{8,0},{12,4},{16,24},{20,28},{24,16},{28,20},{1,9},{5... | collective-permute-start | bytes 442376 | tf_op jit(solution)/shard_map/ppermute | solution.py:203
  14.9 0.9 %copy-start = (s16[144,512]{1,0:T(8,128)(2,1)S(1)}, s16[144,512]{1,0:T(8,128)(2,1)}, u32[]{:S(2)}) copy-start(s16[144,512]{1,0:T(8,128)(2,1)} %get-tuple-element.28.rest_0_) | copy-start | bytes 442372
  16.5 5.6 %collective-permute-start.6 = (s16[4,144,512]{2,1,0:T(8,128)(2,1)S(1)}, s16[4,144,512]{2,1,0:T(8,128)(2,1)S(1)}, u32[]{:S(2)}, u32[]{:S(2)}) collective-permute-start(s16[4,144,512]{2,1,0:T(8,128)(2,1)S(1)} %shard_map.65), channel_id=1, source_target_pairs={{0,4},{4,0},{8,12},{12,8},{16,20},{20,16},{24,28},{28,24},{1,5},{5... | collective-permute-start | bytes 1769480 | tf_op jit(solution)/shard_map/ppermute | solution.py:209
  16.5 11.4 %collective-permute-start = (bf16[2,128,512]{2,1,0:T(8,128)(2,1)}, bf16[2,128,512]{2,1,0:T(8,128)(2,1)S(1)}, u32[]{:S(2)}, u32[]{:S(2)}) collective-permute-start(bf16[2,128,512]{2,1,0:T(8,128)(2,1)} %get-tuple-element.25), channel_id=1, source_target_pairs={{0,1},{1,2},{2,3},{3,0},{4,5},{5,6},{6,7},{7,4},{8,9},{9,10},{10,1... | collective-permute-start | bytes 786440 | tf_op jit(solution)/shard_map/ppermute | solution.py:201
  18.2 21.0 %collective-permute-start.1 = (bf16[2,128,512]{2,1,0:T(8,128)(2,1)}, bf16[2,128,512]{2,1,0:T(8,128)(2,1)S(1)}, u32[]{:S(2)}, u32[]{:S(2)}) collective-permute-start(bf16[2,128,512]{2,1,0:T(8,128)(2,1)} %get-tuple-element.26), channel_id=1, source_target_pairs={{0,2},{1,3},{2,0},{3,1},{4,6},{5,7},{6,4},{7,5},{8,10},{9,11},{10,... | collective-permute-start | bytes 786440 | tf_op jit(solution)/shard_map/ppermute | solution.py:201
  20.8 18.4 %collective-permute-start.2 = (bf16[2,128,512]{2,1,0:T(8,128)(2,1)}, bf16[2,128,512]{2,1,0:T(8,128)(2,1)S(1)}, u32[]{:S(2)}, u32[]{:S(2)}) collective-permute-start(bf16[2,128,512]{2,1,0:T(8,128)(2,1)} %get-tuple-element.27), channel_id=1, source_target_pairs={{0,3},{1,0},{2,1},{3,2},{4,7},{5,4},{6,5},{7,6},{8,11},{9,8},{10,9... | collective-permute-start | bytes 786440 | tf_op jit(solution)/shard_map/ppermute | solution.py:201
  22.9 19.5 %collective-permute-start.7 = (s16[144,512]{1,0:T(8,128)(2,1)S(1)}, s16[144,512]{1,0:T(8,128)(2,1)S(1)}, u32[]{:S(2)}, u32[]{:S(2)}) collective-permute-start(s16[144,512]{1,0:T(8,128)(2,1)S(1)} %get-tuple-element.30), channel_id=1, source_target_pairs={{0,1},{1,2},{2,3},{3,0},{4,5},{5,6},{6,7},{7,4},{8,9},{9,10},{10,1... | collective-permute-start | bytes 442376 | tf_op jit(solution)/shard_map/ppermute | solution.py:215
  23.6 30.2 %collective-permute-start.8 = (s16[144,512]{1,0:T(8,128)(2,1)S(1)}, s16[144,512]{1,0:T(8,128)(2,1)S(1)}, u32[]{:S(2)}, u32[]{:S(2)}) collective-permute-start(s16[144,512]{1,0:T(8,128)(2,1)S(1)} %get-tuple-element.31), channel_id=1, source_target_pairs={{0,2},{1,3},{2,0},{3,1},{4,6},{5,7},{6,4},{7,5},{8,10},{9,11},{10,... | collective-permute-start | bytes 442376 | tf_op jit(solution)/shard_map/ppermute | solution.py:215
  27.9 25.9 %collective-permute-start.9 = (s16[144,512]{1,0:T(8,128)(2,1)S(1)}, s16[144,512]{1,0:T(8,128)(2,1)S(1)}, u32[]{:S(2)}, u32[]{:S(2)}) collective-permute-start(s16[144,512]{1,0:T(8,128)(2,1)S(1)} %get-tuple-element.32), channel_id=1, source_target_pairs={{0,3},{1,0},{2,1},{3,2},{4,7},{5,4},{6,5},{7,6},{8,11},{9,8},{10,9... | collective-permute-start | bytes 442376 | tf_op jit(solution)/shard_map/ppermute | solution.py:215
  53.8 1.0 %copy-start.3 = (bf16[2,128,512]{2,1,0:T(8,128)(2,1)S(1)}, bf16[2,128,512]{2,1,0:T(8,128)(2,1)}, u32[]{:S(2)}) copy-start(bf16[2,128,512]{2,1,0:T(8,128)(2,1)} %get-tuple-element.24.refs_0_) | copy-start | bytes 786436
  56.5 9.5 %collective-permute-start.10 = (s16[144,512]{1,0:T(8,128)(2,1)S(1)}, s16[144,512]{1,0:T(8,128)(2,1)S(1)}, u32[]{:S(2)}, u32[]{:S(2)}) collective-permute-start(s16[144,512]{1,0:T(8,128)(2,1)S(1)} %get-tuple-element.34), channel_id=1, source_target_pairs={{0,1},{1,2},{2,3},{3,0},{4,5},{5,6},{6,7},{7,4},{8,9},{9,10},{10,1... | collective-permute-start | bytes 442376 | tf_op jit(solution)/shard_map/ppermute | solution.py:224
  60.2 11.0 %collective-permute-start.11 = (s16[144,512]{1,0:T(8,128)(2,1)S(1)}, s16[144,512]{1,0:T(8,128)(2,1)S(1)}, u32[]{:S(2)}, u32[]{:S(2)}) collective-permute-start(s16[144,512]{1,0:T(8,128)(2,1)S(1)} %get-tuple-element.35), channel_id=1, source_target_pairs={{0,2},{1,3},{2,0},{3,1},{4,6},{5,7},{6,4},{7,5},{8,10},{9,11},{10,... | collective-permute-start | bytes 442376 | tf_op jit(solution)/shard_map/ppermute | solution.py:224
  61.8 9.4 %collective-permute-start.12 = (s16[144,512]{1,0:T(8,128)(2,1)S(1)}, s16[144,512]{1,0:T(8,128)(2,1)S(1)}, u32[]{:S(2)}, u32[]{:S(2)}) collective-permute-start(s16[144,512]{1,0:T(8,128)(2,1)S(1)} %get-tuple-element.36), channel_id=1, source_target_pairs={{0,3},{1,0},{2,1},{3,2},{4,7},{5,4},{6,5},{7,6},{8,11},{9,8},{10,9... | collective-permute-start | bytes 442376 | tf_op jit(solution)/shard_map/ppermute | solution.py:224
  72.2 2.7 %collective-permute-start.13 = (f32[4,128,512]{2,1,0:T(8,128)S(1)}, f32[4,128,512]{2,1,0:T(8,128)S(1)}, u32[]{:S(2)}, u32[]{:S(2)}) collective-permute-start(f32[4,128,512]{2,1,0:T(8,128)S(1)} %get-tuple-element.38), channel_id=1, source_target_pairs={{0,4},{4,0},{8,12},{12,8},{16,20},{20,16},{24,28},{28,24},{1,5},{5... | collective-permute-start | bytes 3145736 | tf_op jit(solution)/shard_map/ppermute | solution.py:232
  75.3 6.7 %collective-permute-start.14 = (s16[144,512]{1,0:T(8,128)(2,1)S(1)}, s16[144,512]{1,0:T(8,128)(2,1)S(1)}, u32[]{:S(2)}, u32[]{:S(2)}) collective-permute-start(s16[144,512]{1,0:T(8,128)(2,1)S(1)} %get-tuple-element.40), channel_id=1, source_target_pairs={{0,8},{4,12},{8,0},{12,4},{16,24},{20,28},{24,16},{28,20},{1,9},{5... | collective-permute-start | bytes 442376 | tf_op jit(solution)/shard_map/ppermute | solution.py:236
  76.8 8.8 %collective-permute-start.15 = (s16[144,512]{1,0:T(8,128)(2,1)S(1)}, s16[144,512]{1,0:T(8,128)(2,1)S(1)}, u32[]{:S(2)}, u32[]{:S(2)}) collective-permute-start(s16[144,512]{1,0:T(8,128)(2,1)S(1)} %get-tuple-element.41), channel_id=1, source_target_pairs={{0,16},{4,20},{8,24},{12,28},{16,0},{20,4},{24,8},{28,12},{1,17},{... | collective-permute-start | bytes 442376 | tf_op jit(solution)/shard_map/ppermute | solution.py:236
  77.5 8.1 %collective-permute-start.16 = (s16[144,512]{1,0:T(8,128)(2,1)S(1)}, s16[144,512]{1,0:T(8,128)(2,1)S(1)}, u32[]{:S(2)}, u32[]{:S(2)}) collective-permute-start(s16[144,512]{1,0:T(8,128)(2,1)S(1)} %get-tuple-element.42), channel_id=1, source_target_pairs={{0,24},{4,28},{8,16},{12,20},{16,8},{20,12},{24,0},{28,4},{1,25},{... | collective-permute-start | bytes 442376 | tf_op jit(solution)/shard_map/ppermute | solution.py:236

commit v2 on v1

--- a/solution.py
+++ b/solution.py
@@ -8,8 +8,8 @@
 from jax.sharding import PartitionSpec as P
 
 
-GRID, LIMIT, LEVELS, HEAD = 1024.0, 32767.0, 256.0, 16
-PREPARE_BYTES = 63_400_000
+GRID, LIMIT, LEVELS, HEAD, HALVES = 1024.0, 32767.0, 256.0, 8, 2
+PREPARE_BYTES = 52_000_000
 VMEM_BYTES = 16 * 1024 * 1024
 VMEM = pl.BlockSpec(memory_space=pltpu.VMEM)
 SMEM = pl.BlockSpec(memory_space=pltpu.SMEM)
@@ -59,7 +59,7 @@
     copies = []
     start, mine = base(), me()
     for step in range(count):
-        term = term_ref[start + lax.rem(mine + step, count)]
+        term = term_ref[start + mine ^ step]
         copies.append(pltpu.make_async_copy(left_ref.at[term], outs[step].at[0], sem.at[2 * step]))
         copies.append(pltpu.make_async_copy(right_ref.at[term], outs[step].at[1], sem.at[2 * step + 1]))
     for copy in copies:
@@ -86,7 +86,7 @@
     start, mine = base(), me()
     chip, core = sec() // 2, lax.rem(sec(), 2)
     for step in range(count):
-        slot = lax.rem(mine + step, count)
+        slot = mine ^ step
         source = in_ref[start + slot]
         same = lax.rem(source, 2) == core
         for hop in range(chips):
@@ -100,12 +100,12 @@
 
 
 def task_kernel(me, count, *refs):
-    envs, psis, outs = refs[:count], refs[count : 2 * count], refs[2 * count : 3 * count]
-    high, low, right = refs[3 * count :]
-    rows = outs[0].shape[0]
+    envs, psis, outs = refs[:count], refs[count : 2 * count], refs[2 * count : -3]
+    high, low, right = refs[-3:]
+    rows, width = outs[0].shape
     mine = me()
     for step in range(count):
-        place = pl.ds(pl.multiple_of(lax.rem(mine + count - step, count) * rows, rows), rows)
+        place = pl.ds(pl.multiple_of((mine ^ step) * rows, rows), rows)
         right[place, :] = envs[step][1]
         psi = decode(psis[step])
         top = psi.astype(jnp.bfloat16)
@@ -118,14 +118,16 @@
     high[...] = top
     low[...] = (mixed - top.astype(jnp.float32)).astype(jnp.bfloat16)
     for step in range(count):
-        left = envs[(count - step) % count][0]
+        left = envs[step][0]
         part = jnp.dot(left, high[...], preferred_element_type=jnp.float32) + jnp.dot(
             left, low[...], preferred_element_type=jnp.float32
         )
-        if step == 0:
-            outs[0][...] = part
-        else:
-            encode(part, outs[step], False)
+        for half in range(HALVES):
+            piece, out = part[:, half * width : (half + 1) * width], outs[half * count + step]
+            if step == 0:
+                out[...] = piece
+            else:
+                encode(piece, out, False)
 
 
 def combine_kernel(base, sec, me, count, target_ref, *rest):
@@ -135,7 +137,7 @@
     keep[...] = jnp.zeros(keep.shape, jnp.float32)
     send[...] = jnp.zeros(send.shape, jnp.float32)
     for step in range(count):
-        target = target_ref[start + lax.rem(mine + count - step, count)]
+        target = target_ref[start + mine ^ step]
         hop = (target // 2) ^ chip
         part = parts[0][...] if step == 0 else decode(parts[step])
         mine_too = lax.rem(target, 2) == core
@@ -159,10 +161,13 @@
 
 
 def finish_kernel(chips, *refs):
-    total = refs[0][...]
-    for hop in range(1, chips):
-        total = total + decode(refs[hop])
-    refs[chips][...] = total
+    width = refs[0].shape[1]
+    for half in range(HALVES):
+        mine = refs[half * chips : (half + 1) * chips]
+        total = mine[0][...]
+        for hop in range(1, chips):
+            total = total + decode(mine[hop])
+        refs[-1][:, half * width : (half + 1) * width] = total
 
 
 def body(wavefunction, left_env, right_env, task_in, task_out, task_term):
@@ -177,16 +182,19 @@
     me = lambda: lax.axis_index("env")
 
     def along(shift):
-        return [(i, (i + shift) % count) for i in range(count)]
+        return [(i, i ^ shift) for i in range(count)]
 
     def across(hop):
         return [(i, i ^ (2 * hop)) for i in range(groups)]
 
     pair = [(i, i ^ 1) for i in range(groups)]
     code = jax.ShapeDtypeStruct((rows + HEAD, cols), jnp.int16)
-    stack = jax.ShapeDtypeStruct((chips, rows, cols), f32)
-
-    keep, send, held = None, None, None
+    width = cols // HALVES
+    part = jax.ShapeDtypeStruct((rows, width), f32)
+    piece = jax.ShapeDtypeStruct((rows + HEAD, width), jnp.int16)
+    stack = jax.ShapeDtypeStruct((chips, rows, width), f32)
+
+    keeps, sends, held = [None] * HALVES, [None] * HALVES, None
     for turn in range(per_device):
         base = lambda: (sec() * per_device + turn) * count
         partner_base = lambda: ((sec() ^ 1) * per_device + turn) * count
@@ -216,25 +224,34 @@
         full = count * rows
         parts = call(
             functools.partial(task_kernel, me, count),
-            [block] + [code] * (count - 1),
+            ([part] + [piece] * (count - 1)) * HALVES,
             [VMEM] * (2 * count),
             [pltpu.VMEM((full, cols), bf16)] * 3,
             flops=8 * full * full * cols,
         )(*envs, *psis)
-        parts = [parts[0]] + [lax.ppermute(parts[s], "env", along(s)) for s in range(1, count)]
-        kept, sends = call(
-            functools.partial(combine_kernel, base, sec, me, count),
-            [stack, stack],
-            [SMEM] + [VMEM] * count,
-        )(targets, *parts)
-        keep = kept if keep is None else keep + kept
-        send = sends if send is None else send + sends
-    other = lax.ppermute(send, "sec", pair)
-    sums = call(
-        functools.partial(join_kernel, chips), [block] + [code] * (chips - 1), [VMEM] * 2
-    )(keep, other)
-    sums = [sums[0]] + [lax.ppermute(sums[hop], "sec", across(hop)) for hop in range(1, chips)]
-    total = call(functools.partial(finish_kernel, chips), block, [VMEM] * chips)(*sums)
+        halves = [parts[half * count : (half + 1) * count] for half in range(HALVES)]
+        halves = [
+            [mine[0]] + [lax.ppermute(mine[s], "env", along(s)) for s in range(1, count)]
+            for mine in halves
+        ]
+        for half, mine in enumerate(halves):
+            kept, sent = call(
+                functools.partial(combine_kernel, base, sec, me, count),
+                [stack, stack],
+                [SMEM] + [VMEM] * count,
+            )(targets, *mine)
+            if turn:
+                kept, sent = keeps[half] + kept, sends[half] + sent
+            keeps[half], sends[half] = kept, sent
+    sums = []
+    for half in range(HALVES):
+        other = lax.ppermute(sends[half], "sec", pair)
+        mine = call(
+            functools.partial(join_kernel, chips), [part] + [piece] * (chips - 1), [VMEM] * 2
+        )(keeps[half], other)
+        sums += [mine[0]]
+        sums += [lax.ppermute(mine[hop], "sec", across(hop)) for hop in range(1, chips)]
+    total = call(functools.partial(finish_kernel, chips), block, [VMEM] * (chips * HALVES))(*sums)
     return total[None]
 
 

time: 87.2 us -> 84.6 us (0.970)
  waiting for transfers between devices: 52.8 us -> 41.6 us
  starting transfers between devices: 23 us -> 33.1 us
    ppermute x7 -> x14, waiting for transfers between devices: 18 us -> 9.97 us  [the longest x6 6.01 us: body(): lax.ppermute(mine[s], 'env', along(s))]
    ppermute x7 -> x14, starting transfers between devices: 9.76 us -> 16.9 us  [the longest x6 9.67 us: body(): lax.ppermute(mine[s], 'env', along(s))]
    ppermute x3, starting transfers between devices: 2.98 us -> 7.06 us  [body(): lax.ppermute(psis[s], 'env', along(s))]
    ppermute x3, waiting for transfers between devices: 13.4 us -> 10.8 us  [body(): lax.ppermute(envs[s], 'env', along(s))]
    pallas_call x1, Pallas kernels: 3.34 us -> 1.93 us  [body(): call(functools.partial(prepare_kernel, base, me, count), [env_block] * co...]
    ppermute x3, starting transfers between devices: 5.57 us -> 4.45 us  [body(): lax.ppermute(envs[s], 'env', along(s))]
    pallas_call x3 -> x4, Pallas kernels: 2.97 us -> 3.13 us  [the longest x1 1.9 us: body(): call(functools.partial(task_kernel, me, count), ([part] + [piece] * (coun...]
  transfers between devices with their start and end apart: 17 -> 24, of which waited for: 12 -> 12; matrix products, arithmetic and copies ran while one was open for 0% -> 0% of each run, Pallas kernels for 1% -> 3%
where the time goes in v2:
time: 84.6 us; the launch traced here: 84.4 us
  waiting for transfers between devices  41.6 us (49%)
  starting transfers between devices  33.1 us (39%)
  Pallas kernels  7.91 us (9%)
  local copies, waits for them, and re-layouts  1.61 us (2%)
    ppermute x3, waiting for transfers between devices, body(): lax.ppermute(psis[s], 'env', along(s))  14.6 us
    ppermute x3, waiting for transfers between devices, body(): lax.ppermute(envs[s], 'env', along(s))  10.8 us
    ppermute x6, starting transfers between devices, body(): lax.ppermute(mine[s], 'env', along(s))  9.67 us
    ppermute x6, starting transfers between devices, body(): lax.ppermute(mine[hop], 'sec', across(hop))  7.11 us
    ppermute x3, starting transfers between devices, body(): lax.ppermute(psis[s], 'env', along(s))  7.06 us
    ppermute x3, waiting for transfers between devices, body(): lax.ppermute(psi, 'sec', across(hop))  6.27 us
    ppermute x6, waiting for transfers between devices, body(): lax.ppermute(mine[s], 'env', along(s))  6.01 us
    ppermute x3, starting transfers between devices, body(): lax.ppermute(psi, 'sec', across(hop))  4.63 us
  transfers between devices with their start and end apart: 24, of which 12 were waited for; matrix products, arithmetic and copies ran while one was open for 0% of the time, Pallas kernels for 3%

profile of v2, /device:TPU:0, one launch (start us, length us, event | category | flops | bytes accessed | tf_op | source)
XLA Modules:
  0.0 84.4 jit_solution(4508141990987582511)
XLA Ops:
  0.0 0.9 %copy-done = f32[1,128,512]{2,1,0:T(8,128)S(1)} copy-done((f32[1,128,512]{2,1,0:T(8,128)S(1)}, f32[1,128,512]{2,1,0:T(8,128)}, u32[]{:S(2)}) %copy-start) | copy-done | bytes 262168
  1.0 0.7 copy-done.3
  1.6 1.9 %shard_map.64 = (bf16[2,128,512]{2,1,0:T(8,128)(2,1)S(1)}, bf16[2,128,512]{2,1,0:T(8,128)(2,1)S(1)}, bf16[2,128,512]{2,1,0:T(8,128)(2,1)S(1)}, bf16[2,128,512]{2,1,0:T(8,128)(2,1)S(1)}, s16[136,512]{1,0:T(8,128)(2,1)S(1)}) custom-call(s32[32]{0:T(128)S(1)} %copy-done.3, f32[128,512]{1,0:T(8,128)S(1)} %bitcast.3, bf16[34,128,512]{2,1,0:T(8,128)(2,1)} %left_ref.1, ...), custom_call_target="tpu_custom_call" | custom-call | flops 1 | bytes 1 | tf_op jit(solution)/shard_map/pallas_call | solution.py:202
  3.5 0.0 copy-start.2
  3.6 4.0 %collective-permute-start.5 = (s16[136,512]{1,0:T(8,128)(2,1)S(1)}, s16[136,512]{1,0:T(8,128)(2,1)S(1)}, u32[]{:S(2)}, u32[]{:S(2)}) collective-permute-start(s16[136,512]{1,0:T(8,128)(2,1)S(1)} %get-tuple-element.38.rest_0_), channel_id=1, source_target_pairs={{0,24},{4,28},{8,16},{12,20},{16,8},{20,12},{24,0},{28,4},{1,25},{... | collective-permute-start | bytes 417800 | tf_op jit(solution)/shard_map/ppermute | solution.py:211
  7.5 0.5 collective-permute-start.4
  8.1 0.1 collective-permute-start.3
  8.2 3.4 %collective-permute-done.5.rest_3_ = s16[136,512]{1,0:T(8,128)(2,1)S(1)} collective-permute-done((s16[136,512]{1,0:T(8,128)(2,1)S(1)}, s16[136,512]{1,0:T(8,128)(2,1)S(1)}, u32[]{:S(2)}, u32[]{:S(2)}) %collective-permute-start.5) | collective-permute-done | bytes 139296 | tf_op jit(solution)/shard_map/ppermute | solution.py:211
  11.6 2.6 %collective-permute-done.4.rest_2_ = s16[136,512]{1,0:T(8,128)(2,1)S(1)} collective-permute-done((s16[136,512]{1,0:T(8,128)(2,1)S(1)}, s16[136,512]{1,0:T(8,128)(2,1)S(1)}, u32[]{:S(2)}, u32[]{:S(2)}) %collective-permute-start.4) | collective-permute-done | bytes 139296 | tf_op jit(solution)/shard_map/ppermute | solution.py:211
  14.2 0.3 collective-permute-done.3.rest_1_
  14.5 0.7 shard_map.65
  15.2 0.1 collective-permute-start.6
  15.2 1.6 %collective-permute-start = (bf16[2,128,512]{2,1,0:T(8,128)(2,1)S(1)}, bf16[2,128,512]{2,1,0:T(8,128)(2,1)S(1)}, u32[]{:S(2)}, u32[]{:S(2)}) collective-permute-start(bf16[2,128,512]{2,1,0:T(8,128)(2,1)S(1)} %get-tuple-element.35), channel_id=1, source_target_pairs={{0,1},{1,0},{2,3},{3,2},{4,5},{5,4},{6,7},{7,6},{8,9},{9,8},{10,11... | collective-permute-start | bytes 786440 | tf_op jit(solution)/shard_map/ppermute | solution.py:209
  16.9 2.6 %collective-permute-start.1 = (bf16[2,128,512]{2,1,0:T(8,128)(2,1)S(1)}, bf16[2,128,512]{2,1,0:T(8,128)(2,1)S(1)}, u32[]{:S(2)}, u32[]{:S(2)}) collective-permute-start(bf16[2,128,512]{2,1,0:T(8,128)(2,1)S(1)} %get-tuple-element.36), channel_id=1, source_target_pairs={{0,2},{1,3},{2,0},{3,1},{4,6},{5,7},{6,4},{7,5},{8,10},{9,11},{10,... | collective-permute-start | bytes 786440 | tf_op jit(solution)/shard_map/ppermute | solution.py:209
  19.5 0.2 collective-permute-start.2
  19.7 0.7 shard_map.66
  20.4 0.7 collective-permute-start.7
  21.2 3.5 %collective-permute-start.8 = (s16[136,512]{1,0:T(8,128)(2,1)S(1)}, s16[136,512]{1,0:T(8,128)(2,1)S(1)}, u32[]{:S(2)}, u32[]{:S(2)}) collective-permute-start(s16[136,512]{1,0:T(8,128)(2,1)S(1)} %get-tuple-element.41), channel_id=1, source_target_pairs={{0,2},{1,3},{2,0},{3,1},{4,6},{5,7},{6,4},{7,5},{8,10},{9,11},{10,... | collective-permute-start | bytes 417800 | tf_op jit(solution)/shard_map/ppermute | solution.py:223
  24.7 5.0 %collective-permute-done.refs_1_ = bf16[2,128,512]{2,1,0:T(8,128)(2,1)S(1)} collective-permute-done((bf16[2,128,512]{2,1,0:T(8,128)(2,1)S(1)}, bf16[2,128,512]{2,1,0:T(8,128)(2,1)S(1)}, u32[]{:S(2)}, u32[]{:S(2)}) %collective-permute-start) | collective-permute-done | bytes 262176 | tf_op jit(solution)/shard_map/ppermute | solution.py:209
  29.6 2.8 %collective-permute-start.9 = (s16[136,512]{1,0:T(8,128)(2,1)S(1)}, s16[136,512]{1,0:T(8,128)(2,1)S(1)}, u32[]{:S(2)}, u32[]{:S(2)}) collective-permute-start(s16[136,512]{1,0:T(8,128)(2,1)S(1)} %get-tuple-element.42), channel_id=1, source_target_pairs={{0,3},{1,2},{2,1},{3,0},{4,7},{5,6},{6,5},{7,4},{8,11},{9,10},{10,... | collective-permute-start | bytes 417800 | tf_op jit(solution)/shard_map/ppermute | solution.py:223
  32.5 5.8 %collective-permute-done.1.refs_2_ = bf16[2,128,512]{2,1,0:T(8,128)(2,1)S(1)} collective-permute-done((bf16[2,128,512]{2,1,0:T(8,128)(2,1)S(1)}, bf16[2,128,512]{2,1,0:T(8,128)(2,1)S(1)}, u32[]{:S(2)}, u32[]{:S(2)}) %collective-permute-start.1) | collective-permute-done | bytes 262176 | tf_op jit(solution)/shard_map/ppermute | solution.py:209
  38.3 14.6 %collective-permute-done.8.refs_6_ = s16[136,512]{1,0:T(8,128)(2,1)S(1)} collective-permute-done((s16[136,512]{1,0:T(8,128)(2,1)S(1)}, s16[136,512]{1,0:T(8,128)(2,1)S(1)}, u32[]{:S(2)}, u32[]{:S(2)}) %collective-permute-start.8) | collective-permute-done | bytes 139296 | tf_op jit(solution)/shard_map/ppermute | solution.py:223
  52.9 1.9 %shard_map.67 = (f32[128,256]{1,0:T(8,128)S(1)}, s16[136,256]{1,0:T(8,128)(2,1)S(1)}, s16[136,256]{1,0:T(8,128)(2,1)S(1)}, s16[136,256]{1,0:T(8,128)(2,1)S(1)}, ...) custom-call(bf16[2,128,512]{2,1,0:T(8,128)(2,1)S(1)} %get-tuple-elem, ...), custom_call_target="tpu_custom_call" | custom-call | flops 1073741824 | bytes 1 | tf_op jit(solution)/shard_map/pallas_call | solution.py:225
  54.8 2.8 %collective-permute-start.17 = (s16[136,256]{1,0:T(8,128)(2,1)S(1)}, s16[136,256]{1,0:T(8,128)(2,1)S(1)}, u32[]{:S(2)}, u32[]{:S(2)}) collective-permute-start(s16[136,256]{1,0:T(8,128)(2,1)S(1)} %get-tuple-element.54), channel_id=1, source_target_pairs={{0,1},{1,0},{2,3},{3,2},{4,5},{5,4},{6,7},{7,6},{8,9},{9,8},{10,11... | collective-permute-start | bytes 208904 | tf_op jit(solution)/shard_map/ppermute | solution.py:234
  57.6 1.1 %collective-permute-start.18 = (s16[136,256]{1,0:T(8,128)(2,1)S(1)}, s16[136,256]{1,0:T(8,128)(2,1)S(1)}, u32[]{:S(2)}, u32[]{:S(2)}) collective-permute-start(s16[136,256]{1,0:T(8,128)(2,1)S(1)} %get-tuple-element.55), channel_id=1, source_target_pairs={{0,2},{1,3},{2,0},{3,1},{4,6},{5,7},{6,4},{7,5},{8,10},{9,11},{10,... | collective-permute-start | bytes 208904 | tf_op jit(solution)/shard_map/ppermute | solution.py:234
  58.7 1.4 %collective-permute-start.19 = (s16[136,256]{1,0:T(8,128)(2,1)S(1)}, s16[136,256]{1,0:T(8,128)(2,1)S(1)}, u32[]{:S(2)}, u32[]{:S(2)}) collective-permute-start(s16[136,256]{1,0:T(8,128)(2,1)S(1)} %get-tuple-element.56), channel_id=1, source_target_pairs={{0,3},{1,2},{2,1},{3,0},{4,7},{5,6},{6,5},{7,4},{8,11},{9,10},{10,... | collective-permute-start | bytes 208904 | tf_op jit(solution)/shard_map/ppermute | solution.py:234
  60.1 1.0 %collective-permute-start.10 = (s16[136,256]{1,0:T(8,128)(2,1)S(1)}, s16[136,256]{1,0:T(8,128)(2,1)S(1)}, u32[]{:S(2)}, u32[]{:S(2)}) collective-permute-start(s16[136,256]{1,0:T(8,128)(2,1)S(1)} %get-tuple-element.44), channel_id=1, source_target_pairs={{0,1},{1,0},{2,3},{3,2},{4,5},{5,4},{6,7},{7,6},{8,9},{9,8},{10,11... | collective-permute-start | bytes 208904 | tf_op jit(solution)/shard_map/ppermute | solution.py:234
  61.1 2.0 %collective-permute-start.11 = (s16[136,256]{1,0:T(8,128)(2,1)S(1)}, s16[136,256]{1,0:T(8,128)(2,1)S(1)}, u32[]{:S(2)}, u32[]{:S(2)}) collective-permute-start(s16[136,256]{1,0:T(8,128)(2,1)S(1)} %get-tuple-element.45), channel_id=1, source_target_pairs={{0,2},{1,3},{2,0},{3,1},{4,6},{5,7},{6,4},{7,5},{8,10},{9,11},{10,... | collective-permute-start | bytes 208904 | tf_op jit(solution)/shard_map/ppermute | solution.py:234
  63.1 1.4 %collective-permute-start.12 = (s16[136,256]{1,0:T(8,128)(2,1)S(1)}, s16[136,256]{1,0:T(8,128)(2,1)S(1)}, u32[]{:S(2)}, u32[]{:S(2)}) collective-permute-start(s16[136,256]{1,0:T(8,128)(2,1)S(1)} %get-tuple-element.46), channel_id=1, source_target_pairs={{0,3},{1,2},{2,1},{3,0},{4,7},{5,6},{6,5},{7,4},{8,11},{9,10},{10,... | collective-permute-start | bytes 208904 | tf_op jit(solution)/shard_map/ppermute | solution.py:234
  64.4 2.0 %collective-permute-done.18.rest_2_ = s16[136,256]{1,0:T(8,128)(2,1)S(1)} collective-permute-done((s16[136,256]{1,0:T(8,128)(2,1)S(1)}, s16[136,256]{1,0:T(8,128)(2,1)S(1)}, u32[]{:S(2)}, u32[]{:S(2)}) %collective-permute-start.18) | collective-permute-done | bytes 69664 | tf_op jit(solution)/shard_map/ppermute | solution.py:234
  66.5 0.7 shard_map.70
  67.2 0.1 collective-permute-start.20
  67.3 4.0 %collective-permute-done.11.rest_2_ = s16[136,256]{1,0:T(8,128)(2,1)S(1)} collective-permute-done((s16[136,256]{1,0:T(8,128)(2,1)S(1)}, s16[136,256]{1,0:T(8,128)(2,1)S(1)}, u32[]{:S(2)}, u32[]{:S(2)}) %collective-permute-start.11) | collective-permute-done | bytes 69664 | tf_op jit(solution)/shard_map/ppermute | solution.py:234
  71.3 0.7 shard_map.68
  72.0 0.1 collective-permute-start.13
  72.1 0.2 shard_map.71
  72.3 1.6 %collective-permute-start.21 = (s16[136,256]{1,0:T(8,128)(2,1)S(1)}, s16[136,256]{1,0:T(8,128)(2,1)S(1)}, u32[]{:S(2)}, u32[]{:S(2)}) collective-permute-start(s16[136,256]{1,0:T(8,128)(2,1)S(1)} %get-tuple-element.60), channel_id=1, source_target_pairs={{0,8},{4,12},{8,0},{12,4},{16,24},{20,28},{24,16},{28,20},{1,9},{5... | collective-permute-start | bytes 208904 | tf_op jit(solution)/shard_map/ppermute | solution.py:253
  73.9 0.7 collective-permute-start.22
  74.6 1.3 %collective-permute-start.23 = (s16[136,256]{1,0:T(8,128)(2,1)S(1)}, s16[136,256]{1,0:T(8,128)(2,1)S(1)}, u32[]{:S(2)}, u32[]{:S(2)}) collective-permute-start(s16[136,256]{1,0:T(8,128)(2,1)S(1)} %get-tuple-element.62), channel_id=1, source_target_pairs={{0,24},{4,28},{8,16},{12,20},{16,8},{20,12},{24,0},{28,4},{1,25},{... | collective-permute-start | bytes 208904 | tf_op jit(solution)/shard_map/ppermute | solution.py:253
  75.8 0.2 shard_map.69
  76.0 1.6 %collective-permute-start.14 = (s16[136,256]{1,0:T(8,128)(2,1)S(1)}, s16[136,256]{1,0:T(8,128)(2,1)S(1)}, u32[]{:S(2)}, u32[]{:S(2)}) collective-permute-start(s16[136,256]{1,0:T(8,128)(2,1)S(1)} %get-tuple-element.50), channel_id=1, source_target_pairs={{0,8},{4,12},{8,0},{12,4},{16,24},{20,28},{24,16},{28,20},{1,9},{5... | collective-permute-start | bytes 208904 | tf_op jit(solution)/shard_map/ppermute | solution.py:253
  77.6 0.7 collective-permute-start.15
  78.3 1.3 %collective-permute-start.16 = (s16[136,256]{1,0:T(8,128)(2,1)S(1)}, s16[136,256]{1,0:T(8,128)(2,1)S(1)}, u32[]{:S(2)}, u32[]{:S(2)}) collective-permute-start(s16[136,256]{1,0:T(8,128)(2,1)S(1)} %get-tuple-element.52), channel_id=1, source_target_pairs={{0,24},{4,28},{8,16},{12,20},{16,8},{20,12},{24,0},{28,4},{1,25},{... | collective-permute-start | bytes 208904 | tf_op jit(solution)/shard_map/ppermute | solution.py:253
  79.6 0.8 collective-permute-done.23.refs_7_
  80.4 0.6 collective-permute-done.14.refs_1_
  80.9 1.6 %collective-permute-done.15.refs_2_ = s16[136,256]{1,0:T(8,128)(2,1)S(1)} collective-permute-done((s16[136,256]{1,0:T(8,128)(2,1)S(1)}, s16[136,256]{1,0:T(8,128)(2,1)S(1)}, u32[]{:S(2)}, u32[]{:S(2)}) %collective-permute-start.15) | collective-permute-done | bytes 69664 | tf_op jit(solution)/shard_map/ppermute | solution.py:253
  82.6 1.0 %collective-permute-done.16.refs_3_ = s16[136,256]{1,0:T(8,128)(2,1)S(1)} collective-permute-done((s16[136,256]{1,0:T(8,128)(2,1)S(1)}, s16[136,256]{1,0:T(8,128)(2,1)S(1)}, u32[]{:S(2)}, u32[]{:S(2)}) %collective-permute-start.16) | collective-permute-done | bytes 69664 | tf_op jit(solution)/shard_map/ppermute | solution.py:253
  83.6 0.9 %shard_map.72 = f32[128,512]{1,0:T(8,128)} custom-call(f32[128,256]{1,0:T(8,128)S(1)} %get-tuple-element.49.refs_0_, s16[136,256]{1,0:T(8,128)(2,1)S(1)} %collective-permute-done.14.refs_1_, s16[136,256]{1,0:T(8,128)(2,1)S(1)} %collective-permute-done.15.refs_2_, s16[136,256]{1,0:T(8,128)(2,1)S(1)} %collective-permute-done.16.refs_3_, ...), custom_call_target="tpu_custom_call" | custom-call | flops 1 | bytes 1 | tf_op jit(solution)/shard_map/pallas_call | solution.py:254
  (17 shorter events, 0.0 us)
Async XLA Ops:
  0.0 0.9 %copy-start = (f32[1,128,512]{2,1,0:T(8,128)S(1)}, f32[1,128,512]{2,1,0:T(8,128)}, u32[]{:S(2)}) copy-start(f32[1,128,512]{2,1,0:T(8,128)} %param.6) | copy-start | bytes 786436
  1.0 0.7 copy-start.3
  1.6 12.9 %copy-start.1 = (s32[32]{0:T(128)S(1)}, s32[32]{0:T(128)}, u32[]{:S(2)}) copy-start(s32[32]{0:T(128)} %in_ref.3) | copy-start | bytes 388
  3.5 62.9 %copy-start.2 = (s32[32,1]{0,1:T(1,128)S(1)}, s32[32,1]{0,1:T(1,128)}, u32[]{:S(2)}) copy-start(s32[32,1]{0,1:T(1,128)} %param.10) | copy-start | bytes 388
  3.6 8.1 %collective-permute-start.5 = (s16[136,512]{1,0:T(8,128)(2,1)S(1)}, s16[136,512]{1,0:T(8,128)(2,1)S(1)}, u32[]{:S(2)}, u32[]{:S(2)}) collective-permute-start(s16[136,512]{1,0:T(8,128)(2,1)S(1)} %get-tuple-element.38.rest_0_), channel_id=1, source_target_pairs={{0,24},{4,28},{8,16},{12,20},{16,8},{20,12},{24,0},{28,4},{1,25},{... | collective-permute-start | bytes 417800 | tf_op jit(solution)/shard_map/ppermute | solution.py:211
  7.5 6.7 %collective-permute-start.4 = (s16[136,512]{1,0:T(8,128)(2,1)S(1)}, s16[136,512]{1,0:T(8,128)(2,1)S(1)}, u32[]{:S(2)}, u32[]{:S(2)}) collective-permute-start(s16[136,512]{1,0:T(8,128)(2,1)S(1)} %get-tuple-element.38.rest_0_), channel_id=1, source_target_pairs={{0,16},{4,20},{8,24},{12,28},{16,0},{20,4},{24,8},{28,12},{1,17},{... | collective-permute-start | bytes 417800 | tf_op jit(solution)/shard_map/ppermute | solution.py:211
  8.1 6.4 %collective-permute-start.3 = (s16[136,512]{1,0:T(8,128)(2,1)S(1)}, s16[136,512]{1,0:T(8,128)(2,1)S(1)}, u32[]{:S(2)}, u32[]{:S(2)}) collective-permute-start(s16[136,512]{1,0:T(8,128)(2,1)S(1)} %get-tuple-element.38.rest_0_), channel_id=1, source_target_pairs={{0,8},{4,12},{8,0},{12,4},{16,24},{20,28},{24,16},{28,20},{1,9},{5... | collective-permute-start | bytes 417800 | tf_op jit(solution)/shard_map/ppermute | solution.py:211
  15.2 4.5 %collective-permute-start.6 = (s16[4,136,512]{2,1,0:T(8,128)(2,1)S(1)}, s16[4,136,512]{2,1,0:T(8,128)(2,1)S(1)}, u32[]{:S(2)}, u32[]{:S(2)}) collective-permute-start(s16[4,136,512]{2,1,0:T(8,128)(2,1)S(1)} %shard_map.65), channel_id=1, source_target_pairs={{0,4},{4,0},{8,12},{12,8},{16,20},{20,16},{24,28},{28,24},{1,5},{5... | collective-permute-start | bytes 1671176 | tf_op jit(solution)/shard_map/ppermute | solution.py:217
  15.2 14.4 %collective-permute-start = (bf16[2,128,512]{2,1,0:T(8,128)(2,1)S(1)}, bf16[2,128,512]{2,1,0:T(8,128)(2,1)S(1)}, u32[]{:S(2)}, u32[]{:S(2)}) collective-permute-start(bf16[2,128,512]{2,1,0:T(8,128)(2,1)S(1)} %get-tuple-element.35), channel_id=1, source_target_pairs={{0,1},{1,0},{2,3},{3,2},{4,5},{5,4},{6,7},{7,6},{8,9},{9,8},{10,11... | collective-permute-start | bytes 786440 | tf_op jit(solution)/shard_map/ppermute | solution.py:209
  16.9 21.4 %collective-permute-start.1 = (bf16[2,128,512]{2,1,0:T(8,128)(2,1)S(1)}, bf16[2,128,512]{2,1,0:T(8,128)(2,1)S(1)}, u32[]{:S(2)}, u32[]{:S(2)}) collective-permute-start(bf16[2,128,512]{2,1,0:T(8,128)(2,1)S(1)} %get-tuple-element.36), channel_id=1, source_target_pairs={{0,2},{1,3},{2,0},{3,1},{4,6},{5,7},{6,4},{7,5},{8,10},{9,11},{10,... | collective-permute-start | bytes 786440 | tf_op jit(solution)/shard_map/ppermute | solution.py:209
  19.5 18.8 %collective-permute-start.2 = (bf16[2,128,512]{2,1,0:T(8,128)(2,1)S(1)}, bf16[2,128,512]{2,1,0:T(8,128)(2,1)S(1)}, u32[]{:S(2)}, u32[]{:S(2)}) collective-permute-start(bf16[2,128,512]{2,1,0:T(8,128)(2,1)S(1)} %get-tuple-element.37), channel_id=1, source_target_pairs={{0,3},{1,2},{2,1},{3,0},{4,7},{5,6},{6,5},{7,4},{8,11},{9,10},{10,... | collective-permute-start | bytes 786440 | tf_op jit(solution)/shard_map/ppermute | solution.py:209
  20.4 17.9 %collective-permute-start.7 = (s16[136,512]{1,0:T(8,128)(2,1)S(1)}, s16[136,512]{1,0:T(8,128)(2,1)S(1)}, u32[]{:S(2)}, u32[]{:S(2)}) collective-permute-start(s16[136,512]{1,0:T(8,128)(2,1)S(1)} %get-tuple-element.40), channel_id=1, source_target_pairs={{0,1},{1,0},{2,3},{3,2},{4,5},{5,4},{6,7},{7,6},{8,9},{9,8},{10,11... | collective-permute-start | bytes 417800 | tf_op jit(solution)/shard_map/ppermute | solution.py:223
  21.2 31.7 %collective-permute-start.8 = (s16[136,512]{1,0:T(8,128)(2,1)S(1)}, s16[136,512]{1,0:T(8,128)(2,1)S(1)}, u32[]{:S(2)}, u32[]{:S(2)}) collective-permute-start(s16[136,512]{1,0:T(8,128)(2,1)S(1)} %get-tuple-element.41), channel_id=1, source_target_pairs={{0,2},{1,3},{2,0},{3,1},{4,6},{5,7},{6,4},{7,5},{8,10},{9,11},{10,... | collective-permute-start | bytes 417800 | tf_op jit(solution)/shard_map/ppermute | solution.py:223
  29.6 23.2 %collective-permute-start.9 = (s16[136,512]{1,0:T(8,128)(2,1)S(1)}, s16[136,512]{1,0:T(8,128)(2,1)S(1)}, u32[]{:S(2)}, u32[]{:S(2)}) collective-permute-start(s16[136,512]{1,0:T(8,128)(2,1)S(1)} %get-tuple-element.42), channel_id=1, source_target_pairs={{0,3},{1,2},{2,1},{3,0},{4,7},{5,6},{6,5},{7,4},{8,11},{9,10},{10,... | collective-permute-start | bytes 417800 | tf_op jit(solution)/shard_map/ppermute | solution.py:223
  54.8 8.3 %collective-permute-start.17 = (s16[136,256]{1,0:T(8,128)(2,1)S(1)}, s16[136,256]{1,0:T(8,128)(2,1)S(1)}, u32[]{:S(2)}, u32[]{:S(2)}) collective-permute-start(s16[136,256]{1,0:T(8,128)(2,1)S(1)} %get-tuple-element.54), channel_id=1, source_target_pairs={{0,1},{1,0},{2,3},{3,2},{4,5},{5,4},{6,7},{7,6},{8,9},{9,8},{10,11... | collective-permute-start | bytes 208904 | tf_op jit(solution)/shard_map/ppermute | solution.py:234
  57.6 8.9 %collective-permute-start.18 = (s16[136,256]{1,0:T(8,128)(2,1)S(1)}, s16[136,256]{1,0:T(8,128)(2,1)S(1)}, u32[]{:S(2)}, u32[]{:S(2)}) collective-permute-start(s16[136,256]{1,0:T(8,128)(2,1)S(1)} %get-tuple-element.55), channel_id=1, source_target_pairs={{0,2},{1,3},{2,0},{3,1},{4,6},{5,7},{6,4},{7,5},{8,10},{9,11},{10,... | collective-permute-start | bytes 208904 | tf_op jit(solution)/shard_map/ppermute | solution.py:234
  58.7 7.8 %collective-permute-start.19 = (s16[136,256]{1,0:T(8,128)(2,1)S(1)}, s16[136,256]{1,0:T(8,128)(2,1)S(1)}, u32[]{:S(2)}, u32[]{:S(2)}) collective-permute-start(s16[136,256]{1,0:T(8,128)(2,1)S(1)} %get-tuple-element.56), channel_id=1, source_target_pairs={{0,3},{1,2},{2,1},{3,0},{4,7},{5,6},{6,5},{7,4},{8,11},{9,10},{10,... | collective-permute-start | bytes 208904 | tf_op jit(solution)/shard_map/ppermute | solution.py:234
  60.1 7.2 %collective-permute-start.10 = (s16[136,256]{1,0:T(8,128)(2,1)S(1)}, s16[136,256]{1,0:T(8,128)(2,1)S(1)}, u32[]{:S(2)}, u32[]{:S(2)}) collective-permute-start(s16[136,256]{1,0:T(8,128)(2,1)S(1)} %get-tuple-element.44), channel_id=1, source_target_pairs={{0,1},{1,0},{2,3},{3,2},{4,5},{5,4},{6,7},{7,6},{8,9},{9,8},{10,11... | collective-permute-start | bytes 208904 | tf_op jit(solution)/shard_map/ppermute | solution.py:234
  61.1 10.2 %collective-permute-start.11 = (s16[136,256]{1,0:T(8,128)(2,1)S(1)}, s16[136,256]{1,0:T(8,128)(2,1)S(1)}, u32[]{:S(2)}, u32[]{:S(2)}) collective-permute-start(s16[136,256]{1,0:T(8,128)(2,1)S(1)} %get-tuple-element.45), channel_id=1, source_target_pairs={{0,2},{1,3},{2,0},{3,1},{4,6},{5,7},{6,4},{7,5},{8,10},{9,11},{10,... | collective-permute-start | bytes 208904 | tf_op jit(solution)/shard_map/ppermute | solution.py:234
  63.1 8.2 %collective-permute-start.12 = (s16[136,256]{1,0:T(8,128)(2,1)S(1)}, s16[136,256]{1,0:T(8,128)(2,1)S(1)}, u32[]{:S(2)}, u32[]{:S(2)}) collective-permute-start(s16[136,256]{1,0:T(8,128)(2,1)S(1)} %get-tuple-element.46), channel_id=1, source_target_pairs={{0,3},{1,2},{2,1},{3,0},{4,7},{5,6},{6,5},{7,4},{8,11},{9,10},{10,... | collective-permute-start | bytes 208904 | tf_op jit(solution)/shard_map/ppermute | solution.py:234
  67.2 4.9 %collective-permute-start.20 = (f32[4,128,256]{2,1,0:T(8,128)S(1)}, f32[4,128,256]{2,1,0:T(8,128)S(1)}, u32[]{:S(2)}, u32[]{:S(2)}) collective-permute-start(f32[4,128,256]{2,1,0:T(8,128)S(1)} %get-tuple-element.58), channel_id=1, source_target_pairs={{0,4},{4,0},{8,12},{12,8},{16,20},{20,16},{24,28},{28,24},{1,5},{5... | collective-permute-start | bytes 1572872 | tf_op jit(solution)/shard_map/ppermute | solution.py:248
  72.0 3.8 %collective-permute-start.13 = (f32[4,128,256]{2,1,0:T(8,128)S(1)}, f32[4,128,256]{2,1,0:T(8,128)S(1)}, u32[]{:S(2)}, u32[]{:S(2)}) collective-permute-start(f32[4,128,256]{2,1,0:T(8,128)S(1)} %get-tuple-element.48), channel_id=1, source_target_pairs={{0,4},{4,0},{8,12},{12,8},{16,20},{20,16},{24,28},{28,24},{1,5},{5... | collective-permute-start | bytes 1572872 | tf_op jit(solution)/shard_map/ppermute | solution.py:248
  72.3 6.1 %collective-permute-start.21 = (s16[136,256]{1,0:T(8,128)(2,1)S(1)}, s16[136,256]{1,0:T(8,128)(2,1)S(1)}, u32[]{:S(2)}, u32[]{:S(2)}) collective-permute-start(s16[136,256]{1,0:T(8,128)(2,1)S(1)} %get-tuple-element.60), channel_id=1, source_target_pairs={{0,8},{4,12},{8,0},{12,4},{16,24},{20,28},{24,16},{28,20},{1,9},{5... | collective-permute-start | bytes 208904 | tf_op jit(solution)/shard_map/ppermute | solution.py:253
  73.9 5.7 %collective-permute-start.22 = (s16[136,256]{1,0:T(8,128)(2,1)S(1)}, s16[136,256]{1,0:T(8,128)(2,1)S(1)}, u32[]{:S(2)}, u32[]{:S(2)}) collective-permute-start(s16[136,256]{1,0:T(8,128)(2,1)S(1)} %get-tuple-element.61), channel_id=1, source_target_pairs={{0,16},{4,20},{8,24},{12,28},{16,0},{20,4},{24,8},{28,12},{1,17},{... | collective-permute-start | bytes 208904 | tf_op jit(solution)/shard_map/ppermute | solution.py:253
  74.6 5.8 %collective-permute-start.23 = (s16[136,256]{1,0:T(8,128)(2,1)S(1)}, s16[136,256]{1,0:T(8,128)(2,1)S(1)}, u32[]{:S(2)}, u32[]{:S(2)}) collective-permute-start(s16[136,256]{1,0:T(8,128)(2,1)S(1)} %get-tuple-element.62), channel_id=1, source_target_pairs={{0,24},{4,28},{8,16},{12,20},{16,8},{20,12},{24,0},{28,4},{1,25},{... | collective-permute-start | bytes 208904 | tf_op jit(solution)/shard_map/ppermute | solution.py:253
  76.0 4.9 %collective-permute-start.14 = (s16[136,256]{1,0:T(8,128)(2,1)S(1)}, s16[136,256]{1,0:T(8,128)(2,1)S(1)}, u32[]{:S(2)}, u32[]{:S(2)}) collective-permute-start(s16[136,256]{1,0:T(8,128)(2,1)S(1)} %get-tuple-element.50), channel_id=1, source_target_pairs={{0,8},{4,12},{8,0},{12,4},{16,24},{20,28},{24,16},{28,20},{1,9},{5... | collective-permute-start | bytes 208904 | tf_op jit(solution)/shard_map/ppermute | solution.py:253
  77.6 4.9 %collective-permute-start.15 = (s16[136,256]{1,0:T(8,128)(2,1)S(1)}, s16[136,256]{1,0:T(8,128)(2,1)S(1)}, u32[]{:S(2)}, u32[]{:S(2)}) collective-permute-start(s16[136,256]{1,0:T(8,128)(2,1)S(1)} %get-tuple-element.51), channel_id=1, source_target_pairs={{0,16},{4,20},{8,24},{12,28},{16,0},{20,4},{24,8},{28,12},{1,17},{... | collective-permute-start | bytes 208904 | tf_op jit(solution)/shard_map/ppermute | solution.py:253
  78.3 5.2 %collective-permute-start.16 = (s16[136,256]{1,0:T(8,128)(2,1)S(1)}, s16[136,256]{1,0:T(8,128)(2,1)S(1)}, u32[]{:S(2)}, u32[]{:S(2)}) collective-permute-start(s16[136,256]{1,0:T(8,128)(2,1)S(1)} %get-tuple-element.52), channel_id=1, source_target_pairs={{0,24},{4,28},{8,16},{12,20},{16,8},{20,12},{24,0},{28,4},{1,25},{... | collective-permute-start | bytes 208904 | tf_op jit(solution)/shard_map/ppermute | solution.py:253

commit v3 on v2

--- a/solution.py
+++ b/solution.py
@@ -8,8 +8,8 @@
 from jax.sharding import PartitionSpec as P
 
 
-GRID, LIMIT, LEVELS, HEAD, HALVES = 1024.0, 32767.0, 256.0, 8, 2
-PREPARE_BYTES = 52_000_000
+GRID, LIMIT, LEVELS, HEAD, HALVES = 1024.0, 32767.0, 256.0, 8, 1
+PICK_BYTES = 54_000_000
 VMEM_BYTES = 16 * 1024 * 1024
 VMEM = pl.BlockSpec(memory_space=pltpu.VMEM)
 SMEM = pl.BlockSpec(memory_space=pltpu.SMEM)
@@ -54,19 +54,22 @@
     return value * step + head[1:2] / GRID
 
 
-def prepare_kernel(base, me, count, term_ref, psi_ref, left_ref, right_ref, *rest):
-    outs, code, sem = rest[:count], rest[count], rest[count + 1]
+def pick_kernel(base, me, count, term_ref, left_ref, right_ref, *rest):
+    outs, sem = rest[:count], rest[count]
     copies = []
     start, mine = base(), me()
     for step in range(count):
-        term = term_ref[start + mine ^ step]
+        term = term_ref[start + (mine ^ step)]
         copies.append(pltpu.make_async_copy(left_ref.at[term], outs[step].at[0], sem.at[2 * step]))
         copies.append(pltpu.make_async_copy(right_ref.at[term], outs[step].at[1], sem.at[2 * step + 1]))
     for copy in copies:
         copy.start()
-    encode(psi_ref[...], code, True)
     for copy in copies:
         copy.wait()
+
+
+def encode_kernel(psi_ref, code):
+    encode(psi_ref[...], code, True)
 
 
 def partner_psi_kernel(base, sec, count, chips, in_ref, *rest):
@@ -187,6 +190,12 @@
     def across(hop):
         return [(i, i ^ (2 * hop)) for i in range(groups)]
 
+    def exchange(blocks):
+        got = list(blocks)
+        for s in far_first(count):
+            got[s] = lax.ppermute(blocks[s], "env", along(s))
+        return got
+
     pair = [(i, i ^ 1) for i in range(groups)]
     code = jax.ShapeDtypeStruct((rows + HEAD, cols), jnp.int16)
     width = cols // HALVES
@@ -199,15 +208,16 @@
         base = lambda: (sec() * per_device + turn) * count
         partner_base = lambda: ((sec() ^ 1) * per_device + turn) * count
         env_block = jax.ShapeDtypeStruct((2, rows, cols), bf16)
-        *envs, psi = call(
-            functools.partial(prepare_kernel, base, me, count),
-            [env_block] * count + [code],
-            [SMEM, VMEM, HBM, HBM],
+        envs = call(
+            functools.partial(pick_kernel, base, me, count),
+            [env_block] * count,
+            [SMEM, HBM, HBM],
             [pltpu.SemaphoreType.DMA((2 * count,))],
-            vmem=PREPARE_BYTES,
-        )(task_term, wavefunction[0], left_env, right_env)
-        envs = [envs[0]] + [lax.ppermute(envs[s], "env", along(s)) for s in range(1, count)]
+            vmem=PICK_BYTES,
+        )(task_term, left_env, right_env)
+        envs = exchange(envs)
         if held is None:
+            psi = call(encode_kernel, code, [VMEM])(wavefunction[0])
             held = [psi] + [lax.ppermute(psi, "sec", across(hop)) for hop in range(1, chips)]
         sent = call(
             functools.partial(partner_psi_kernel, partner_base, sec, count, chips),
@@ -220,7 +230,7 @@
             [code] * count,
             [SMEM] + [VMEM] * (chips + 1),
         )(task_in, *held, paired)
-        psis = [psis[0]] + [lax.ppermute(psis[s], "env", along(s)) for s in range(1, count)]
+        psis = exchange(psis)
         full = count * rows
         parts = call(
             functools.partial(task_kernel, me, count),
@@ -230,10 +240,7 @@
             flops=8 * full * full * cols,
         )(*envs, *psis)
         halves = [parts[half * count : (half + 1) * count] for half in range(HALVES)]
-        halves = [
-            [mine[0]] + [lax.ppermute(mine[s], "env", along(s)) for s in range(1, count)]
-            for mine in halves
-        ]
+        halves = [exchange(mine) for mine in halves]
         for half, mine in enumerate(halves):
             kept, sent = call(
                 functools.partial(combine_kernel, base, sec, me, count),
@@ -255,6 +262,10 @@
     return total[None]
 
 
+def far_first(count):
+    return sorted(range(1, count), key=lambda step: -step.bit_length())
+
+
 def solution(mesh):
     placed = (P("sec", "env", None), P(None, "env", None), P(None, "env", None), P(), P(), P())
     return jax.shard_map(

time: 84.6 us -> 86.6 us (1.024)
  waiting for transfers between devices: 41.6 us -> 51.4 us
  starting transfers between devices: 33.1 us -> 25.1 us
    ppermute x12 -> x9, waiting for transfers between devices: 31.4 us -> 36 us  [exchange(): got[s] = lax.ppermute(blocks[s], 'env', along(s))]
    ppermute x12 -> x9, starting transfers between devices: 21.2 us -> 16.8 us  [exchange(): got[s] = lax.ppermute(blocks[s], 'env', along(s))]
    ppermute x6 -> x3, starting transfers between devices: 7.11 us -> 3.55 us  [body(): lax.ppermute(mine[hop], 'sec', across(hop))]
    ppermute x2 -> x1, waiting for transfers between devices: 0.01 us -> 2.65 us  [body(): other = lax.ppermute(sends[half], 'sec', pair)]
    ppermute x6 -> x3, waiting for transfers between devices: 3.96 us -> 6.45 us  [body(): lax.ppermute(mine[hop], 'sec', across(hop))]
    unnamed x8 -> x10, local copies, waits for them, and re-layouts: 1.61 us -> 2.27 us
    pallas_call x1 -> x2, Pallas kernels: 1.93 us -> 2.05 us  [the longest x1 1.9 us: body(): call(functools.partial(pick_kernel, base, me, count), [env_block] * count...]
  transfers between devices with their start and end apart: 24 -> 17, of which waited for: 12 -> 11; matrix products, arithmetic and copies ran while one was open for 0% -> 0% of each run, Pallas kernels for 3% -> 3%
where the time goes in v3:
time: 86.6 us; the launch traced here: 86.4 us
  waiting for transfers between devices  51.4 us (59%)
  starting transfers between devices  25.1 us (29%)
  Pallas kernels  7.54 us (9%)
  local copies, waits for them, and re-layouts  2.27 us (3%)
    ppermute x9, waiting for transfers between devices, exchange(): got[s] = lax.ppermute(blocks[s], 'env', along(s))  36 us
    ppermute x9, starting transfers between devices, exchange(): got[s] = lax.ppermute(blocks[s], 'env', along(s))  16.8 us
    ppermute x3, waiting for transfers between devices, body(): lax.ppermute(mine[hop], 'sec', across(hop))  6.45 us
    ppermute x3, waiting for transfers between devices, body(): lax.ppermute(psi, 'sec', across(hop))  6.27 us
    ppermute x3, starting transfers between devices, body(): lax.ppermute(psi, 'sec', across(hop))  4.63 us
    ppermute x3, starting transfers between devices, body(): lax.ppermute(mine[hop], 'sec', across(hop))  3.55 us
    ppermute x1, waiting for transfers between devices, body(): other = lax.ppermute(sends[half], 'sec', pair)  2.65 us
    unnamed x10, local copies, waits for them, and re-layouts  2.27 us
  transfers between devices with their start and end apart: 17, of which 11 were waited for; matrix products, arithmetic and copies ran while one was open for 0% of the time, Pallas kernels for 3%

profile of v3, /device:TPU:0, one launch (start us, length us, event | category | flops | bytes accessed | tf_op | source)
XLA Modules:
  0.0 86.4 jit_solution(10553979085607462969)
XLA Ops:
  0.0 0.9 %copy-done = f32[1,128,512]{2,1,0:T(8,128)S(1)} copy-done((f32[1,128,512]{2,1,0:T(8,128)S(1)}, f32[1,128,512]{2,1,0:T(8,128)}, u32[]{:S(2)}) %copy-start) | copy-done | bytes 262168
  1.0 0.1 shard_map.65.rest_0_
  1.1 4.0 %collective-permute-start.5 = (s16[136,512]{1,0:T(8,128)(2,1)S(1)}, s16[136,512]{1,0:T(8,128)(2,1)S(1)}, u32[]{:S(2)}, u32[]{:S(2)}) collective-permute-start(s16[136,512]{1,0:T(8,128)(2,1)S(1)} %shard_map.65.rest_0_), channel_id=1, source_target_pairs={{0,24},{4,28},{8,16},{12,20},{16,8},{20,12},{24,0},{28,4},{1,25},{... | collective-permute-start | bytes 417800 | tf_op jit(solution)/shard_map/ppermute | solution.py:221
  5.1 0.5 collective-permute-start.4
  5.6 0.1 collective-permute-start.3
  5.7 3.4 %collective-permute-done.5.rest_3_ = s16[136,512]{1,0:T(8,128)(2,1)S(1)} collective-permute-done((s16[136,512]{1,0:T(8,128)(2,1)S(1)}, s16[136,512]{1,0:T(8,128)(2,1)S(1)}, u32[]{:S(2)}, u32[]{:S(2)}) %collective-permute-start.5) | collective-permute-done | bytes 139296 | tf_op jit(solution)/shard_map/ppermute | solution.py:221
  9.2 2.6 %collective-permute-done.4.rest_2_ = s16[136,512]{1,0:T(8,128)(2,1)S(1)} collective-permute-done((s16[136,512]{1,0:T(8,128)(2,1)S(1)}, s16[136,512]{1,0:T(8,128)(2,1)S(1)}, u32[]{:S(2)}, u32[]{:S(2)}) %collective-permute-start.4) | collective-permute-done | bytes 139296 | tf_op jit(solution)/shard_map/ppermute | solution.py:221
  11.7 0.3 collective-permute-done.3.rest_1_
  12.0 0.7 copy-done.1
  12.7 0.7 shard_map.66
  13.4 0.0 copy-start.2
  13.4 0.1 collective-permute-start.6
  13.5 0.0 copy-start.3
  13.5 0.6 copy-done.3
  14.1 1.9 %shard_map.64 = (bf16[2,128,512]{2,1,0:T(8,128)(2,1)S(1)}, bf16[2,128,512]{2,1,0:T(8,128)(2,1)S(1)}, bf16[2,128,512]{2,1,0:T(8,128)(2,1)S(1)}, bf16[2,128,512]{2,1,0:T(8,128)(2,1)S(1)}) custom-call(s32[32]{0:T(128)S(1)} %copy-done.3, bf16[34,128,512]{2,1,0:T(8,128)(2,1)} %left_ref.1, bf16[34,128,512]{2,1,0:T(8,128)(2,1)} %right_ref.1), custom_call_target="tpu_custom_call" | custom-call | flops 1 | bytes 1 | tf_op jit(solution)/shard_map/pallas_call | solution.py:211
  16.0 0.0 copy-start.4
  16.0 1.6 %collective-permute-start = (bf16[2,128,512]{2,1,0:T(8,128)(2,1)S(1)}, bf16[2,128,512]{2,1,0:T(8,128)(2,1)S(1)}, u32[]{:S(2)}, u32[]{:S(2)}) collective-permute-start(bf16[2,128,512]{2,1,0:T(8,128)(2,1)S(1)} %get-tuple-element.24), channel_id=1, source_target_pairs={{0,1},{1,0},{2,3},{3,2},{4,5},{5,4},{6,7},{7,6},{8,9},{9,8},{10,11... | collective-permute-start | bytes 786440 | tf_op jit(solution)/shard_map/ppermute | solution.py:196
  17.7 2.6 %collective-permute-start.1 = (bf16[2,128,512]{2,1,0:T(8,128)(2,1)S(1)}, bf16[2,128,512]{2,1,0:T(8,128)(2,1)S(1)}, u32[]{:S(2)}, u32[]{:S(2)}) collective-permute-start(bf16[2,128,512]{2,1,0:T(8,128)(2,1)S(1)} %get-tuple-element.25), channel_id=1, source_target_pairs={{0,2},{1,3},{2,0},{3,1},{4,6},{5,7},{6,4},{7,5},{8,10},{9,11},{10,... | collective-permute-start | bytes 786440 | tf_op jit(solution)/shard_map/ppermute | solution.py:196
  20.3 0.2 collective-permute-start.2
  20.5 0.0 collective-permute-done.6.rest_4_
  20.5 0.7 shard_map.67
  21.2 0.7 collective-permute-start.7
  22.0 3.5 %collective-permute-start.8 = (s16[136,512]{1,0:T(8,128)(2,1)S(1)}, s16[136,512]{1,0:T(8,128)(2,1)S(1)}, u32[]{:S(2)}, u32[]{:S(2)}) collective-permute-start(s16[136,512]{1,0:T(8,128)(2,1)S(1)} %get-tuple-element.29), channel_id=1, source_target_pairs={{0,2},{1,3},{2,0},{3,1},{4,6},{5,7},{6,4},{7,5},{8,10},{9,11},{10,... | collective-permute-start | bytes 417800 | tf_op jit(solution)/shard_map/ppermute | solution.py:196
  25.5 5.0 %collective-permute-done.refs_1_ = bf16[2,128,512]{2,1,0:T(8,128)(2,1)S(1)} collective-permute-done((bf16[2,128,512]{2,1,0:T(8,128)(2,1)S(1)}, bf16[2,128,512]{2,1,0:T(8,128)(2,1)S(1)}, u32[]{:S(2)}, u32[]{:S(2)}) %collective-permute-start) | collective-permute-done | bytes 262176 | tf_op jit(solution)/shard_map/ppermute | solution.py:196
  30.5 2.8 %collective-permute-start.9 = (s16[136,512]{1,0:T(8,128)(2,1)S(1)}, s16[136,512]{1,0:T(8,128)(2,1)S(1)}, u32[]{:S(2)}, u32[]{:S(2)}) collective-permute-start(s16[136,512]{1,0:T(8,128)(2,1)S(1)} %get-tuple-element.30), channel_id=1, source_target_pairs={{0,3},{1,2},{2,1},{3,0},{4,7},{5,6},{6,5},{7,4},{8,11},{9,10},{10,... | collective-permute-start | bytes 417800 | tf_op jit(solution)/shard_map/ppermute | solution.py:196
  33.3 5.8 %collective-permute-done.1.refs_2_ = bf16[2,128,512]{2,1,0:T(8,128)(2,1)S(1)} collective-permute-done((bf16[2,128,512]{2,1,0:T(8,128)(2,1)S(1)}, bf16[2,128,512]{2,1,0:T(8,128)(2,1)S(1)}, u32[]{:S(2)}, u32[]{:S(2)}) %collective-permute-start.1) | collective-permute-done | bytes 262176 | tf_op jit(solution)/shard_map/ppermute | solution.py:196
  39.1 0.0 collective-permute-done.2.refs_3_
  39.1 0.0 collective-permute-done.7.refs_5_
  39.1 14.6 %collective-permute-done.8.refs_6_ = s16[136,512]{1,0:T(8,128)(2,1)S(1)} collective-permute-done((s16[136,512]{1,0:T(8,128)(2,1)S(1)}, s16[136,512]{1,0:T(8,128)(2,1)S(1)}, u32[]{:S(2)}, u32[]{:S(2)}) %collective-permute-start.8) | collective-permute-done | bytes 139296 | tf_op jit(solution)/shard_map/ppermute | solution.py:196
  53.6 0.0 collective-permute-done.9.refs_7_
  53.7 1.9 %shard_map.68 = (f32[128,512]{1,0:T(8,128)S(1)}, s16[136,512]{1,0:T(8,128)(2,1)S(1)}, s16[136,512]{1,0:T(8,128)(2,1)S(1)}, s16[136,512]{1,0:T(8,128)(2,1)S(1)}) custom-call(bf16[2,128,512]{2,1,0:T(8,128)(2,1)S(1)} %get-tuple-element.23.refs_0_, bf16[2,128,512]{2,1,0:T(8,128)(2,1)S(1)} %collective-permute-done.refs_1_, ...), custom_call_target="tpu_custom_call" | custom-call | flops 1073741824 | bytes 1 | tf_op jit(solution)/shard_map/pallas_call | solution.py:235
  55.6 2.9 %collective-permute-start.10 = (s16[136,512]{1,0:T(8,128)(2,1)S(1)}, s16[136,512]{1,0:T(8,128)(2,1)S(1)}, u32[]{:S(2)}, u32[]{:S(2)}) collective-permute-start(s16[136,512]{1,0:T(8,128)(2,1)S(1)} %get-tuple-element.32), channel_id=1, source_target_pairs={{0,1},{1,0},{2,3},{3,2},{4,5},{5,4},{6,7},{7,6},{8,9},{9,8},{10,11... | collective-permute-start | bytes 417800 | tf_op jit(solution)/shard_map/ppermute | solution.py:196
  58.4 1.1 %collective-permute-start.11 = (s16[136,512]{1,0:T(8,128)(2,1)S(1)}, s16[136,512]{1,0:T(8,128)(2,1)S(1)}, u32[]{:S(2)}, u32[]{:S(2)}) collective-permute-start(s16[136,512]{1,0:T(8,128)(2,1)S(1)} %get-tuple-element.33), channel_id=1, source_target_pairs={{0,2},{1,3},{2,0},{3,1},{4,6},{5,7},{6,4},{7,5},{8,10},{9,11},{10,... | collective-permute-start | bytes 417800 | tf_op jit(solution)/shard_map/ppermute | solution.py:196
  59.5 1.4 %collective-permute-start.12 = (s16[136,512]{1,0:T(8,128)(2,1)S(1)}, s16[136,512]{1,0:T(8,128)(2,1)S(1)}, u32[]{:S(2)}, u32[]{:S(2)}) collective-permute-start(s16[136,512]{1,0:T(8,128)(2,1)S(1)} %get-tuple-element.34), channel_id=1, source_target_pairs={{0,3},{1,2},{2,1},{3,0},{4,7},{5,6},{6,5},{7,4},{8,11},{9,10},{10,... | collective-permute-start | bytes 417800 | tf_op jit(solution)/shard_map/ppermute | solution.py:196
  60.9 2.3 %collective-permute-done.10.rest_1_ = s16[136,512]{1,0:T(8,128)(2,1)S(1)} collective-permute-done((s16[136,512]{1,0:T(8,128)(2,1)S(1)}, s16[136,512]{1,0:T(8,128)(2,1)S(1)}, u32[]{:S(2)}, u32[]{:S(2)}) %collective-permute-start.10) | collective-permute-done | bytes 139296 | tf_op jit(solution)/shard_map/ppermute | solution.py:196
  63.2 8.3 %collective-permute-done.11.rest_2_ = s16[136,512]{1,0:T(8,128)(2,1)S(1)} collective-permute-done((s16[136,512]{1,0:T(8,128)(2,1)S(1)}, s16[136,512]{1,0:T(8,128)(2,1)S(1)}, u32[]{:S(2)}, u32[]{:S(2)}) %collective-permute-start.11) | collective-permute-done | bytes 139296 | tf_op jit(solution)/shard_map/ppermute | solution.py:196
  71.5 0.0 collective-permute-done.12.rest_3_
  71.5 0.9 %shard_map.69 = (f32[4,128,512]{2,1,0:T(8,128)S(1)}, f32[4,128,512]{2,1,0:T(8,128)S(1)}) custom-call(s32[32]{0:T(128)S(1)} %bitcast.4, f32[128,512]{1,0:T(8,128)S(1)} %get-tuple-element.31.rest_0_, s16[136,512]{1,0:T(8,128)(2,1)S(1)} %collective-permute-done.10.rest_1_, s16[136,512]{1,0:T(8,128)(2,1)S(1)} %collective-permute-done.11.rest_2_, ...), custom_call_target="tpu_custom_call" | custom-call | flops 1 | bytes 1 | tf_op jit(solution)/shard_map/pallas_call | solution.py:245
  72.4 0.1 collective-permute-start.13
  72.5 2.6 %collective-permute-done.13.other = f32[4,128,512]{2,1,0:T(8,128)S(1)} collective-permute-done((f32[4,128,512]{2,1,0:T(8,128)S(1)}, f32[4,128,512]{2,1,0:T(8,128)S(1)}, u32[]{:S(2)}, u32[]{:S(2)}) %collective-permute-start.13) | collective-permute-done | bytes 1048608 | tf_op jit(solution)/shard_map/ppermute | solution.py:255
  75.2 0.4 shard_map.70
  75.6 1.6 %collective-permute-start.14 = (s16[136,512]{1,0:T(8,128)(2,1)S(1)}, s16[136,512]{1,0:T(8,128)(2,1)S(1)}, u32[]{:S(2)}, u32[]{:S(2)}) collective-permute-start(s16[136,512]{1,0:T(8,128)(2,1)S(1)} %get-tuple-element.38), channel_id=1, source_target_pairs={{0,8},{4,12},{8,0},{12,4},{16,24},{20,28},{24,16},{28,20},{1,9},{5... | collective-permute-start | bytes 417800 | tf_op jit(solution)/shard_map/ppermute | solution.py:260
  77.2 0.7 collective-permute-start.15
  77.9 1.3 %collective-permute-start.16 = (s16[136,512]{1,0:T(8,128)(2,1)S(1)}, s16[136,512]{1,0:T(8,128)(2,1)S(1)}, u32[]{:S(2)}, u32[]{:S(2)}) collective-permute-start(s16[136,512]{1,0:T(8,128)(2,1)S(1)} %get-tuple-element.40), channel_id=1, source_target_pairs={{0,24},{4,28},{8,16},{12,20},{16,8},{20,12},{24,0},{28,4},{1,25},{... | collective-permute-start | bytes 417800 | tf_op jit(solution)/shard_map/ppermute | solution.py:260
  79.1 2.8 %collective-permute-done.14.refs_1_ = s16[136,512]{1,0:T(8,128)(2,1)S(1)} collective-permute-done((s16[136,512]{1,0:T(8,128)(2,1)S(1)}, s16[136,512]{1,0:T(8,128)(2,1)S(1)}, u32[]{:S(2)}, u32[]{:S(2)}) %collective-permute-start.14) | collective-permute-done | bytes 139296 | tf_op jit(solution)/shard_map/ppermute | solution.py:260
  81.9 3.7 %collective-permute-done.15.refs_2_ = s16[136,512]{1,0:T(8,128)(2,1)S(1)} collective-permute-done((s16[136,512]{1,0:T(8,128)(2,1)S(1)}, s16[136,512]{1,0:T(8,128)(2,1)S(1)}, u32[]{:S(2)}, u32[]{:S(2)}) %collective-permute-start.15) | collective-permute-done | bytes 139296 | tf_op jit(solution)/shard_map/ppermute | solution.py:260
  85.6 0.0 collective-permute-done.16.refs_3_
  85.6 0.8 shard_map.71
  (4 shorter events, 0.0 us)
Async XLA Ops:
  0.0 0.9 %copy-start = (f32[1,128,512]{2,1,0:T(8,128)S(1)}, f32[1,128,512]{2,1,0:T(8,128)}, u32[]{:S(2)}) copy-start(f32[1,128,512]{2,1,0:T(8,128)} %param.6) | copy-start | bytes 786436
  1.1 8.1 %collective-permute-start.5 = (s16[136,512]{1,0:T(8,128)(2,1)S(1)}, s16[136,512]{1,0:T(8,128)(2,1)S(1)}, u32[]{:S(2)}, u32[]{:S(2)}) collective-permute-start(s16[136,512]{1,0:T(8,128)(2,1)S(1)} %shard_map.65.rest_0_), channel_id=1, source_target_pairs={{0,24},{4,28},{8,16},{12,20},{16,8},{20,12},{24,0},{28,4},{1,25},{... | collective-permute-start | bytes 417800 | tf_op jit(solution)/shard_map/ppermute | solution.py:221
  5.1 6.7 %collective-permute-start.4 = (s16[136,512]{1,0:T(8,128)(2,1)S(1)}, s16[136,512]{1,0:T(8,128)(2,1)S(1)}, u32[]{:S(2)}, u32[]{:S(2)}) collective-permute-start(s16[136,512]{1,0:T(8,128)(2,1)S(1)} %shard_map.65.rest_0_), channel_id=1, source_target_pairs={{0,16},{4,20},{8,24},{12,28},{16,0},{20,4},{24,8},{28,12},{1,17},{... | collective-permute-start | bytes 417800 | tf_op jit(solution)/shard_map/ppermute | solution.py:221
  5.6 6.4 %collective-permute-start.3 = (s16[136,512]{1,0:T(8,128)(2,1)S(1)}, s16[136,512]{1,0:T(8,128)(2,1)S(1)}, u32[]{:S(2)}, u32[]{:S(2)}) collective-permute-start(s16[136,512]{1,0:T(8,128)(2,1)S(1)} %shard_map.65.rest_0_), channel_id=1, source_target_pairs={{0,8},{4,12},{8,0},{12,4},{16,24},{20,28},{24,16},{28,20},{1,9},{5... | collective-permute-start | bytes 417800 | tf_op jit(solution)/shard_map/ppermute | solution.py:221
  12.0 0.7 copy-start.1
  13.4 7.1 %copy-start.2 = (s32[32]{0:T(128)S(1)}, s32[32]{0:T(128)}, u32[]{:S(2)}) copy-start(s32[32]{0:T(128)} %in_ref.3) | copy-start | bytes 388
  13.4 7.1 %collective-permute-start.6 = (s16[4,136,512]{2,1,0:T(8,128)(2,1)S(1)}, s16[4,136,512]{2,1,0:T(8,128)(2,1)S(1)}, u32[]{:S(2)}, u32[]{:S(2)}) collective-permute-start(s16[4,136,512]{2,1,0:T(8,128)(2,1)S(1)} %shard_map.66), channel_id=1, source_target_pairs={{0,4},{4,0},{8,12},{12,8},{16,20},{20,16},{24,28},{28,24},{1,5},{5... | collective-permute-start | bytes 1671176 | tf_op jit(solution)/shard_map/ppermute | solution.py:227
  13.5 0.7 copy-start.3
  16.0 55.5 %copy-start.4 = (s32[32,1]{0,1:T(1,128)S(1)}, s32[32,1]{0,1:T(1,128)}, u32[]{:S(2)}) copy-start(s32[32,1]{0,1:T(1,128)} %param.10) | copy-start | bytes 388
  16.0 14.4 %collective-permute-start = (bf16[2,128,512]{2,1,0:T(8,128)(2,1)S(1)}, bf16[2,128,512]{2,1,0:T(8,128)(2,1)S(1)}, u32[]{:S(2)}, u32[]{:S(2)}) collective-permute-start(bf16[2,128,512]{2,1,0:T(8,128)(2,1)S(1)} %get-tuple-element.24), channel_id=1, source_target_pairs={{0,1},{1,0},{2,3},{3,2},{4,5},{5,4},{6,7},{7,6},{8,9},{9,8},{10,11... | collective-permute-start | bytes 786440 | tf_op jit(solution)/shard_map/ppermute | solution.py:196
  17.7 21.4 %collective-permute-start.1 = (bf16[2,128,512]{2,1,0:T(8,128)(2,1)S(1)}, bf16[2,128,512]{2,1,0:T(8,128)(2,1)S(1)}, u32[]{:S(2)}, u32[]{:S(2)}) collective-permute-start(bf16[2,128,512]{2,1,0:T(8,128)(2,1)S(1)} %get-tuple-element.25), channel_id=1, source_target_pairs={{0,2},{1,3},{2,0},{3,1},{4,6},{5,7},{6,4},{7,5},{8,10},{9,11},{10,... | collective-permute-start | bytes 786440 | tf_op jit(solution)/shard_map/ppermute | solution.py:196
  20.3 18.8 %collective-permute-start.2 = (bf16[2,128,512]{2,1,0:T(8,128)(2,1)S(1)}, bf16[2,128,512]{2,1,0:T(8,128)(2,1)S(1)}, u32[]{:S(2)}, u32[]{:S(2)}) collective-permute-start(bf16[2,128,512]{2,1,0:T(8,128)(2,1)S(1)} %get-tuple-element.26), channel_id=1, source_target_pairs={{0,3},{1,2},{2,1},{3,0},{4,7},{5,6},{6,5},{7,4},{8,11},{9,10},{10,... | collective-permute-start | bytes 786440 | tf_op jit(solution)/shard_map/ppermute | solution.py:196
  21.2 17.9 %collective-permute-start.7 = (s16[136,512]{1,0:T(8,128)(2,1)S(1)}, s16[136,512]{1,0:T(8,128)(2,1)S(1)}, u32[]{:S(2)}, u32[]{:S(2)}) collective-permute-start(s16[136,512]{1,0:T(8,128)(2,1)S(1)} %get-tuple-element.28), channel_id=1, source_target_pairs={{0,1},{1,0},{2,3},{3,2},{4,5},{5,4},{6,7},{7,6},{8,9},{9,8},{10,11... | collective-permute-start | bytes 417800 | tf_op jit(solution)/shard_map/ppermute | solution.py:196
  22.0 31.7 %collective-permute-start.8 = (s16[136,512]{1,0:T(8,128)(2,1)S(1)}, s16[136,512]{1,0:T(8,128)(2,1)S(1)}, u32[]{:S(2)}, u32[]{:S(2)}) collective-permute-start(s16[136,512]{1,0:T(8,128)(2,1)S(1)} %get-tuple-element.29), channel_id=1, source_target_pairs={{0,2},{1,3},{2,0},{3,1},{4,6},{5,7},{6,4},{7,5},{8,10},{9,11},{10,... | collective-permute-start | bytes 417800 | tf_op jit(solution)/shard_map/ppermute | solution.py:196
  30.5 23.2 %collective-permute-start.9 = (s16[136,512]{1,0:T(8,128)(2,1)S(1)}, s16[136,512]{1,0:T(8,128)(2,1)S(1)}, u32[]{:S(2)}, u32[]{:S(2)}) collective-permute-start(s16[136,512]{1,0:T(8,128)(2,1)S(1)} %get-tuple-element.30), channel_id=1, source_target_pairs={{0,3},{1,2},{2,1},{3,0},{4,7},{5,6},{6,5},{7,4},{8,11},{9,10},{10,... | collective-permute-start | bytes 417800 | tf_op jit(solution)/shard_map/ppermute | solution.py:196
  55.6 7.6 %collective-permute-start.10 = (s16[136,512]{1,0:T(8,128)(2,1)S(1)}, s16[136,512]{1,0:T(8,128)(2,1)S(1)}, u32[]{:S(2)}, u32[]{:S(2)}) collective-permute-start(s16[136,512]{1,0:T(8,128)(2,1)S(1)} %get-tuple-element.32), channel_id=1, source_target_pairs={{0,1},{1,0},{2,3},{3,2},{4,5},{5,4},{6,7},{7,6},{8,9},{9,8},{10,11... | collective-permute-start | bytes 417800 | tf_op jit(solution)/shard_map/ppermute | solution.py:196
  58.4 13.1 %collective-permute-start.11 = (s16[136,512]{1,0:T(8,128)(2,1)S(1)}, s16[136,512]{1,0:T(8,128)(2,1)S(1)}, u32[]{:S(2)}, u32[]{:S(2)}) collective-permute-start(s16[136,512]{1,0:T(8,128)(2,1)S(1)} %get-tuple-element.33), channel_id=1, source_target_pairs={{0,2},{1,3},{2,0},{3,1},{4,6},{5,7},{6,4},{7,5},{8,10},{9,11},{10,... | collective-permute-start | bytes 417800 | tf_op jit(solution)/shard_map/ppermute | solution.py:196
  59.5 12.0 %collective-permute-start.12 = (s16[136,512]{1,0:T(8,128)(2,1)S(1)}, s16[136,512]{1,0:T(8,128)(2,1)S(1)}, u32[]{:S(2)}, u32[]{:S(2)}) collective-permute-start(s16[136,512]{1,0:T(8,128)(2,1)S(1)} %get-tuple-element.34), channel_id=1, source_target_pairs={{0,3},{1,2},{2,1},{3,0},{4,7},{5,6},{6,5},{7,4},{8,11},{9,10},{10,... | collective-permute-start | bytes 417800 | tf_op jit(solution)/shard_map/ppermute | solution.py:196
  72.4 2.7 %collective-permute-start.13 = (f32[4,128,512]{2,1,0:T(8,128)S(1)}, f32[4,128,512]{2,1,0:T(8,128)S(1)}, u32[]{:S(2)}, u32[]{:S(2)}) collective-permute-start(f32[4,128,512]{2,1,0:T(8,128)S(1)} %get-tuple-element.36), channel_id=1, source_target_pairs={{0,4},{4,0},{8,12},{12,8},{16,20},{20,16},{24,28},{28,24},{1,5},{5... | collective-permute-start | bytes 3145736 | tf_op jit(solution)/shard_map/ppermute | solution.py:255
  75.6 6.3 %collective-permute-start.14 = (s16[136,512]{1,0:T(8,128)(2,1)S(1)}, s16[136,512]{1,0:T(8,128)(2,1)S(1)}, u32[]{:S(2)}, u32[]{:S(2)}) collective-permute-start(s16[136,512]{1,0:T(8,128)(2,1)S(1)} %get-tuple-element.38), channel_id=1, source_target_pairs={{0,8},{4,12},{8,0},{12,4},{16,24},{20,28},{24,16},{28,20},{1,9},{5... | collective-permute-start | bytes 417800 | tf_op jit(solution)/shard_map/ppermute | solution.py:260
  77.2 8.4 %collective-permute-start.15 = (s16[136,512]{1,0:T(8,128)(2,1)S(1)}, s16[136,512]{1,0:T(8,128)(2,1)S(1)}, u32[]{:S(2)}, u32[]{:S(2)}) collective-permute-start(s16[136,512]{1,0:T(8,128)(2,1)S(1)} %get-tuple-element.39), channel_id=1, source_target_pairs={{0,16},{4,20},{8,24},{12,28},{16,0},{20,4},{24,8},{28,12},{1,17},{... | collective-permute-start | bytes 417800 | tf_op jit(solution)/shard_map/ppermute | solution.py:260
  77.9 7.7 %collective-permute-start.16 = (s16[136,512]{1,0:T(8,128)(2,1)S(1)}, s16[136,512]{1,0:T(8,128)(2,1)S(1)}, u32[]{:S(2)}, u32[]{:S(2)}) collective-permute-start(s16[136,512]{1,0:T(8,128)(2,1)S(1)} %get-tuple-element.40), channel_id=1, source_target_pairs={{0,24},{4,28},{8,16},{12,20},{16,8},{20,12},{24,0},{28,4},{1,25},{... | collective-permute-start | bytes 417800 | tf_op jit(solution)/shard_map/ppermute | solution.py:260

commit v4 on v3

--- a/solution.py
+++ b/solution.py
@@ -8,7 +8,7 @@
 from jax.sharding import PartitionSpec as P
 
 
-GRID, LIMIT, LEVELS, HEAD, HALVES = 1024.0, 32767.0, 256.0, 8, 1
+GRID, LIMIT, LEVELS, HEAD, HALVES = 1024.0, 32767.0, 256.0, 8, 2
 PICK_BYTES = 54_000_000
 VMEM_BYTES = 16 * 1024 * 1024
 VMEM = pl.BlockSpec(memory_space=pltpu.VMEM)
@@ -55,13 +55,23 @@
 
 
 def pick_kernel(base, me, count, term_ref, left_ref, right_ref, *rest):
-    outs, sem = rest[:count], rest[count]
+    outs, sem = rest[:-1], rest[-1]
+    _, cols = left_ref.shape[1:]
+    width = cols // HALVES
     copies = []
     start, mine = base(), me()
     for step in range(count):
         term = term_ref[start + (mine ^ step)]
-        copies.append(pltpu.make_async_copy(left_ref.at[term], outs[step].at[0], sem.at[2 * step]))
-        copies.append(pltpu.make_async_copy(right_ref.at[term], outs[step].at[1], sem.at[2 * step + 1]))
+        copies.append((left_ref.at[term], outs[step].at[:, pl.ds(0, cols)]))
+        for half in range(HALVES):
+            out = outs[half * count + step]
+            copies.append(
+                (
+                    right_ref.at[term, :, pl.ds(half * width, width)],
+                    out if half else out.at[:, pl.ds(cols, width)],
+                )
+            )
+    copies = [pltpu.make_async_copy(*copy, sem.at[i]) for i, copy in enumerate(copies)]
     for copy in copies:
         copy.start()
     for copy in copies:
@@ -102,14 +112,15 @@
             outs[step][...] = paired[slot]
 
 
-def task_kernel(me, count, *refs):
-    envs, psis, outs = refs[:count], refs[count : 2 * count], refs[2 * count : -3]
+def task_kernel(me, count, half, *refs):
+    envs, psis, lates, outs = refs[:count], refs[count : 2 * count], refs[2 * count : -3 - count], refs[-3 - count : -3]
     high, low, right = refs[-3:]
     rows, width = outs[0].shape
+    cols = high.shape[1]
     mine = me()
     for step in range(count):
         place = pl.ds(pl.multiple_of((mine ^ step) * rows, rows), rows)
-        right[place, :] = envs[step][1]
+        right[place, :] = lates[step][...] if half else envs[step][:, pl.ds(cols, width)]
         psi = decode(psis[step])
         top = psi.astype(jnp.bfloat16)
         high[place, :] = top
@@ -118,19 +129,16 @@
         low[...], right[...], preferred_element_type=jnp.float32
     )
     top = mixed.astype(jnp.bfloat16)
-    high[...] = top
-    low[...] = (mixed - top.astype(jnp.float32)).astype(jnp.bfloat16)
-    for step in range(count):
-        left = envs[step][0]
-        part = jnp.dot(left, high[...], preferred_element_type=jnp.float32) + jnp.dot(
-            left, low[...], preferred_element_type=jnp.float32
+    rest = (mixed - top.astype(jnp.float32)).astype(jnp.bfloat16)
+    for step in far_first(count) + [0]:
+        left = envs[step][:, pl.ds(0, cols)]
+        part = jnp.dot(left, top, preferred_element_type=jnp.float32) + jnp.dot(
+            left, rest, preferred_element_type=jnp.float32
         )
-        for half in range(HALVES):
-            piece, out = part[:, half * width : (half + 1) * width], outs[half * count + step]
-            if step == 0:
-                out[...] = piece
-            else:
-                encode(piece, out, False)
+        if step == 0:
+            outs[step][...] = part
+        else:
+            encode(part, outs[step], False)
 
 
 def combine_kernel(base, sec, me, count, target_ref, *rest):
@@ -207,15 +215,16 @@
     for turn in range(per_device):
         base = lambda: (sec() * per_device + turn) * count
         partner_base = lambda: ((sec() ^ 1) * per_device + turn) * count
-        env_block = jax.ShapeDtypeStruct((2, rows, cols), bf16)
-        envs = call(
+        early = jax.ShapeDtypeStruct((rows, cols + width), bf16)
+        late = jax.ShapeDtypeStruct((rows, width), bf16)
+        picked = call(
             functools.partial(pick_kernel, base, me, count),
-            [env_block] * count,
+            [early] * count + [late] * (count * (HALVES - 1)),
             [SMEM, HBM, HBM],
-            [pltpu.SemaphoreType.DMA((2 * count,))],
+            [pltpu.SemaphoreType.DMA((count * (HALVES + 1),))],
             vmem=PICK_BYTES,
         )(task_term, left_env, right_env)
-        envs = exchange(envs)
+        envs = exchange(picked[:count])
         if held is None:
             psi = call(encode_kernel, code, [VMEM])(wavefunction[0])
             held = [psi] + [lax.ppermute(psi, "sec", across(hop)) for hop in range(1, chips)]
@@ -231,16 +240,19 @@
             [SMEM] + [VMEM] * (chips + 1),
         )(task_in, *held, paired)
         psis = exchange(psis)
+        lates = [exchange(picked[half * count : (half + 1) * count]) for half in range(1, HALVES)]
         full = count * rows
-        parts = call(
-            functools.partial(task_kernel, me, count),
-            ([part] + [piece] * (count - 1)) * HALVES,
-            [VMEM] * (2 * count),
-            [pltpu.VMEM((full, cols), bf16)] * 3,
-            flops=8 * full * full * cols,
-        )(*envs, *psis)
-        halves = [parts[half * count : (half + 1) * count] for half in range(HALVES)]
-        halves = [exchange(mine) for mine in halves]
+        halves = []
+        for half in range(HALVES):
+            extra = lates[half - 1] if half else []
+            parts = call(
+                functools.partial(task_kernel, me, count, half),
+                [part] + [piece] * (count - 1),
+                [VMEM] * (2 * count + len(extra)),
+                [pltpu.VMEM((full, cols), bf16)] * 2 + [pltpu.VMEM((full, width), bf16)],
+                flops=8 * full * full * width,
+            )(*envs, *psis, *extra)
+            halves.append(exchange(parts))
         for half, mine in enumerate(halves):
             kept, sent = call(
                 functools.partial(combine_kernel, base, sec, me, count),

time: 86.6 us -> 82.8 us (0.956)
  waiting for transfers between devices: 51.4 us -> 21.6 us
  starting transfers between devices: 25.1 us -> 49.2 us
  Pallas kernels: 7.54 us -> 9.43 us
    ppermute x9 -> x15, waiting for transfers between devices: 36 us -> 11.4 us  [exchange(): got[s] = lax.ppermute(blocks[s], 'env', along(s))]
    ppermute x9 -> x15, starting transfers between devices: 16.8 us -> 37.2 us  [exchange(): got[s] = lax.ppermute(blocks[s], 'env', along(s))]
    ppermute x3 -> x6, starting transfers between devices: 3.55 us -> 7.11 us  [body(): lax.ppermute(mine[hop], 'sec', across(hop))]
    ppermute x1 -> x2, waiting for transfers between devices: 2.65 us -> 0.01 us  [body(): other = lax.ppermute(sends[half], 'sec', pair)]
    ppermute x3 -> x6, waiting for transfers between devices: 6.45 us -> 3.96 us  [body(): lax.ppermute(mine[hop], 'sec', across(hop))]
    pallas_call x2 -> x3, Pallas kernels: 3.81 us -> 5.2 us  [the longest x2 3.3 us: body(): call(functools.partial(task_kernel, me, count, half), [part] + [piece] *...]
  transfers between devices with their start and end apart: 17 -> 27, of which waited for: 11 -> 12; matrix products, arithmetic and copies ran while one was open for 0% -> 0% of each run, Pallas kernels for 3% -> 9%
where the time goes in v4:
time: 82.8 us; the launch traced here: 82.7 us
  starting transfers between devices  49.2 us (59%)
  waiting for transfers between devices  21.6 us (26%)
  Pallas kernels  9.43 us (11%)
  local copies, waits for them, and re-layouts  2.27 us (3%)
    ppermute x15, starting transfers between devices, exchange(): got[s] = lax.ppermute(blocks[s], 'env', along(s))  37.2 us
    ppermute x15, waiting for transfers between devices, exchange(): got[s] = lax.ppermute(blocks[s], 'env', along(s))  11.4 us
    ppermute x6, starting transfers between devices, body(): lax.ppermute(mine[hop], 'sec', across(hop))  7.11 us
    ppermute x3, waiting for transfers between devices, body(): lax.ppermute(psi, 'sec', across(hop))  6.27 us
    ppermute x3, starting transfers between devices, body(): lax.ppermute(psi, 'sec', across(hop))  4.63 us
    ppermute x6, waiting for transfers between devices, body(): lax.ppermute(mine[hop], 'sec', across(hop))  3.96 us
    pallas_call x2, Pallas kernels, body(): call(functools.partial(task_kernel, me, count, half), [part] + [piece] *...  3.3 us
    unnamed x10, local copies, waits for them, and re-layouts  2.27 us
  transfers between devices with their start and end apart: 27, of which 12 were waited for; matrix products, arithmetic and copies ran while one was open for 0% of the time, Pallas kernels for 9%

profile of v4, /device:TPU:0, one launch (start us, length us, event | category | flops | bytes accessed | tf_op | source)
XLA Modules:
  0.0 82.7 jit_solution(17073480527564809447)
XLA Ops:
  0.0 0.9 %copy-done = f32[1,128,512]{2,1,0:T(8,128)S(1)} copy-done((f32[1,128,512]{2,1,0:T(8,128)S(1)}, f32[1,128,512]{2,1,0:T(8,128)}, u32[]{:S(2)}) %copy-start) | copy-done | bytes 262168
  1.0 0.1 shard_map.65.rest_0_
  1.1 4.0 %collective-permute-start.5 = (s16[136,512]{1,0:T(8,128)(2,1)S(1)}, s16[136,512]{1,0:T(8,128)(2,1)S(1)}, u32[]{:S(2)}, u32[]{:S(2)}) collective-permute-start(s16[136,512]{1,0:T(8,128)(2,1)S(1)} %shard_map.65.rest_0_), channel_id=1, source_target_pairs={{0,24},{4,28},{8,16},{12,20},{16,8},{20,12},{24,0},{28,4},{1,25},{... | collective-permute-start | bytes 417800 | tf_op jit(solution)/shard_map/ppermute | solution.py:230
  5.1 0.5 collective-permute-start.4
  5.7 3.4 %collective-permute-done.5.rest_3_ = s16[136,512]{1,0:T(8,128)(2,1)S(1)} collective-permute-done((s16[136,512]{1,0:T(8,128)(2,1)S(1)}, s16[136,512]{1,0:T(8,128)(2,1)S(1)}, u32[]{:S(2)}, u32[]{:S(2)}) %collective-permute-start.5) | collective-permute-done | bytes 139296 | tf_op jit(solution)/shard_map/ppermute | solution.py:230
  9.2 2.6 %collective-permute-done.4.rest_2_ = s16[136,512]{1,0:T(8,128)(2,1)S(1)} collective-permute-done((s16[136,512]{1,0:T(8,128)(2,1)S(1)}, s16[136,512]{1,0:T(8,128)(2,1)S(1)}, u32[]{:S(2)}, u32[]{:S(2)}) %collective-permute-start.4) | collective-permute-done | bytes 139296 | tf_op jit(solution)/shard_map/ppermute | solution.py:230
  11.7 0.3 collective-permute-done.3.rest_1_
  12.0 0.7 copy-done.1
  12.7 0.7 shard_map.66
  13.5 0.6 copy-done.4
  14.1 1.9 %shard_map.64 = (bf16[128,768]{1,0:T(8,128)(2,1)S(1)}, bf16[128,768]{1,0:T(8,128)(2,1)S(1)}, bf16[128,768]{1,0:T(8,128)(2,1)S(1)}, bf16[128,768]{1,0:T(8,128)(2,...) custom-call(s32[32]{0:T(128)S(1)} %copy-done.4, ...), custom_call_target="tpu_custom_call" | custom-call | flops 1 | bytes 1 | tf_op jit(solution)/shard_map/pallas_call | solution.py:220
  16.0 1.6 %collective-permute-start = (bf16[128,768]{1,0:T(8,128)(2,1)S(1)}, bf16[128,768]{1,0:T(8,128)(2,1)S(1)}, u32[]{:S(2)}, u32[]{:S(2)}) collective-permute-start(bf16[128,768]{1,0:T(8,128)(2,1)S(1)} %get-tuple-element.38), channel_id=1, source_target_pairs={{0,1},{1,0},{2,3},{3,2},{4,5},{5,4},{6,7},{7,6},{8,9},{9,8},{10,11... | collective-permute-start | bytes 589832 | tf_op jit(solution)/shard_map/ppermute | solution.py:204
  17.7 2.6 %collective-permute-start.1 = (bf16[128,768]{1,0:T(8,128)(2,1)S(1)}, bf16[128,768]{1,0:T(8,128)(2,1)S(1)}, u32[]{:S(2)}, u32[]{:S(2)}) collective-permute-start(bf16[128,768]{1,0:T(8,128)(2,1)S(1)} %get-tuple-element.39), channel_id=1, source_target_pairs={{0,2},{1,3},{2,0},{3,1},{4,6},{5,7},{6,4},{7,5},{8,10},{9,11},{10,... | collective-permute-start | bytes 589832 | tf_op jit(solution)/shard_map/ppermute | solution.py:204
  20.3 0.2 collective-permute-start.2
  20.5 0.7 shard_map.67
  21.2 0.7 collective-permute-start.7
  22.0 3.5 %collective-permute-start.8 = (s16[136,512]{1,0:T(8,128)(2,1)S(1)}, s16[136,512]{1,0:T(8,128)(2,1)S(1)}, u32[]{:S(2)}, u32[]{:S(2)}) collective-permute-start(s16[136,512]{1,0:T(8,128)(2,1)S(1)} %get-tuple-element.43), channel_id=1, source_target_pairs={{0,2},{1,3},{2,0},{3,1},{4,6},{5,7},{6,4},{7,5},{8,10},{9,11},{10,... | collective-permute-start | bytes 417800 | tf_op jit(solution)/shard_map/ppermute | solution.py:204
  25.5 2.2 %collective-permute-done.refs_1_ = bf16[128,768]{1,0:T(8,128)(2,1)S(1)} collective-permute-done((bf16[128,768]{1,0:T(8,128)(2,1)S(1)}, bf16[128,768]{1,0:T(8,128)(2,1)S(1)}, u32[]{:S(2)}, u32[]{:S(2)}) %collective-permute-start) | collective-permute-done | bytes 196640 | tf_op jit(solution)/shard_map/ppermute | solution.py:204
  27.7 2.8 %collective-permute-start.9 = (s16[136,512]{1,0:T(8,128)(2,1)S(1)}, s16[136,512]{1,0:T(8,128)(2,1)S(1)}, u32[]{:S(2)}, u32[]{:S(2)}) collective-permute-start(s16[136,512]{1,0:T(8,128)(2,1)S(1)} %get-tuple-element.44), channel_id=1, source_target_pairs={{0,3},{1,2},{2,1},{3,0},{4,7},{5,6},{6,5},{7,4},{8,11},{9,10},{10,... | collective-permute-start | bytes 417800 | tf_op jit(solution)/shard_map/ppermute | solution.py:204
  30.5 4.4 %collective-permute-done.1.refs_2_ = bf16[128,768]{1,0:T(8,128)(2,1)S(1)} collective-permute-done((bf16[128,768]{1,0:T(8,128)(2,1)S(1)}, bf16[128,768]{1,0:T(8,128)(2,1)S(1)}, u32[]{:S(2)}, u32[]{:S(2)}) %collective-permute-start.1) | collective-permute-done | bytes 196640 | tf_op jit(solution)/shard_map/ppermute | solution.py:204
  34.9 11.8 %collective-permute-start.18 = (bf16[128,256]{1,0:T(8,128)(2,1)S(1)}, bf16[128,256]{1,0:T(8,128)(2,1)S(1)}, u32[]{:S(2)}, u32[]{:S(2)}) collective-permute-start(bf16[128,256]{1,0:T(8,128)(2,1)S(1)} %get-tuple-element.57), channel_id=1, source_target_pairs={{0,2},{1,3},{2,0},{3,1},{4,6},{5,7},{6,4},{7,5},{8,10},{9,11},{10,... | collective-permute-start | bytes 196616 | tf_op jit(solution)/shard_map/ppermute | solution.py:204
  46.6 1.3 %collective-permute-start.19 = (bf16[128,256]{1,0:T(8,128)(2,1)S(1)}, bf16[128,256]{1,0:T(8,128)(2,1)S(1)}, u32[]{:S(2)}, u32[]{:S(2)}) collective-permute-start(bf16[128,256]{1,0:T(8,128)(2,1)S(1)} %get-tuple-element.58), channel_id=1, source_target_pairs={{0,3},{1,2},{2,1},{3,0},{4,7},{5,6},{6,5},{7,4},{8,11},{9,10},{10,... | collective-permute-start | bytes 196616 | tf_op jit(solution)/shard_map/ppermute | solution.py:204
  48.0 0.8 collective-permute-done.8.refs_6_
  48.7 1.6 %shard_map.68 = (f32[128,256]{1,0:T(8,128)S(1)}, s16[136,256]{1,0:T(8,128)(2,1)S(1)}, s16[136,256]{1,0:T(8,128)(2,1)S(1)}, s16[136,256]{1,0:T(8,128)(2,1)S(1)}) custom-call(bf16[128,768]{1,0:T(8,128)(2,1)S(1)} %get-tuple-element.37.refs_0_, bf16[128,768]{1,0:T(8,128)(2,1)S(1)} %collective-permute-done.refs_1_, ...), custom_call_target="tpu_custom_call" | custom-call | flops 536870912 | bytes 1 | tf_op jit(solution)/shard_map/pallas_call | solution.py:248
  50.4 5.7 %collective-permute-start.10 = (s16[136,256]{1,0:T(8,128)(2,1)S(1)}, s16[136,256]{1,0:T(8,128)(2,1)S(1)}, u32[]{:S(2)}, u32[]{:S(2)}) collective-permute-start(s16[136,256]{1,0:T(8,128)(2,1)S(1)} %get-tuple-element.46), channel_id=1, source_target_pairs={{0,1},{1,0},{2,3},{3,2},{4,5},{5,4},{6,7},{7,6},{8,9},{9,8},{10,11... | collective-permute-start | bytes 208904 | tf_op jit(solution)/shard_map/ppermute | solution.py:204
  56.1 1.1 %collective-permute-start.11 = (s16[136,256]{1,0:T(8,128)(2,1)S(1)}, s16[136,256]{1,0:T(8,128)(2,1)S(1)}, u32[]{:S(2)}, u32[]{:S(2)}) collective-permute-start(s16[136,256]{1,0:T(8,128)(2,1)S(1)} %get-tuple-element.47), channel_id=1, source_target_pairs={{0,2},{1,3},{2,0},{3,1},{4,6},{5,7},{6,4},{7,5},{8,10},{9,11},{10,... | collective-permute-start | bytes 208904 | tf_op jit(solution)/shard_map/ppermute | solution.py:204
  57.2 1.4 %collective-permute-start.12 = (s16[136,256]{1,0:T(8,128)(2,1)S(1)}, s16[136,256]{1,0:T(8,128)(2,1)S(1)}, u32[]{:S(2)}, u32[]{:S(2)}) collective-permute-start(s16[136,256]{1,0:T(8,128)(2,1)S(1)} %get-tuple-element.48), channel_id=1, source_target_pairs={{0,3},{1,2},{2,1},{3,0},{4,7},{5,6},{6,5},{7,4},{8,11},{9,10},{10,... | collective-permute-start | bytes 208904 | tf_op jit(solution)/shard_map/ppermute | solution.py:204
  58.6 1.6 %shard_map.71 = (f32[128,256]{1,0:T(8,128)S(1)}, s16[136,256]{1,0:T(8,128)(2,1)S(1)}, s16[136,256]{1,0:T(8,128)(2,1)S(1)}, s16[136,256]{1,0:T(8,128)(2,1)S(1)}) custom-call(bf16[128,768]{1,0:T(8,128)(2,1)S(1)} %get-tuple-element.37.refs_0_, bf16[128,768]{1,0:T(8,128)(2,1)S(1)} %collective-permute-done.refs_1_, ...), custom_call_target="tpu_custom_call" | custom-call | flops 536870912 | bytes 1 | tf_op jit(solution)/shard_map/pallas_call | solution.py:248
  60.2 1.1 %collective-permute-start.20 = (s16[136,256]{1,0:T(8,128)(2,1)S(1)}, s16[136,256]{1,0:T(8,128)(2,1)S(1)}, u32[]{:S(2)}, u32[]{:S(2)}) collective-permute-start(s16[136,256]{1,0:T(8,128)(2,1)S(1)} %get-tuple-element.60), channel_id=1, source_target_pairs={{0,1},{1,0},{2,3},{3,2},{4,5},{5,4},{6,7},{7,6},{8,9},{9,8},{10,11... | collective-permute-start | bytes 208904 | tf_op jit(solution)/shard_map/ppermute | solution.py:204
  61.3 2.0 %collective-permute-start.21 = (s16[136,256]{1,0:T(8,128)(2,1)S(1)}, s16[136,256]{1,0:T(8,128)(2,1)S(1)}, u32[]{:S(2)}, u32[]{:S(2)}) collective-permute-start(s16[136,256]{1,0:T(8,128)(2,1)S(1)} %get-tuple-element.61), channel_id=1, source_target_pairs={{0,2},{1,3},{2,0},{3,1},{4,6},{5,7},{6,4},{7,5},{8,10},{9,11},{10,... | collective-permute-start | bytes 208904 | tf_op jit(solution)/shard_map/ppermute | solution.py:204
  63.3 1.4 %collective-permute-start.22 = (s16[136,256]{1,0:T(8,128)(2,1)S(1)}, s16[136,256]{1,0:T(8,128)(2,1)S(1)}, u32[]{:S(2)}, u32[]{:S(2)}) collective-permute-start(s16[136,256]{1,0:T(8,128)(2,1)S(1)} %get-tuple-element.62), channel_id=1, source_target_pairs={{0,3},{1,2},{2,1},{3,0},{4,7},{5,6},{6,5},{7,4},{8,11},{9,10},{10,... | collective-permute-start | bytes 208904 | tf_op jit(solution)/shard_map/ppermute | solution.py:204
  64.7 0.7 shard_map.69
  65.5 2.8 %collective-permute-done.21.rest_2_ = s16[136,256]{1,0:T(8,128)(2,1)S(1)} collective-permute-done((s16[136,256]{1,0:T(8,128)(2,1)S(1)}, s16[136,256]{1,0:T(8,128)(2,1)S(1)}, u32[]{:S(2)}, u32[]{:S(2)}) %collective-permute-start.21) | collective-permute-done | bytes 69664 | tf_op jit(solution)/shard_map/ppermute | solution.py:204
  68.4 1.2 %collective-permute-done.22.rest_3_ = s16[136,256]{1,0:T(8,128)(2,1)S(1)} collective-permute-done((s16[136,256]{1,0:T(8,128)(2,1)S(1)}, s16[136,256]{1,0:T(8,128)(2,1)S(1)}, u32[]{:S(2)}, u32[]{:S(2)}) %collective-permute-start.22) | collective-permute-done | bytes 69664 | tf_op jit(solution)/shard_map/ppermute | solution.py:204
  69.5 0.7 shard_map.72
  70.3 0.2 shard_map.70
  70.5 1.6 %collective-permute-start.14 = (s16[136,256]{1,0:T(8,128)(2,1)S(1)}, s16[136,256]{1,0:T(8,128)(2,1)S(1)}, u32[]{:S(2)}, u32[]{:S(2)}) collective-permute-start(s16[136,256]{1,0:T(8,128)(2,1)S(1)} %get-tuple-element.52), channel_id=1, source_target_pairs={{0,8},{4,12},{8,0},{12,4},{16,24},{20,28},{24,16},{28,20},{1,9},{5... | collective-permute-start | bytes 208904 | tf_op jit(solution)/shard_map/ppermute | solution.py:272
  72.1 0.7 collective-permute-start.15
  72.8 1.3 %collective-permute-start.16 = (s16[136,256]{1,0:T(8,128)(2,1)S(1)}, s16[136,256]{1,0:T(8,128)(2,1)S(1)}, u32[]{:S(2)}, u32[]{:S(2)}) collective-permute-start(s16[136,256]{1,0:T(8,128)(2,1)S(1)} %get-tuple-element.54), channel_id=1, source_target_pairs={{0,24},{4,28},{8,16},{12,20},{16,8},{20,12},{24,0},{28,4},{1,25},{... | collective-permute-start | bytes 208904 | tf_op jit(solution)/shard_map/ppermute | solution.py:272
  74.1 0.2 shard_map.73
  74.3 1.6 %collective-permute-start.24 = (s16[136,256]{1,0:T(8,128)(2,1)S(1)}, s16[136,256]{1,0:T(8,128)(2,1)S(1)}, u32[]{:S(2)}, u32[]{:S(2)}) collective-permute-start(s16[136,256]{1,0:T(8,128)(2,1)S(1)} %get-tuple-element.66), channel_id=1, source_target_pairs={{0,8},{4,12},{8,0},{12,4},{16,24},{20,28},{24,16},{28,20},{1,9},{5... | collective-permute-start | bytes 208904 | tf_op jit(solution)/shard_map/ppermute | solution.py:272
  75.9 0.7 collective-permute-start.25
  76.6 1.3 %collective-permute-start.26 = (s16[136,256]{1,0:T(8,128)(2,1)S(1)}, s16[136,256]{1,0:T(8,128)(2,1)S(1)}, u32[]{:S(2)}, u32[]{:S(2)}) collective-permute-start(s16[136,256]{1,0:T(8,128)(2,1)S(1)} %get-tuple-element.68), channel_id=1, source_target_pairs={{0,24},{4,28},{8,16},{12,20},{16,8},{20,12},{24,0},{28,4},{1,25},{... | collective-permute-start | bytes 208904 | tf_op jit(solution)/shard_map/ppermute | solution.py:272
  77.9 0.7 collective-permute-done.16.refs_3_
  78.6 0.6 collective-permute-done.24.refs_5_
  79.2 1.6 %collective-permute-done.25.refs_6_ = s16[136,256]{1,0:T(8,128)(2,1)S(1)} collective-permute-done((s16[136,256]{1,0:T(8,128)(2,1)S(1)}, s16[136,256]{1,0:T(8,128)(2,1)S(1)}, u32[]{:S(2)}, u32[]{:S(2)}) %collective-permute-start.25) | collective-permute-done | bytes 69664 | tf_op jit(solution)/shard_map/ppermute | solution.py:272
  80.8 1.0 %collective-permute-done.26.refs_7_ = s16[136,256]{1,0:T(8,128)(2,1)S(1)} collective-permute-done((s16[136,256]{1,0:T(8,128)(2,1)S(1)}, s16[136,256]{1,0:T(8,128)(2,1)S(1)}, u32[]{:S(2)}, u32[]{:S(2)}) %collective-permute-start.26) | collective-permute-done | bytes 69664 | tf_op jit(solution)/shard_map/ppermute | solution.py:272
  81.8 0.8 %shard_map.74 = f32[128,512]{1,0:T(8,128)} custom-call(f32[128,256]{1,0:T(8,128)S(1)} %get-tuple-element.51.refs_0_, s16[136,256]{1,0:T(8,128)(2,1)S(1)} %collective-permute-done.14.refs_1_, s16[136,256]{1,0:T(8,128)(2,1)S(1)} %collective-permute-done.15.refs_2_, s16[136,256]{1,0:T(8,128)(2,1)S(1)} %collective-permute-done.16.refs_3_, ...), custom_call_target="tpu_custom_call" | custom-call | flops 1 | bytes 1 | tf_op jit(solution)/shard_map/pallas_call | solution.py:273
  (27 shorter events, 0.4 us)
Async XLA Ops:
  0.0 0.9 %copy-start = (f32[1,128,512]{2,1,0:T(8,128)S(1)}, f32[1,128,512]{2,1,0:T(8,128)}, u32[]{:S(2)}) copy-start(f32[1,128,512]{2,1,0:T(8,128)} %param.6) | copy-start | bytes 786436
  1.1 8.1 %collective-permute-start.5 = (s16[136,512]{1,0:T(8,128)(2,1)S(1)}, s16[136,512]{1,0:T(8,128)(2,1)S(1)}, u32[]{:S(2)}, u32[]{:S(2)}) collective-permute-start(s16[136,512]{1,0:T(8,128)(2,1)S(1)} %shard_map.65.rest_0_), channel_id=1, source_target_pairs={{0,24},{4,28},{8,16},{12,20},{16,8},{20,12},{24,0},{28,4},{1,25},{... | collective-permute-start | bytes 417800 | tf_op jit(solution)/shard_map/ppermute | solution.py:230
  5.1 6.7 %collective-permute-start.4 = (s16[136,512]{1,0:T(8,128)(2,1)S(1)}, s16[136,512]{1,0:T(8,128)(2,1)S(1)}, u32[]{:S(2)}, u32[]{:S(2)}) collective-permute-start(s16[136,512]{1,0:T(8,128)(2,1)S(1)} %shard_map.65.rest_0_), channel_id=1, source_target_pairs={{0,16},{4,20},{8,24},{12,28},{16,0},{20,4},{24,8},{28,12},{1,17},{... | collective-permute-start | bytes 417800 | tf_op jit(solution)/shard_map/ppermute | solution.py:230
  5.6 6.4 %collective-permute-start.3 = (s16[136,512]{1,0:T(8,128)(2,1)S(1)}, s16[136,512]{1,0:T(8,128)(2,1)S(1)}, u32[]{:S(2)}, u32[]{:S(2)}) collective-permute-start(s16[136,512]{1,0:T(8,128)(2,1)S(1)} %shard_map.65.rest_0_), channel_id=1, source_target_pairs={{0,8},{4,12},{8,0},{12,4},{16,24},{20,28},{24,16},{28,20},{1,9},{5... | collective-permute-start | bytes 417800 | tf_op jit(solution)/shard_map/ppermute | solution.py:230
  12.0 0.7 copy-start.1
  13.4 7.1 %copy-start.2 = (s32[32]{0:T(128)S(1)}, s32[32]{0:T(128)}, u32[]{:S(2)}) copy-start(s32[32]{0:T(128)} %in_ref.3) | copy-start | bytes 388
  13.4 7.1 %collective-permute-start.6 = (s16[4,136,512]{2,1,0:T(8,128)(2,1)S(1)}, s16[4,136,512]{2,1,0:T(8,128)(2,1)S(1)}, u32[]{:S(2)}, u32[]{:S(2)}) collective-permute-start(s16[4,136,512]{2,1,0:T(8,128)(2,1)S(1)} %shard_map.66), channel_id=1, source_target_pairs={{0,4},{4,0},{8,12},{12,8},{16,20},{20,16},{24,28},{28,24},{1,5},{5... | collective-permute-start | bytes 1671176 | tf_op jit(solution)/shard_map/ppermute | solution.py:236
  13.5 0.7 copy-start.4
  16.0 48.7 %copy-start.3 = (s32[32,1]{0,1:T(1,128)S(1)}, s32[32,1]{0,1:T(1,128)}, u32[]{:S(2)}) copy-start(s32[32,1]{0,1:T(1,128)} %param.10) | copy-start | bytes 388
  16.0 11.6 %collective-permute-start = (bf16[128,768]{1,0:T(8,128)(2,1)S(1)}, bf16[128,768]{1,0:T(8,128)(2,1)S(1)}, u32[]{:S(2)}, u32[]{:S(2)}) collective-permute-start(bf16[128,768]{1,0:T(8,128)(2,1)S(1)} %get-tuple-element.38), channel_id=1, source_target_pairs={{0,1},{1,0},{2,3},{3,2},{4,5},{5,4},{6,7},{7,6},{8,9},{9,8},{10,11... | collective-permute-start | bytes 589832 | tf_op jit(solution)/shard_map/ppermute | solution.py:204
  17.7 17.2 %collective-permute-start.1 = (bf16[128,768]{1,0:T(8,128)(2,1)S(1)}, bf16[128,768]{1,0:T(8,128)(2,1)S(1)}, u32[]{:S(2)}, u32[]{:S(2)}) collective-permute-start(bf16[128,768]{1,0:T(8,128)(2,1)S(1)} %get-tuple-element.39), channel_id=1, source_target_pairs={{0,2},{1,3},{2,0},{3,1},{4,6},{5,7},{6,4},{7,5},{8,10},{9,11},{10,... | collective-permute-start | bytes 589832 | tf_op jit(solution)/shard_map/ppermute | solution.py:204
  20.3 14.6 %collective-permute-start.2 = (bf16[128,768]{1,0:T(8,128)(2,1)S(1)}, bf16[128,768]{1,0:T(8,128)(2,1)S(1)}, u32[]{:S(2)}, u32[]{:S(2)}) collective-permute-start(bf16[128,768]{1,0:T(8,128)(2,1)S(1)} %get-tuple-element.40), channel_id=1, source_target_pairs={{0,3},{1,2},{2,1},{3,0},{4,7},{5,6},{6,5},{7,4},{8,11},{9,10},{10,... | collective-permute-start | bytes 589832 | tf_op jit(solution)/shard_map/ppermute | solution.py:204
  21.2 25.4 %collective-permute-start.7 = (s16[136,512]{1,0:T(8,128)(2,1)S(1)}, s16[136,512]{1,0:T(8,128)(2,1)S(1)}, u32[]{:S(2)}, u32[]{:S(2)}) collective-permute-start(s16[136,512]{1,0:T(8,128)(2,1)S(1)} %get-tuple-element.42), channel_id=1, source_target_pairs={{0,1},{1,0},{2,3},{3,2},{4,5},{5,4},{6,7},{7,6},{8,9},{9,8},{10,11... | collective-permute-start | bytes 417800 | tf_op jit(solution)/shard_map/ppermute | solution.py:204
  22.0 26.8 %collective-permute-start.8 = (s16[136,512]{1,0:T(8,128)(2,1)S(1)}, s16[136,512]{1,0:T(8,128)(2,1)S(1)}, u32[]{:S(2)}, u32[]{:S(2)}) collective-permute-start(s16[136,512]{1,0:T(8,128)(2,1)S(1)} %get-tuple-element.43), channel_id=1, source_target_pairs={{0,2},{1,3},{2,0},{3,1},{4,6},{5,7},{6,4},{7,5},{8,10},{9,11},{10,... | collective-permute-start | bytes 417800 | tf_op jit(solution)/shard_map/ppermute | solution.py:204
  27.7 21.1 %collective-permute-start.9 = (s16[136,512]{1,0:T(8,128)(2,1)S(1)}, s16[136,512]{1,0:T(8,128)(2,1)S(1)}, u32[]{:S(2)}, u32[]{:S(2)}) collective-permute-start(s16[136,512]{1,0:T(8,128)(2,1)S(1)} %get-tuple-element.44), channel_id=1, source_target_pairs={{0,3},{1,2},{2,1},{3,0},{4,7},{5,6},{6,5},{7,4},{8,11},{9,10},{10,... | collective-permute-start | bytes 417800 | tf_op jit(solution)/shard_map/ppermute | solution.py:204
  34.9 22.3 %collective-permute-start.17 = (bf16[128,256]{1,0:T(8,128)(2,1)S(1)}, bf16[128,256]{1,0:T(8,128)(2,1)S(1)}, u32[]{:S(2)}, u32[]{:S(2)}) collective-permute-start(bf16[128,256]{1,0:T(8,128)(2,1)S(1)} %get-tuple-element.56), channel_id=1, source_target_pairs={{0,1},{1,0},{2,3},{3,2},{4,5},{5,4},{6,7},{7,6},{8,9},{9,8},{10,11... | collective-permute-start | bytes 196616 | tf_op jit(solution)/shard_map/ppermute | solution.py:204
  34.9 23.7 %collective-permute-start.18 = (bf16[128,256]{1,0:T(8,128)(2,1)S(1)}, bf16[128,256]{1,0:T(8,128)(2,1)S(1)}, u32[]{:S(2)}, u32[]{:S(2)}) collective-permute-start(bf16[128,256]{1,0:T(8,128)(2,1)S(1)} %get-tuple-element.57), channel_id=1, source_target_pairs={{0,2},{1,3},{2,0},{3,1},{4,6},{5,7},{6,4},{7,5},{8,10},{9,11},{10,... | collective-permute-start | bytes 196616 | tf_op jit(solution)/shard_map/ppermute | solution.py:204
  46.6 12.0 %collective-permute-start.19 = (bf16[128,256]{1,0:T(8,128)(2,1)S(1)}, bf16[128,256]{1,0:T(8,128)(2,1)S(1)}, u32[]{:S(2)}, u32[]{:S(2)}) collective-permute-start(bf16[128,256]{1,0:T(8,128)(2,1)S(1)} %get-tuple-element.58), channel_id=1, source_target_pairs={{0,3},{1,2},{2,1},{3,0},{4,7},{5,6},{6,5},{7,4},{8,11},{9,10},{10,... | collective-permute-start | bytes 196616 | tf_op jit(solution)/shard_map/ppermute | solution.py:204
  50.4 12.9 %collective-permute-start.10 = (s16[136,256]{1,0:T(8,128)(2,1)S(1)}, s16[136,256]{1,0:T(8,128)(2,1)S(1)}, u32[]{:S(2)}, u32[]{:S(2)}) collective-permute-start(s16[136,256]{1,0:T(8,128)(2,1)S(1)} %get-tuple-element.46), channel_id=1, source_target_pairs={{0,1},{1,0},{2,3},{3,2},{4,5},{5,4},{6,7},{7,6},{8,9},{9,8},{10,11... | collective-permute-start | bytes 208904 | tf_op jit(solution)/shard_map/ppermute | solution.py:204
  56.1 8.6 %collective-permute-start.11 = (s16[136,256]{1,0:T(8,128)(2,1)S(1)}, s16[136,256]{1,0:T(8,128)(2,1)S(1)}, u32[]{:S(2)}, u32[]{:S(2)}) collective-permute-start(s16[136,256]{1,0:T(8,128)(2,1)S(1)} %get-tuple-element.47), channel_id=1, source_target_pairs={{0,2},{1,3},{2,0},{3,1},{4,6},{5,7},{6,4},{7,5},{8,10},{9,11},{10,... | collective-permute-start | bytes 208904 | tf_op jit(solution)/shard_map/ppermute | solution.py:204
  57.2 7.5 %collective-permute-start.12 = (s16[136,256]{1,0:T(8,128)(2,1)S(1)}, s16[136,256]{1,0:T(8,128)(2,1)S(1)}, u32[]{:S(2)}, u32[]{:S(2)}) collective-permute-start(s16[136,256]{1,0:T(8,128)(2,1)S(1)} %get-tuple-element.48), channel_id=1, source_target_pairs={{0,3},{1,2},{2,1},{3,0},{4,7},{5,6},{6,5},{7,4},{8,11},{9,10},{10,... | collective-permute-start | bytes 208904 | tf_op jit(solution)/shard_map/ppermute | solution.py:204
  60.2 5.3 %collective-permute-start.20 = (s16[136,256]{1,0:T(8,128)(2,1)S(1)}, s16[136,256]{1,0:T(8,128)(2,1)S(1)}, u32[]{:S(2)}, u32[]{:S(2)}) collective-permute-start(s16[136,256]{1,0:T(8,128)(2,1)S(1)} %get-tuple-element.60), channel_id=1, source_target_pairs={{0,1},{1,0},{2,3},{3,2},{4,5},{5,4},{6,7},{7,6},{8,9},{9,8},{10,11... | collective-permute-start | bytes 208904 | tf_op jit(solution)/shard_map/ppermute | solution.py:204
  61.3 7.0 %collective-permute-start.21 = (s16[136,256]{1,0:T(8,128)(2,1)S(1)}, s16[136,256]{1,0:T(8,128)(2,1)S(1)}, u32[]{:S(2)}, u32[]{:S(2)}) collective-permute-start(s16[136,256]{1,0:T(8,128)(2,1)S(1)} %get-tuple-element.61), channel_id=1, source_target_pairs={{0,2},{1,3},{2,0},{3,1},{4,6},{5,7},{6,4},{7,5},{8,10},{9,11},{10,... | collective-permute-start | bytes 208904 | tf_op jit(solution)/shard_map/ppermute | solution.py:204
  63.3 6.2 %collective-permute-start.22 = (s16[136,256]{1,0:T(8,128)(2,1)S(1)}, s16[136,256]{1,0:T(8,128)(2,1)S(1)}, u32[]{:S(2)}, u32[]{:S(2)}) collective-permute-start(s16[136,256]{1,0:T(8,128)(2,1)S(1)} %get-tuple-element.62), channel_id=1, source_target_pairs={{0,3},{1,2},{2,1},{3,0},{4,7},{5,6},{6,5},{7,4},{8,11},{9,10},{10,... | collective-permute-start | bytes 208904 | tf_op jit(solution)/shard_map/ppermute | solution.py:204
  65.4 4.9 %collective-permute-start.13 = (f32[4,128,256]{2,1,0:T(8,128)S(1)}, f32[4,128,256]{2,1,0:T(8,128)S(1)}, u32[]{:S(2)}, u32[]{:S(2)}) collective-permute-start(f32[4,128,256]{2,1,0:T(8,128)S(1)} %get-tuple-element.50), channel_id=1, source_target_pairs={{0,4},{4,0},{8,12},{12,8},{16,20},{20,16},{24,28},{28,24},{1,5},{5... | collective-permute-start | bytes 1572872 | tf_op jit(solution)/shard_map/ppermute | solution.py:267
  70.3 3.8 %collective-permute-start.23 = (f32[4,128,256]{2,1,0:T(8,128)S(1)}, f32[4,128,256]{2,1,0:T(8,128)S(1)}, u32[]{:S(2)}, u32[]{:S(2)}) collective-permute-start(f32[4,128,256]{2,1,0:T(8,128)S(1)} %get-tuple-element.64), channel_id=1, source_target_pairs={{0,4},{4,0},{8,12},{12,8},{16,20},{20,16},{24,28},{28,24},{1,5},{5... | collective-permute-start | bytes 1572872 | tf_op jit(solution)/shard_map/ppermute | solution.py:267
  70.5 6.1 %collective-permute-start.14 = (s16[136,256]{1,0:T(8,128)(2,1)S(1)}, s16[136,256]{1,0:T(8,128)(2,1)S(1)}, u32[]{:S(2)}, u32[]{:S(2)}) collective-permute-start(s16[136,256]{1,0:T(8,128)(2,1)S(1)} %get-tuple-element.52), channel_id=1, source_target_pairs={{0,8},{4,12},{8,0},{12,4},{16,24},{20,28},{24,16},{28,20},{1,9},{5... | collective-permute-start | bytes 208904 | tf_op jit(solution)/shard_map/ppermute | solution.py:272
  72.1 5.7 %collective-permute-start.15 = (s16[136,256]{1,0:T(8,128)(2,1)S(1)}, s16[136,256]{1,0:T(8,128)(2,1)S(1)}, u32[]{:S(2)}, u32[]{:S(2)}) collective-permute-start(s16[136,256]{1,0:T(8,128)(2,1)S(1)} %get-tuple-element.53), channel_id=1, source_target_pairs={{0,16},{4,20},{8,24},{12,28},{16,0},{20,4},{24,8},{28,12},{1,17},{... | collective-permute-start | bytes 208904 | tf_op jit(solution)/shard_map/ppermute | solution.py:272
  72.8 5.8 %collective-permute-start.16 = (s16[136,256]{1,0:T(8,128)(2,1)S(1)}, s16[136,256]{1,0:T(8,128)(2,1)S(1)}, u32[]{:S(2)}, u32[]{:S(2)}) collective-permute-start(s16[136,256]{1,0:T(8,128)(2,1)S(1)} %get-tuple-element.54), channel_id=1, source_target_pairs={{0,24},{4,28},{8,16},{12,20},{16,8},{20,12},{24,0},{28,4},{1,25},{... | collective-permute-start | bytes 208904 | tf_op jit(solution)/shard_map/ppermute | solution.py:272
  74.3 4.9 %collective-permute-start.24 = (s16[136,256]{1,0:T(8,128)(2,1)S(1)}, s16[136,256]{1,0:T(8,128)(2,1)S(1)}, u32[]{:S(2)}, u32[]{:S(2)}) collective-permute-start(s16[136,256]{1,0:T(8,128)(2,1)S(1)} %get-tuple-element.66), channel_id=1, source_target_pairs={{0,8},{4,12},{8,0},{12,4},{16,24},{20,28},{24,16},{28,20},{1,9},{5... | collective-permute-start | bytes 208904 | tf_op jit(solution)/shard_map/ppermute | solution.py:272
  75.9 4.9 %collective-permute-start.25 = (s16[136,256]{1,0:T(8,128)(2,1)S(1)}, s16[136,256]{1,0:T(8,128)(2,1)S(1)}, u32[]{:S(2)}, u32[]{:S(2)}) collective-permute-start(s16[136,256]{1,0:T(8,128)(2,1)S(1)} %get-tuple-element.67), channel_id=1, source_target_pairs={{0,16},{4,20},{8,24},{12,28},{16,0},{20,4},{24,8},{28,12},{1,17},{... | collective-permute-start | bytes 208904 | tf_op jit(solution)/shard_map/ppermute | solution.py:272
  76.6 5.2 %collective-permute-start.26 = (s16[136,256]{1,0:T(8,128)(2,1)S(1)}, s16[136,256]{1,0:T(8,128)(2,1)S(1)}, u32[]{:S(2)}, u32[]{:S(2)}) collective-permute-start(s16[136,256]{1,0:T(8,128)(2,1)S(1)} %get-tuple-element.68), channel_id=1, source_target_pairs={{0,24},{4,28},{8,16},{12,20},{16,8},{20,12},{24,0},{28,4},{1,25},{... | collective-permute-start | bytes 208904 | tf_op jit(solution)/shard_map/ppermute | solution.py:272

commit v5 on v4

--- a/solution.py
+++ b/solution.py
@@ -26,6 +26,11 @@
         cost_estimate=pl.CostEstimate(flops=flops, bytes_accessed=1, transcendentals=0),
         compiler_params=pltpu.CompilerParams(vmem_limit_bytes=vmem),
     )
+
+
+def entry(table, index):
+    places = lax.broadcasted_iota(jnp.int32, table.shape, 1)
+    return jnp.sum(jnp.where(places == index, table[...], 0).astype(jnp.float32)).astype(jnp.int32)
 
 
 def encode(value, out, centred):
@@ -61,7 +66,7 @@
     copies = []
     start, mine = base(), me()
     for step in range(count):
-        term = term_ref[start + (mine ^ step)]
+        term = entry(term_ref, start + (mine ^ step))
         copies.append((left_ref.at[term], outs[step].at[:, pl.ds(0, cols)]))
         for half in range(HALVES):
             out = outs[half * count + step]
@@ -148,7 +153,7 @@
     keep[...] = jnp.zeros(keep.shape, jnp.float32)
     send[...] = jnp.zeros(send.shape, jnp.float32)
     for step in range(count):
-        target = target_ref[start + mine ^ step]
+        target = entry(target_ref, start + (mine ^ step))
         hop = (target // 2) ^ chip
         part = parts[0][...] if step == 0 else decode(parts[step])
         mine_too = lax.rem(target, 2) == core
@@ -186,7 +191,7 @@
     chips = groups // 2
     _, rows, cols = wavefunction.shape
     per_device = task_in.shape[0] // (groups * count)
-    targets = task_out[:, 0]
+    targets = task_out[:, 0][None]
     f32, bf16 = jnp.float32, jnp.bfloat16
     block = jax.ShapeDtypeStruct((rows, cols), f32)
     sec = lambda: lax.axis_index("sec")
@@ -220,10 +225,10 @@
         picked = call(
             functools.partial(pick_kernel, base, me, count),
             [early] * count + [late] * (count * (HALVES - 1)),
-            [SMEM, HBM, HBM],
+            [VMEM, HBM, HBM],
             [pltpu.SemaphoreType.DMA((count * (HALVES + 1),))],
             vmem=PICK_BYTES,
-        )(task_term, left_env, right_env)
+        )(task_term[None], left_env, right_env)
         envs = exchange(picked[:count])
         if held is None:
             psi = call(encode_kernel, code, [VMEM])(wavefunction[0])
@@ -257,7 +262,7 @@
             kept, sent = call(
                 functools.partial(combine_kernel, base, sec, me, count),
                 [stack, stack],
-                [SMEM] + [VMEM] * count,
+                [VMEM] * (count + 1),
             )(targets, *mine)
             if turn:
                 kept, sent = keeps[half] + kept, sends[half] + sent

time: 82.8 us -> 82.3 us (level)
  no operation moved by 1% of the time
where the time goes in v5:
time: 82.3 us; the launch traced here: 82.1 us
  starting transfers between devices  49.2 us (60%)
  waiting for transfers between devices  21.8 us (26%)
  Pallas kernels  8.71 us (11%)
  local copies, waits for them, and re-layouts  2.27 us (3%)
    ppermute x15, starting transfers between devices, exchange(): got[s] = lax.ppermute(blocks[s], 'env', along(s))  37.2 us
    ppermute x15, waiting for transfers between devices, exchange(): got[s] = lax.ppermute(blocks[s], 'env', along(s))  11.5 us
    ppermute x6, starting transfers between devices, body(): lax.ppermute(mine[hop], 'sec', across(hop))  7.11 us
    ppermute x3, waiting for transfers between devices, body(): lax.ppermute(psi, 'sec', across(hop))  6.27 us
    ppermute x3, starting transfers between devices, body(): lax.ppermute(psi, 'sec', across(hop))  4.63 us
    ppermute x6, waiting for transfers between devices, body(): lax.ppermute(mine[hop], 'sec', across(hop))  3.96 us
    pallas_call x2, Pallas kernels, body(): call(functools.partial(task_kernel, me, count, half), [part] + [piece] *...  3.3 us
    unnamed x10, local copies, waits for them, and re-layouts  2.27 us
  transfers between devices with their start and end apart: 27, of which 12 were waited for; matrix products, arithmetic and copies ran while one was open for 0% of the time, Pallas kernels for 9%

profile of v5, /device:TPU:0, one launch (start us, length us, event | category | flops | bytes accessed | tf_op | source)
XLA Modules:
  0.0 82.1 jit_solution(10614194844622329109)
XLA Ops:
  0.0 0.9 %copy-done = f32[1,128,512]{2,1,0:T(8,128)S(1)} copy-done((f32[1,128,512]{2,1,0:T(8,128)S(1)}, f32[1,128,512]{2,1,0:T(8,128)}, u32[]{:S(2)}) %copy-start) | copy-done | bytes 262168
  1.0 0.1 shard_map.65.rest_0_
  1.1 4.0 %collective-permute-start.5 = (s16[136,512]{1,0:T(8,128)(2,1)S(1)}, s16[136,512]{1,0:T(8,128)(2,1)S(1)}, u32[]{:S(2)}, u32[]{:S(2)}) collective-permute-start(s16[136,512]{1,0:T(8,128)(2,1)S(1)} %shard_map.65.rest_0_), channel_id=1, source_target_pairs={{0,24},{4,28},{8,16},{12,20},{16,8},{20,12},{24,0},{28,4},{1,25},{... | collective-permute-start | bytes 417800 | tf_op jit(solution)/shard_map/ppermute | solution.py:235
  5.1 0.5 collective-permute-start.4
  5.7 3.4 %collective-permute-done.5.rest_3_ = s16[136,512]{1,0:T(8,128)(2,1)S(1)} collective-permute-done((s16[136,512]{1,0:T(8,128)(2,1)S(1)}, s16[136,512]{1,0:T(8,128)(2,1)S(1)}, u32[]{:S(2)}, u32[]{:S(2)}) %collective-permute-start.5) | collective-permute-done | bytes 139296 | tf_op jit(solution)/shard_map/ppermute | solution.py:235
  9.2 2.6 %collective-permute-done.4.rest_2_ = s16[136,512]{1,0:T(8,128)(2,1)S(1)} collective-permute-done((s16[136,512]{1,0:T(8,128)(2,1)S(1)}, s16[136,512]{1,0:T(8,128)(2,1)S(1)}, u32[]{:S(2)}, u32[]{:S(2)}) %collective-permute-start.4) | collective-permute-done | bytes 139296 | tf_op jit(solution)/shard_map/ppermute | solution.py:235
  11.7 0.3 collective-permute-done.3.rest_1_
  12.0 0.7 copy-done.1
  12.7 0.7 shard_map.66
  13.5 0.6 copy-done.4
  14.1 1.5 %shard_map.64 = (bf16[128,768]{1,0:T(8,128)(2,1)S(1)}, bf16[128,768]{1,0:T(8,128)(2,1)S(1)}, bf16[128,768]{1,0:T(8,128)(2,1)S(1)}, bf16[128,768]{1,0:T(8,128)(2,...) custom-call(s32[1,32]{1,0:T(1,128)S(1)} %bitcast.7, ...), custom_call_target="tpu_custom_call" | custom-call | flops 1 | bytes 1 | tf_op jit(solution)/shard_map/pallas_call | solution.py:225
  15.6 1.6 %collective-permute-start = (bf16[128,768]{1,0:T(8,128)(2,1)S(1)}, bf16[128,768]{1,0:T(8,128)(2,1)S(1)}, u32[]{:S(2)}, u32[]{:S(2)}) collective-permute-start(bf16[128,768]{1,0:T(8,128)(2,1)S(1)} %get-tuple-element.38), channel_id=1, source_target_pairs={{0,1},{1,0},{2,3},{3,2},{4,5},{5,4},{6,7},{7,6},{8,9},{9,8},{10,11... | collective-permute-start | bytes 589832 | tf_op jit(solution)/shard_map/ppermute | solution.py:209
  17.2 2.6 %collective-permute-start.1 = (bf16[128,768]{1,0:T(8,128)(2,1)S(1)}, bf16[128,768]{1,0:T(8,128)(2,1)S(1)}, u32[]{:S(2)}, u32[]{:S(2)}) collective-permute-start(bf16[128,768]{1,0:T(8,128)(2,1)S(1)} %get-tuple-element.39), channel_id=1, source_target_pairs={{0,2},{1,3},{2,0},{3,1},{4,6},{5,7},{6,4},{7,5},{8,10},{9,11},{10,... | collective-permute-start | bytes 589832 | tf_op jit(solution)/shard_map/ppermute | solution.py:209
  19.8 0.2 collective-permute-start.2
  20.1 0.7 shard_map.67
  20.8 0.7 collective-permute-start.7
  21.5 3.5 %collective-permute-start.8 = (s16[136,512]{1,0:T(8,128)(2,1)S(1)}, s16[136,512]{1,0:T(8,128)(2,1)S(1)}, u32[]{:S(2)}, u32[]{:S(2)}) collective-permute-start(s16[136,512]{1,0:T(8,128)(2,1)S(1)} %get-tuple-element.43), channel_id=1, source_target_pairs={{0,2},{1,3},{2,0},{3,1},{4,6},{5,7},{6,4},{7,5},{8,10},{9,11},{10,... | collective-permute-start | bytes 417800 | tf_op jit(solution)/shard_map/ppermute | solution.py:209
  25.0 2.2 %collective-permute-done.refs_1_ = bf16[128,768]{1,0:T(8,128)(2,1)S(1)} collective-permute-done((bf16[128,768]{1,0:T(8,128)(2,1)S(1)}, bf16[128,768]{1,0:T(8,128)(2,1)S(1)}, u32[]{:S(2)}, u32[]{:S(2)}) %collective-permute-start) | collective-permute-done | bytes 196640 | tf_op jit(solution)/shard_map/ppermute | solution.py:209
  27.2 2.8 %collective-permute-start.9 = (s16[136,512]{1,0:T(8,128)(2,1)S(1)}, s16[136,512]{1,0:T(8,128)(2,1)S(1)}, u32[]{:S(2)}, u32[]{:S(2)}) collective-permute-start(s16[136,512]{1,0:T(8,128)(2,1)S(1)} %get-tuple-element.44), channel_id=1, source_target_pairs={{0,3},{1,2},{2,1},{3,0},{4,7},{5,6},{6,5},{7,4},{8,11},{9,10},{10,... | collective-permute-start | bytes 417800 | tf_op jit(solution)/shard_map/ppermute | solution.py:209
  30.0 4.4 %collective-permute-done.1.refs_2_ = bf16[128,768]{1,0:T(8,128)(2,1)S(1)} collective-permute-done((bf16[128,768]{1,0:T(8,128)(2,1)S(1)}, bf16[128,768]{1,0:T(8,128)(2,1)S(1)}, u32[]{:S(2)}, u32[]{:S(2)}) %collective-permute-start.1) | collective-permute-done | bytes 196640 | tf_op jit(solution)/shard_map/ppermute | solution.py:209
  34.4 11.8 %collective-permute-start.18 = (bf16[128,256]{1,0:T(8,128)(2,1)S(1)}, bf16[128,256]{1,0:T(8,128)(2,1)S(1)}, u32[]{:S(2)}, u32[]{:S(2)}) collective-permute-start(bf16[128,256]{1,0:T(8,128)(2,1)S(1)} %get-tuple-element.57), channel_id=1, source_target_pairs={{0,2},{1,3},{2,0},{3,1},{4,6},{5,7},{6,4},{7,5},{8,10},{9,11},{10,... | collective-permute-start | bytes 196616 | tf_op jit(solution)/shard_map/ppermute | solution.py:209
  46.2 1.3 %collective-permute-start.19 = (bf16[128,256]{1,0:T(8,128)(2,1)S(1)}, bf16[128,256]{1,0:T(8,128)(2,1)S(1)}, u32[]{:S(2)}, u32[]{:S(2)}) collective-permute-start(bf16[128,256]{1,0:T(8,128)(2,1)S(1)} %get-tuple-element.58), channel_id=1, source_target_pairs={{0,3},{1,2},{2,1},{3,0},{4,7},{5,6},{6,5},{7,4},{8,11},{9,10},{10,... | collective-permute-start | bytes 196616 | tf_op jit(solution)/shard_map/ppermute | solution.py:209
  47.5 0.8 collective-permute-done.8.refs_6_
  48.3 1.6 %shard_map.68 = (f32[128,256]{1,0:T(8,128)S(1)}, s16[136,256]{1,0:T(8,128)(2,1)S(1)}, s16[136,256]{1,0:T(8,128)(2,1)S(1)}, s16[136,256]{1,0:T(8,128)(2,1)S(1)}) custom-call(bf16[128,768]{1,0:T(8,128)(2,1)S(1)} %get-tuple-element.37.refs_0_, bf16[128,768]{1,0:T(8,128)(2,1)S(1)} %collective-permute-done.refs_1_, ...), custom_call_target="tpu_custom_call" | custom-call | flops 536870912 | bytes 1 | tf_op jit(solution)/shard_map/pallas_call | solution.py:253
  50.0 5.7 %collective-permute-start.10 = (s16[136,256]{1,0:T(8,128)(2,1)S(1)}, s16[136,256]{1,0:T(8,128)(2,1)S(1)}, u32[]{:S(2)}, u32[]{:S(2)}) collective-permute-start(s16[136,256]{1,0:T(8,128)(2,1)S(1)} %get-tuple-element.46), channel_id=1, source_target_pairs={{0,1},{1,0},{2,3},{3,2},{4,5},{5,4},{6,7},{7,6},{8,9},{9,8},{10,11... | collective-permute-start | bytes 208904 | tf_op jit(solution)/shard_map/ppermute | solution.py:209
  55.7 1.1 %collective-permute-start.11 = (s16[136,256]{1,0:T(8,128)(2,1)S(1)}, s16[136,256]{1,0:T(8,128)(2,1)S(1)}, u32[]{:S(2)}, u32[]{:S(2)}) collective-permute-start(s16[136,256]{1,0:T(8,128)(2,1)S(1)} %get-tuple-element.47), channel_id=1, source_target_pairs={{0,2},{1,3},{2,0},{3,1},{4,6},{5,7},{6,4},{7,5},{8,10},{9,11},{10,... | collective-permute-start | bytes 208904 | tf_op jit(solution)/shard_map/ppermute | solution.py:209
  56.8 1.4 %collective-permute-start.12 = (s16[136,256]{1,0:T(8,128)(2,1)S(1)}, s16[136,256]{1,0:T(8,128)(2,1)S(1)}, u32[]{:S(2)}, u32[]{:S(2)}) collective-permute-start(s16[136,256]{1,0:T(8,128)(2,1)S(1)} %get-tuple-element.48), channel_id=1, source_target_pairs={{0,3},{1,2},{2,1},{3,0},{4,7},{5,6},{6,5},{7,4},{8,11},{9,10},{10,... | collective-permute-start | bytes 208904 | tf_op jit(solution)/shard_map/ppermute | solution.py:209
  58.2 1.6 %shard_map.71 = (f32[128,256]{1,0:T(8,128)S(1)}, s16[136,256]{1,0:T(8,128)(2,1)S(1)}, s16[136,256]{1,0:T(8,128)(2,1)S(1)}, s16[136,256]{1,0:T(8,128)(2,1)S(1)}) custom-call(bf16[128,768]{1,0:T(8,128)(2,1)S(1)} %get-tuple-element.37.refs_0_, bf16[128,768]{1,0:T(8,128)(2,1)S(1)} %collective-permute-done.refs_1_, ...), custom_call_target="tpu_custom_call" | custom-call | flops 536870912 | bytes 1 | tf_op jit(solution)/shard_map/pallas_call | solution.py:253
  59.8 1.1 %collective-permute-start.20 = (s16[136,256]{1,0:T(8,128)(2,1)S(1)}, s16[136,256]{1,0:T(8,128)(2,1)S(1)}, u32[]{:S(2)}, u32[]{:S(2)}) collective-permute-start(s16[136,256]{1,0:T(8,128)(2,1)S(1)} %get-tuple-element.60), channel_id=1, source_target_pairs={{0,1},{1,0},{2,3},{3,2},{4,5},{5,4},{6,7},{7,6},{8,9},{9,8},{10,11... | collective-permute-start | bytes 208904 | tf_op jit(solution)/shard_map/ppermute | solution.py:209
  60.9 2.0 %collective-permute-start.21 = (s16[136,256]{1,0:T(8,128)(2,1)S(1)}, s16[136,256]{1,0:T(8,128)(2,1)S(1)}, u32[]{:S(2)}, u32[]{:S(2)}) collective-permute-start(s16[136,256]{1,0:T(8,128)(2,1)S(1)} %get-tuple-element.61), channel_id=1, source_target_pairs={{0,2},{1,3},{2,0},{3,1},{4,6},{5,7},{6,4},{7,5},{8,10},{9,11},{10,... | collective-permute-start | bytes 208904 | tf_op jit(solution)/shard_map/ppermute | solution.py:209
  62.9 1.4 %collective-permute-start.22 = (s16[136,256]{1,0:T(8,128)(2,1)S(1)}, s16[136,256]{1,0:T(8,128)(2,1)S(1)}, u32[]{:S(2)}, u32[]{:S(2)}) collective-permute-start(s16[136,256]{1,0:T(8,128)(2,1)S(1)} %get-tuple-element.62), channel_id=1, source_target_pairs={{0,3},{1,2},{2,1},{3,0},{4,7},{5,6},{6,5},{7,4},{8,11},{9,10},{10,... | collective-permute-start | bytes 208904 | tf_op jit(solution)/shard_map/ppermute | solution.py:209
  64.3 0.6 shard_map.69
  65.0 3.0 %collective-permute-done.21.rest_2_ = s16[136,256]{1,0:T(8,128)(2,1)S(1)} collective-permute-done((s16[136,256]{1,0:T(8,128)(2,1)S(1)}, s16[136,256]{1,0:T(8,128)(2,1)S(1)}, u32[]{:S(2)}, u32[]{:S(2)}) %collective-permute-start.21) | collective-permute-done | bytes 69664 | tf_op jit(solution)/shard_map/ppermute | solution.py:209
  67.9 1.2 %collective-permute-done.22.rest_3_ = s16[136,256]{1,0:T(8,128)(2,1)S(1)} collective-permute-done((s16[136,256]{1,0:T(8,128)(2,1)S(1)}, s16[136,256]{1,0:T(8,128)(2,1)S(1)}, u32[]{:S(2)}, u32[]{:S(2)}) %collective-permute-start.22) | collective-permute-done | bytes 69664 | tf_op jit(solution)/shard_map/ppermute | solution.py:209
  69.1 0.6 shard_map.72
  69.8 0.2 shard_map.70
  70.0 1.6 %collective-permute-start.14 = (s16[136,256]{1,0:T(8,128)(2,1)S(1)}, s16[136,256]{1,0:T(8,128)(2,1)S(1)}, u32[]{:S(2)}, u32[]{:S(2)}) collective-permute-start(s16[136,256]{1,0:T(8,128)(2,1)S(1)} %get-tuple-element.52), channel_id=1, source_target_pairs={{0,8},{4,12},{8,0},{12,4},{16,24},{20,28},{24,16},{28,20},{1,9},{5... | collective-permute-start | bytes 208904 | tf_op jit(solution)/shard_map/ppermute | solution.py:277
  71.6 0.7 collective-permute-start.15
  72.3 1.3 %collective-permute-start.16 = (s16[136,256]{1,0:T(8,128)(2,1)S(1)}, s16[136,256]{1,0:T(8,128)(2,1)S(1)}, u32[]{:S(2)}, u32[]{:S(2)}) collective-permute-start(s16[136,256]{1,0:T(8,128)(2,1)S(1)} %get-tuple-element.54), channel_id=1, source_target_pairs={{0,24},{4,28},{8,16},{12,20},{16,8},{20,12},{24,0},{28,4},{1,25},{... | collective-permute-start | bytes 208904 | tf_op jit(solution)/shard_map/ppermute | solution.py:277
  73.5 0.2 shard_map.73
  73.7 1.6 %collective-permute-start.24 = (s16[136,256]{1,0:T(8,128)(2,1)S(1)}, s16[136,256]{1,0:T(8,128)(2,1)S(1)}, u32[]{:S(2)}, u32[]{:S(2)}) collective-permute-start(s16[136,256]{1,0:T(8,128)(2,1)S(1)} %get-tuple-element.66), channel_id=1, source_target_pairs={{0,8},{4,12},{8,0},{12,4},{16,24},{20,28},{24,16},{28,20},{1,9},{5... | collective-permute-start | bytes 208904 | tf_op jit(solution)/shard_map/ppermute | solution.py:277
  75.3 0.7 collective-permute-start.25
  76.0 1.3 %collective-permute-start.26 = (s16[136,256]{1,0:T(8,128)(2,1)S(1)}, s16[136,256]{1,0:T(8,128)(2,1)S(1)}, u32[]{:S(2)}, u32[]{:S(2)}) collective-permute-start(s16[136,256]{1,0:T(8,128)(2,1)S(1)} %get-tuple-element.68), channel_id=1, source_target_pairs={{0,24},{4,28},{8,16},{12,20},{16,8},{20,12},{24,0},{28,4},{1,25},{... | collective-permute-start | bytes 208904 | tf_op jit(solution)/shard_map/ppermute | solution.py:277
  77.3 0.8 collective-permute-done.16.refs_3_
  78.0 0.6 collective-permute-done.24.refs_5_
  78.6 1.6 %collective-permute-done.25.refs_6_ = s16[136,256]{1,0:T(8,128)(2,1)S(1)} collective-permute-done((s16[136,256]{1,0:T(8,128)(2,1)S(1)}, s16[136,256]{1,0:T(8,128)(2,1)S(1)}, u32[]{:S(2)}, u32[]{:S(2)}) %collective-permute-start.25) | collective-permute-done | bytes 69664 | tf_op jit(solution)/shard_map/ppermute | solution.py:277
  80.2 1.0 %collective-permute-done.26.refs_7_ = s16[136,256]{1,0:T(8,128)(2,1)S(1)} collective-permute-done((s16[136,256]{1,0:T(8,128)(2,1)S(1)}, s16[136,256]{1,0:T(8,128)(2,1)S(1)}, u32[]{:S(2)}, u32[]{:S(2)}) %collective-permute-start.26) | collective-permute-done | bytes 69664 | tf_op jit(solution)/shard_map/ppermute | solution.py:277
  81.2 0.8 %shard_map.74 = f32[128,512]{1,0:T(8,128)} custom-call(f32[128,256]{1,0:T(8,128)S(1)} %get-tuple-element.51.refs_0_, s16[136,256]{1,0:T(8,128)(2,1)S(1)} %collective-permute-done.14.refs_1_, s16[136,256]{1,0:T(8,128)(2,1)S(1)} %collective-permute-done.15.refs_2_, s16[136,256]{1,0:T(8,128)(2,1)S(1)} %collective-permute-done.16.refs_3_, ...), custom_call_target="tpu_custom_call" | custom-call | flops 1 | bytes 1 | tf_op jit(solution)/shard_map/pallas_call | solution.py:278
  (27 shorter events, 0.4 us)
Async XLA Ops:
  0.0 0.9 %copy-start = (f32[1,128,512]{2,1,0:T(8,128)S(1)}, f32[1,128,512]{2,1,0:T(8,128)}, u32[]{:S(2)}) copy-start(f32[1,128,512]{2,1,0:T(8,128)} %param.6) | copy-start | bytes 786436
  1.1 8.1 %collective-permute-start.5 = (s16[136,512]{1,0:T(8,128)(2,1)S(1)}, s16[136,512]{1,0:T(8,128)(2,1)S(1)}, u32[]{:S(2)}, u32[]{:S(2)}) collective-permute-start(s16[136,512]{1,0:T(8,128)(2,1)S(1)} %shard_map.65.rest_0_), channel_id=1, source_target_pairs={{0,24},{4,28},{8,16},{12,20},{16,8},{20,12},{24,0},{28,4},{1,25},{... | collective-permute-start | bytes 417800 | tf_op jit(solution)/shard_map/ppermute | solution.py:235
  5.1 6.7 %collective-permute-start.4 = (s16[136,512]{1,0:T(8,128)(2,1)S(1)}, s16[136,512]{1,0:T(8,128)(2,1)S(1)}, u32[]{:S(2)}, u32[]{:S(2)}) collective-permute-start(s16[136,512]{1,0:T(8,128)(2,1)S(1)} %shard_map.65.rest_0_), channel_id=1, source_target_pairs={{0,16},{4,20},{8,24},{12,28},{16,0},{20,4},{24,8},{28,12},{1,17},{... | collective-permute-start | bytes 417800 | tf_op jit(solution)/shard_map/ppermute | solution.py:235
  5.6 6.4 %collective-permute-start.3 = (s16[136,512]{1,0:T(8,128)(2,1)S(1)}, s16[136,512]{1,0:T(8,128)(2,1)S(1)}, u32[]{:S(2)}, u32[]{:S(2)}) collective-permute-start(s16[136,512]{1,0:T(8,128)(2,1)S(1)} %shard_map.65.rest_0_), channel_id=1, source_target_pairs={{0,8},{4,12},{8,0},{12,4},{16,24},{20,28},{24,16},{28,20},{1,9},{5... | collective-permute-start | bytes 417800 | tf_op jit(solution)/shard_map/ppermute | solution.py:235
  12.0 0.7 copy-start.1
  13.4 6.7 %collective-permute-start.6 = (s16[4,136,512]{2,1,0:T(8,128)(2,1)S(1)}, s16[4,136,512]{2,1,0:T(8,128)(2,1)S(1)}, u32[]{:S(2)}, u32[]{:S(2)}) collective-permute-start(s16[4,136,512]{2,1,0:T(8,128)(2,1)S(1)} %shard_map.66), channel_id=1, source_target_pairs={{0,4},{4,0},{8,12},{12,8},{16,20},{20,16},{24,28},{28,24},{1,5},{5... | collective-permute-start | bytes 1671176 | tf_op jit(solution)/shard_map/ppermute | solution.py:241
  13.4 0.7 copy-start.4
  14.1 6.0 %copy-start.2 = (s32[32]{0:T(128)S(1)}, s32[32]{0:T(128)}, u32[]{:S(2)}) copy-start(s32[32]{0:T(128)} %in_ref.3) | copy-start | bytes 388
  15.6 48.7 %copy-start.3 = (s32[32,1]{0,1:T(1,128)S(1)}, s32[32,1]{0,1:T(1,128)}, u32[]{:S(2)}) copy-start(s32[32,1]{0,1:T(1,128)} %param.10) | copy-start | bytes 388
  15.6 11.6 %collective-permute-start = (bf16[128,768]{1,0:T(8,128)(2,1)S(1)}, bf16[128,768]{1,0:T(8,128)(2,1)S(1)}, u32[]{:S(2)}, u32[]{:S(2)}) collective-permute-start(bf16[128,768]{1,0:T(8,128)(2,1)S(1)} %get-tuple-element.38), channel_id=1, source_target_pairs={{0,1},{1,0},{2,3},{3,2},{4,5},{5,4},{6,7},{7,6},{8,9},{9,8},{10,11... | collective-permute-start | bytes 589832 | tf_op jit(solution)/shard_map/ppermute | solution.py:209
  17.2 17.2 %collective-permute-start.1 = (bf16[128,768]{1,0:T(8,128)(2,1)S(1)}, bf16[128,768]{1,0:T(8,128)(2,1)S(1)}, u32[]{:S(2)}, u32[]{:S(2)}) collective-permute-start(bf16[128,768]{1,0:T(8,128)(2,1)S(1)} %get-tuple-element.39), channel_id=1, source_target_pairs={{0,2},{1,3},{2,0},{3,1},{4,6},{5,7},{6,4},{7,5},{8,10},{9,11},{10,... | collective-permute-start | bytes 589832 | tf_op jit(solution)/shard_map/ppermute | solution.py:209
  19.8 14.6 %collective-permute-start.2 = (bf16[128,768]{1,0:T(8,128)(2,1)S(1)}, bf16[128,768]{1,0:T(8,128)(2,1)S(1)}, u32[]{:S(2)}, u32[]{:S(2)}) collective-permute-start(bf16[128,768]{1,0:T(8,128)(2,1)S(1)} %get-tuple-element.40), channel_id=1, source_target_pairs={{0,3},{1,2},{2,1},{3,0},{4,7},{5,6},{6,5},{7,4},{8,11},{9,10},{10,... | collective-permute-start | bytes 589832 | tf_op jit(solution)/shard_map/ppermute | solution.py:209
  20.8 25.4 %collective-permute-start.7 = (s16[136,512]{1,0:T(8,128)(2,1)S(1)}, s16[136,512]{1,0:T(8,128)(2,1)S(1)}, u32[]{:S(2)}, u32[]{:S(2)}) collective-permute-start(s16[136,512]{1,0:T(8,128)(2,1)S(1)} %get-tuple-element.42), channel_id=1, source_target_pairs={{0,1},{1,0},{2,3},{3,2},{4,5},{5,4},{6,7},{7,6},{8,9},{9,8},{10,11... | collective-permute-start | bytes 417800 | tf_op jit(solution)/shard_map/ppermute | solution.py:209
  21.5 26.8 %collective-permute-start.8 = (s16[136,512]{1,0:T(8,128)(2,1)S(1)}, s16[136,512]{1,0:T(8,128)(2,1)S(1)}, u32[]{:S(2)}, u32[]{:S(2)}) collective-permute-start(s16[136,512]{1,0:T(8,128)(2,1)S(1)} %get-tuple-element.43), channel_id=1, source_target_pairs={{0,2},{1,3},{2,0},{3,1},{4,6},{5,7},{6,4},{7,5},{8,10},{9,11},{10,... | collective-permute-start | bytes 417800 | tf_op jit(solution)/shard_map/ppermute | solution.py:209
  27.2 21.1 %collective-permute-start.9 = (s16[136,512]{1,0:T(8,128)(2,1)S(1)}, s16[136,512]{1,0:T(8,128)(2,1)S(1)}, u32[]{:S(2)}, u32[]{:S(2)}) collective-permute-start(s16[136,512]{1,0:T(8,128)(2,1)S(1)} %get-tuple-element.44), channel_id=1, source_target_pairs={{0,3},{1,2},{2,1},{3,0},{4,7},{5,6},{6,5},{7,4},{8,11},{9,10},{10,... | collective-permute-start | bytes 417800 | tf_op jit(solution)/shard_map/ppermute | solution.py:209
  34.4 22.3 %collective-permute-start.17 = (bf16[128,256]{1,0:T(8,128)(2,1)S(1)}, bf16[128,256]{1,0:T(8,128)(2,1)S(1)}, u32[]{:S(2)}, u32[]{:S(2)}) collective-permute-start(bf16[128,256]{1,0:T(8,128)(2,1)S(1)} %get-tuple-element.56), channel_id=1, source_target_pairs={{0,1},{1,0},{2,3},{3,2},{4,5},{5,4},{6,7},{7,6},{8,9},{9,8},{10,11... | collective-permute-start | bytes 196616 | tf_op jit(solution)/shard_map/ppermute | solution.py:209
  34.4 23.7 %collective-permute-start.18 = (bf16[128,256]{1,0:T(8,128)(2,1)S(1)}, bf16[128,256]{1,0:T(8,128)(2,1)S(1)}, u32[]{:S(2)}, u32[]{:S(2)}) collective-permute-start(bf16[128,256]{1,0:T(8,128)(2,1)S(1)} %get-tuple-element.57), channel_id=1, source_target_pairs={{0,2},{1,3},{2,0},{3,1},{4,6},{5,7},{6,4},{7,5},{8,10},{9,11},{10,... | collective-permute-start | bytes 196616 | tf_op jit(solution)/shard_map/ppermute | solution.py:209
  46.2 12.0 %collective-permute-start.19 = (bf16[128,256]{1,0:T(8,128)(2,1)S(1)}, bf16[128,256]{1,0:T(8,128)(2,1)S(1)}, u32[]{:S(2)}, u32[]{:S(2)}) collective-permute-start(bf16[128,256]{1,0:T(8,128)(2,1)S(1)} %get-tuple-element.58), channel_id=1, source_target_pairs={{0,3},{1,2},{2,1},{3,0},{4,7},{5,6},{6,5},{7,4},{8,11},{9,10},{10,... | collective-permute-start | bytes 196616 | tf_op jit(solution)/shard_map/ppermute | solution.py:209
  50.0 12.9 %collective-permute-start.10 = (s16[136,256]{1,0:T(8,128)(2,1)S(1)}, s16[136,256]{1,0:T(8,128)(2,1)S(1)}, u32[]{:S(2)}, u32[]{:S(2)}) collective-permute-start(s16[136,256]{1,0:T(8,128)(2,1)S(1)} %get-tuple-element.46), channel_id=1, source_target_pairs={{0,1},{1,0},{2,3},{3,2},{4,5},{5,4},{6,7},{7,6},{8,9},{9,8},{10,11... | collective-permute-start | bytes 208904 | tf_op jit(solution)/shard_map/ppermute | solution.py:209
  55.7 8.6 %collective-permute-start.11 = (s16[136,256]{1,0:T(8,128)(2,1)S(1)}, s16[136,256]{1,0:T(8,128)(2,1)S(1)}, u32[]{:S(2)}, u32[]{:S(2)}) collective-permute-start(s16[136,256]{1,0:T(8,128)(2,1)S(1)} %get-tuple-element.47), channel_id=1, source_target_pairs={{0,2},{1,3},{2,0},{3,1},{4,6},{5,7},{6,4},{7,5},{8,10},{9,11},{10,... | collective-permute-start | bytes 208904 | tf_op jit(solution)/shard_map/ppermute | solution.py:209
  56.8 7.5 %collective-permute-start.12 = (s16[136,256]{1,0:T(8,128)(2,1)S(1)}, s16[136,256]{1,0:T(8,128)(2,1)S(1)}, u32[]{:S(2)}, u32[]{:S(2)}) collective-permute-start(s16[136,256]{1,0:T(8,128)(2,1)S(1)} %get-tuple-element.48), channel_id=1, source_target_pairs={{0,3},{1,2},{2,1},{3,0},{4,7},{5,6},{6,5},{7,4},{8,11},{9,10},{10,... | collective-permute-start | bytes 208904 | tf_op jit(solution)/shard_map/ppermute | solution.py:209
  59.8 5.1 %collective-permute-start.20 = (s16[136,256]{1,0:T(8,128)(2,1)S(1)}, s16[136,256]{1,0:T(8,128)(2,1)S(1)}, u32[]{:S(2)}, u32[]{:S(2)}) collective-permute-start(s16[136,256]{1,0:T(8,128)(2,1)S(1)} %get-tuple-element.60), channel_id=1, source_target_pairs={{0,1},{1,0},{2,3},{3,2},{4,5},{5,4},{6,7},{7,6},{8,9},{9,8},{10,11... | collective-permute-start | bytes 208904 | tf_op jit(solution)/shard_map/ppermute | solution.py:209
  60.9 7.0 %collective-permute-start.21 = (s16[136,256]{1,0:T(8,128)(2,1)S(1)}, s16[136,256]{1,0:T(8,128)(2,1)S(1)}, u32[]{:S(2)}, u32[]{:S(2)}) collective-permute-start(s16[136,256]{1,0:T(8,128)(2,1)S(1)} %get-tuple-element.61), channel_id=1, source_target_pairs={{0,2},{1,3},{2,0},{3,1},{4,6},{5,7},{6,4},{7,5},{8,10},{9,11},{10,... | collective-permute-start | bytes 208904 | tf_op jit(solution)/shard_map/ppermute | solution.py:209
  62.9 6.2 %collective-permute-start.22 = (s16[136,256]{1,0:T(8,128)(2,1)S(1)}, s16[136,256]{1,0:T(8,128)(2,1)S(1)}, u32[]{:S(2)}, u32[]{:S(2)}) collective-permute-start(s16[136,256]{1,0:T(8,128)(2,1)S(1)} %get-tuple-element.62), channel_id=1, source_target_pairs={{0,3},{1,2},{2,1},{3,0},{4,7},{5,6},{6,5},{7,4},{8,11},{9,10},{10,... | collective-permute-start | bytes 208904 | tf_op jit(solution)/shard_map/ppermute | solution.py:209
  64.9 4.9 %collective-permute-start.13 = (f32[4,128,256]{2,1,0:T(8,128)S(1)}, f32[4,128,256]{2,1,0:T(8,128)S(1)}, u32[]{:S(2)}, u32[]{:S(2)}) collective-permute-start(f32[4,128,256]{2,1,0:T(8,128)S(1)} %get-tuple-element.50), channel_id=1, source_target_pairs={{0,4},{4,0},{8,12},{12,8},{16,20},{20,16},{24,28},{28,24},{1,5},{5... | collective-permute-start | bytes 1572872 | tf_op jit(solution)/shard_map/ppermute | solution.py:272
  69.7 3.8 %collective-permute-start.23 = (f32[4,128,256]{2,1,0:T(8,128)S(1)}, f32[4,128,256]{2,1,0:T(8,128)S(1)}, u32[]{:S(2)}, u32[]{:S(2)}) collective-permute-start(f32[4,128,256]{2,1,0:T(8,128)S(1)} %get-tuple-element.64), channel_id=1, source_target_pairs={{0,4},{4,0},{8,12},{12,8},{16,20},{20,16},{24,28},{28,24},{1,5},{5... | collective-permute-start | bytes 1572872 | tf_op jit(solution)/shard_map/ppermute | solution.py:272
  70.0 6.1 %collective-permute-start.14 = (s16[136,256]{1,0:T(8,128)(2,1)S(1)}, s16[136,256]{1,0:T(8,128)(2,1)S(1)}, u32[]{:S(2)}, u32[]{:S(2)}) collective-permute-start(s16[136,256]{1,0:T(8,128)(2,1)S(1)} %get-tuple-element.52), channel_id=1, source_target_pairs={{0,8},{4,12},{8,0},{12,4},{16,24},{20,28},{24,16},{28,20},{1,9},{5... | collective-permute-start | bytes 208904 | tf_op jit(solution)/shard_map/ppermute | solution.py:277
  71.6 5.7 %collective-permute-start.15 = (s16[136,256]{1,0:T(8,128)(2,1)S(1)}, s16[136,256]{1,0:T(8,128)(2,1)S(1)}, u32[]{:S(2)}, u32[]{:S(2)}) collective-permute-start(s16[136,256]{1,0:T(8,128)(2,1)S(1)} %get-tuple-element.53), channel_id=1, source_target_pairs={{0,16},{4,20},{8,24},{12,28},{16,0},{20,4},{24,8},{28,12},{1,17},{... | collective-permute-start | bytes 208904 | tf_op jit(solution)/shard_map/ppermute | solution.py:277
  72.3 5.8 %collective-permute-start.16 = (s16[136,256]{1,0:T(8,128)(2,1)S(1)}, s16[136,256]{1,0:T(8,128)(2,1)S(1)}, u32[]{:S(2)}, u32[]{:S(2)}) collective-permute-start(s16[136,256]{1,0:T(8,128)(2,1)S(1)} %get-tuple-element.54), channel_id=1, source_target_pairs={{0,24},{4,28},{8,16},{12,20},{16,8},{20,12},{24,0},{28,4},{1,25},{... | collective-permute-start | bytes 208904 | tf_op jit(solution)/shard_map/ppermute | solution.py:277
  73.7 4.9 %collective-permute-start.24 = (s16[136,256]{1,0:T(8,128)(2,1)S(1)}, s16[136,256]{1,0:T(8,128)(2,1)S(1)}, u32[]{:S(2)}, u32[]{:S(2)}) collective-permute-start(s16[136,256]{1,0:T(8,128)(2,1)S(1)} %get-tuple-element.66), channel_id=1, source_target_pairs={{0,8},{4,12},{8,0},{12,4},{16,24},{20,28},{24,16},{28,20},{1,9},{5... | collective-permute-start | bytes 208904 | tf_op jit(solution)/shard_map/ppermute | solution.py:277
  75.3 4.9 %collective-permute-start.25 = (s16[136,256]{1,0:T(8,128)(2,1)S(1)}, s16[136,256]{1,0:T(8,128)(2,1)S(1)}, u32[]{:S(2)}, u32[]{:S(2)}) collective-permute-start(s16[136,256]{1,0:T(8,128)(2,1)S(1)} %get-tuple-element.67), channel_id=1, source_target_pairs={{0,16},{4,20},{8,24},{12,28},{16,0},{20,4},{24,8},{28,12},{1,17},{... | collective-permute-start | bytes 208904 | tf_op jit(solution)/shard_map/ppermute | solution.py:277
  76.0 5.2 %collective-permute-start.26 = (s16[136,256]{1,0:T(8,128)(2,1)S(1)}, s16[136,256]{1,0:T(8,128)(2,1)S(1)}, u32[]{:S(2)}, u32[]{:S(2)}) collective-permute-start(s16[136,256]{1,0:T(8,128)(2,1)S(1)} %get-tuple-element.68), channel_id=1, source_target_pairs={{0,24},{4,28},{8,16},{12,20},{16,8},{20,12},{24,0},{28,4},{1,25},{... | collective-permute-start | bytes 208904 | tf_op jit(solution)/shard_map/ppermute | solution.py:277

commit v6 on v5

--- a/solution.py
+++ b/solution.py
@@ -8,7 +8,7 @@
 from jax.sharding import PartitionSpec as P
 
 
-GRID, LIMIT, LEVELS, HEAD, HALVES = 1024.0, 32767.0, 256.0, 8, 2
+GRID, LIMIT, LEVELS, LANES, HALVES = 1024.0, 32767.0, 256.0, 128, 2
 PICK_BYTES = 54_000_000
 VMEM_BYTES = 16 * 1024 * 1024
 VMEM = pl.BlockSpec(memory_space=pltpu.VMEM)
@@ -33,8 +33,14 @@
     return jnp.sum(jnp.where(places == index, table[...], 0).astype(jnp.float32)).astype(jnp.int32)
 
 
+def coded(rows, cols):
+    runs = cols // LANES
+    return (runs * rows + -(-2 * runs // 8) * 8, LANES)
+
+
 def encode(value, out, centred):
-    rows = value.shape[0]
+    rows, cols = value.shape
+    runs = cols // LANES
     centre = jnp.zeros_like(value[:1])
     if centred:
         middle = (jnp.max(value, axis=0, keepdims=True) + jnp.min(value, axis=0, keepdims=True)) / 2
@@ -45,18 +51,27 @@
     level = (level + jnp.where(level > 0, 1.0, 0.0)).astype(jnp.int32).astype(jnp.float32)
     scaled = value * (LIMIT / jnp.exp(level / LEVELS))
     scaled = jnp.clip(scaled + jnp.where(scaled > 0, 0.5, -0.5), -LIMIT, LIMIT)
-    out[pl.ds(0, rows), :] = scaled.astype(jnp.int32).astype(jnp.int16)
-    lines = lax.broadcasted_iota(jnp.int32, (HEAD, value.shape[1]), 0)
-    head = jnp.where(lines == 0, level.astype(jnp.int32), centre.astype(jnp.int32))
-    out[pl.ds(rows, HEAD), :] = head.astype(jnp.int16)
-
-
-def decode(code):
-    rows = code.shape[0] - HEAD
-    head = code[pl.ds(rows, HEAD), :].astype(jnp.int32).astype(jnp.float32)
-    step = jnp.exp(head[0:1] / LEVELS) / LIMIT
-    value = code[pl.ds(0, rows), :].astype(jnp.int32).astype(jnp.float32)
-    return value * step + head[1:2] / GRID
+    scaled = scaled.astype(jnp.int32).astype(jnp.int16)
+    height = out.shape[0] - runs * rows
+    lines = lax.broadcasted_iota(jnp.int32, (height, LANES), 0)
+    head = jnp.zeros((height, LANES), jnp.float32)
+    for run in range(runs):
+        place = slice(run * LANES, (run + 1) * LANES)
+        out[pl.ds(run * rows, rows), :] = scaled[:, place]
+        head = jnp.where(lines == run, level[:, place], head)
+        head = jnp.where(lines == runs + run, centre[:, place], head)
+    out[pl.ds(runs * rows, height), :] = head.astype(jnp.int32).astype(jnp.int16)
+
+
+def decode(code, rows, cols):
+    runs = cols // LANES
+    head = code[pl.ds(runs * rows, code.shape[0] - runs * rows), :].astype(jnp.int32).astype(jnp.float32)
+    pieces = []
+    for run in range(runs):
+        step = jnp.exp(head[run : run + 1] / LEVELS) / LIMIT
+        value = code[pl.ds(run * rows, rows), :].astype(jnp.int32).astype(jnp.float32)
+        pieces.append(value * step + head[runs + run : runs + run + 1] / GRID)
+    return jnp.concatenate(pieces, axis=1)
 
 
 def pick_kernel(base, me, count, term_ref, left_ref, right_ref, *rest):
@@ -65,8 +80,8 @@
     width = cols // HALVES
     copies = []
     start, mine = base(), me()
-    for step in range(count):
-        term = entry(term_ref, start + (mine ^ step))
+    terms = [entry(term_ref, start + (mine ^ step)) for step in range(count)]
+    for step, term in enumerate(terms):
         copies.append((left_ref.at[term], outs[step].at[:, pl.ds(0, cols)]))
         for half in range(HALVES):
             out = outs[half * count + step]
@@ -91,8 +106,8 @@
     held, out = rest[:chips], rest[chips]
     start = base()
     chip, core = sec() // 2, lax.rem(sec(), 2)
-    for slot in range(count):
-        source = in_ref[start + slot]
+    sources = [entry(in_ref, start + slot) for slot in range(count)]
+    for slot, source in enumerate(sources):
         for step in range(chips):
             @pl.when((source // 2 == chip ^ step) & (lax.rem(source, 2) == core))
             def _():
@@ -103,9 +118,9 @@
     held, paired, outs = rest[:chips], rest[chips], rest[chips + 1 :]
     start, mine = base(), me()
     chip, core = sec() // 2, lax.rem(sec(), 2)
-    for step in range(count):
-        slot = mine ^ step
-        source = in_ref[start + slot]
+    slots = [mine ^ step for step in range(count)]
+    sources = [entry(in_ref, start + slot) for slot in slots]
+    for step, (slot, source) in enumerate(zip(slots, sources)):
         same = lax.rem(source, 2) == core
         for hop in range(chips):
             @pl.when((source // 2 == chip ^ hop) & same)
@@ -126,7 +141,7 @@
     for step in range(count):
         place = pl.ds(pl.multiple_of((mine ^ step) * rows, rows), rows)
         right[place, :] = lates[step][...] if half else envs[step][:, pl.ds(cols, width)]
-        psi = decode(psis[step])
+        psi = decode(psis[step], rows, cols)
         top = psi.astype(jnp.bfloat16)
         high[place, :] = top
         low[place, :] = (psi - top.astype(jnp.float32)).astype(jnp.bfloat16)
@@ -152,10 +167,10 @@
     chip, core = sec() // 2, lax.rem(sec(), 2)
     keep[...] = jnp.zeros(keep.shape, jnp.float32)
     send[...] = jnp.zeros(send.shape, jnp.float32)
-    for step in range(count):
-        target = entry(target_ref, start + (mine ^ step))
+    targets = [entry(target_ref, start + (mine ^ step)) for step in range(count)]
+    for step, target in enumerate(targets):
         hop = (target // 2) ^ chip
-        part = parts[0][...] if step == 0 else decode(parts[step])
+        part = parts[0][...] if step == 0 else decode(parts[step], *parts[0].shape)
         mine_too = lax.rem(target, 2) == core
 
         @pl.when(mine_too)
@@ -182,7 +197,7 @@
         mine = refs[half * chips : (half + 1) * chips]
         total = mine[0][...]
         for hop in range(1, chips):
-            total = total + decode(mine[hop])
+            total = total + decode(mine[hop], *mine[0].shape)
         refs[-1][:, half * width : (half + 1) * width] = total
 
 
@@ -210,10 +225,10 @@
         return got
 
     pair = [(i, i ^ 1) for i in range(groups)]
-    code = jax.ShapeDtypeStruct((rows + HEAD, cols), jnp.int16)
+    code = jax.ShapeDtypeStruct(coded(rows, cols), jnp.int16)
     width = cols // HALVES
     part = jax.ShapeDtypeStruct((rows, width), f32)
-    piece = jax.ShapeDtypeStruct((rows + HEAD, width), jnp.int16)
+    piece = jax.ShapeDtypeStruct(coded(rows, width), jnp.int16)
     stack = jax.ShapeDtypeStruct((chips, rows, width), f32)
 
     keeps, sends, held = [None] * HALVES, [None] * HALVES, None
@@ -236,14 +251,14 @@
         sent = call(
             functools.partial(partner_psi_kernel, partner_base, sec, count, chips),
             jax.ShapeDtypeStruct((count, *code.shape), code.dtype),
-            [SMEM] + [VMEM] * chips,
-        )(task_in, *held)
+            [VMEM] * (chips + 1),
+        )(task_in[None], *held)
         paired = lax.ppermute(sent, "sec", pair)
         psis = call(
             functools.partial(own_psi_kernel, base, sec, me, count, chips),
             [code] * count,
-            [SMEM] + [VMEM] * (chips + 1),
-        )(task_in, *held, paired)
+            [VMEM] * (chips + 2),
+        )(task_in[None], *held, paired)
         psis = exchange(psis)
         lates = [exchange(picked[half * count : (half + 1) * count]) for half in range(1, HALVES)]
         full = count * rows

time: 82.3 us -> 80.6 us (0.979)
  Pallas kernels: 8.71 us -> 7.13 us
  transfers between devices with their start and end apart: 27 -> 27, of which waited for: 12 -> 12; matrix products, arithmetic and copies ran while one was open for 0% -> 0% of each run, Pallas kernels for 9% -> 7%
where the time goes in v6:
time: 80.6 us; the launch traced here: 80.4 us
  starting transfers between devices  48.8 us (61%)
  waiting for transfers between devices  22.1 us (27%)
  Pallas kernels  7.13 us (9%)
  local copies, waits for them, and re-layouts  2.27 us (3%)
    ppermute x15, starting transfers between devices, exchange(): got[s] = lax.ppermute(blocks[s], 'env', along(s))  36.8 us
    ppermute x15, waiting for transfers between devices, exchange(): got[s] = lax.ppermute(blocks[s], 'env', along(s))  12.1 us
    ppermute x6, starting transfers between devices, body(): lax.ppermute(mine[hop], 'sec', across(hop))  7.11 us
    ppermute x3, waiting for transfers between devices, body(): lax.ppermute(psi, 'sec', across(hop))  6 us
    ppermute x3, starting transfers between devices, body(): lax.ppermute(psi, 'sec', across(hop))  4.63 us
    ppermute x6, waiting for transfers between devices, body(): lax.ppermute(mine[hop], 'sec', across(hop))  3.95 us
    pallas_call x2, Pallas kernels, body(): call(functools.partial(task_kernel, me, count, half), [part] + [piece] *...  3.22 us
    unnamed x10, local copies, waits for them, and re-layouts  2.27 us
  transfers between devices with their start and end apart: 27, of which 12 were waited for; matrix products, arithmetic and copies ran while one was open for 0% of the time, Pallas kernels for 7%

profile of v6, /device:TPU:0, one launch (start us, length us, event | category | flops | bytes accessed | tf_op | source)
XLA Modules:
  0.0 80.4 jit_solution(9671723966270866709)
XLA Ops:
  0.0 0.9 %copy-done = f32[1,128,512]{2,1,0:T(8,128)S(1)} copy-done((f32[1,128,512]{2,1,0:T(8,128)S(1)}, f32[1,128,512]{2,1,0:T(8,128)}, u32[]{:S(2)}) %copy-start) | copy-done | bytes 262168
  1.0 0.2 shard_map.65.rest_0_
  1.1 4.0 %collective-permute-start.5 = (s16[520,128]{1,0:T(8,128)(2,1)S(1)}, s16[520,128]{1,0:T(8,128)(2,1)S(1)}, u32[]{:S(2)}, u32[]{:S(2)}) collective-permute-start(s16[520,128]{1,0:T(8,128)(2,1)S(1)} %shard_map.65.rest_0_), channel_id=1, source_target_pairs={{0,24},{4,28},{8,16},{12,20},{16,8},{20,12},{24,0},{28,4},{1,25},{... | collective-permute-start | bytes 399368 | tf_op jit(solution)/shard_map/ppermute | solution.py:250
  5.1 0.5 collective-permute-start.4
  5.7 3.3 %collective-permute-done.5.rest_3_ = s16[520,128]{1,0:T(8,128)(2,1)S(1)} collective-permute-done((s16[520,128]{1,0:T(8,128)(2,1)S(1)}, s16[520,128]{1,0:T(8,128)(2,1)S(1)}, u32[]{:S(2)}, u32[]{:S(2)}) %collective-permute-start.5) | collective-permute-done | bytes 133152 | tf_op jit(solution)/shard_map/ppermute | solution.py:250
  9.0 2.5 %collective-permute-done.4.rest_2_ = s16[520,128]{1,0:T(8,128)(2,1)S(1)} collective-permute-done((s16[520,128]{1,0:T(8,128)(2,1)S(1)}, s16[520,128]{1,0:T(8,128)(2,1)S(1)}, u32[]{:S(2)}, u32[]{:S(2)}) %collective-permute-start.4) | collective-permute-done | bytes 133152 | tf_op jit(solution)/shard_map/ppermute | solution.py:250
  11.5 0.2 collective-permute-done.3.rest_1_
  11.7 0.7 copy-done.1
  12.4 0.2 shard_map.66
  12.7 0.6 copy-done.4
  13.4 1.5 %shard_map.64 = (bf16[128,768]{1,0:T(8,128)(2,1)S(1)}, bf16[128,768]{1,0:T(8,128)(2,1)S(1)}, bf16[128,768]{1,0:T(8,128)(2,1)S(1)}, bf16[128,768]{1,0:T(8,128)(2,...) custom-call(s32[1,32]{1,0:T(1,128)S(1)} %bitcast.10, ...), custom_call_target="tpu_custom_call" | custom-call | flops 1 | bytes 1 | tf_op jit(solution)/shard_map/pallas_call | solution.py:240
  14.9 1.6 %collective-permute-start = (bf16[128,768]{1,0:T(8,128)(2,1)S(1)}, bf16[128,768]{1,0:T(8,128)(2,1)S(1)}, u32[]{:S(2)}, u32[]{:S(2)}) collective-permute-start(bf16[128,768]{1,0:T(8,128)(2,1)S(1)} %get-tuple-element.38), channel_id=1, source_target_pairs={{0,1},{1,0},{2,3},{3,2},{4,5},{5,4},{6,7},{7,6},{8,9},{9,8},{10,11... | collective-permute-start | bytes 589832 | tf_op jit(solution)/shard_map/ppermute | solution.py:224
  16.5 2.6 %collective-permute-start.1 = (bf16[128,768]{1,0:T(8,128)(2,1)S(1)}, bf16[128,768]{1,0:T(8,128)(2,1)S(1)}, u32[]{:S(2)}, u32[]{:S(2)}) collective-permute-start(bf16[128,768]{1,0:T(8,128)(2,1)S(1)} %get-tuple-element.39), channel_id=1, source_target_pairs={{0,2},{1,3},{2,0},{3,1},{4,6},{5,7},{6,4},{7,5},{8,10},{9,11},{10,... | collective-permute-start | bytes 589832 | tf_op jit(solution)/shard_map/ppermute | solution.py:224
  19.1 0.2 collective-permute-start.2
  19.3 0.3 shard_map.67
  19.6 0.7 collective-permute-start.7
  20.4 3.5 %collective-permute-start.8 = (s16[520,128]{1,0:T(8,128)(2,1)S(1)}, s16[520,128]{1,0:T(8,128)(2,1)S(1)}, u32[]{:S(2)}, u32[]{:S(2)}) collective-permute-start(s16[520,128]{1,0:T(8,128)(2,1)S(1)} %get-tuple-element.43), channel_id=1, source_target_pairs={{0,2},{1,3},{2,0},{3,1},{4,6},{5,7},{6,4},{7,5},{8,10},{9,11},{10,... | collective-permute-start | bytes 399368 | tf_op jit(solution)/shard_map/ppermute | solution.py:224
  23.9 2.6 %collective-permute-done.refs_1_ = bf16[128,768]{1,0:T(8,128)(2,1)S(1)} collective-permute-done((bf16[128,768]{1,0:T(8,128)(2,1)S(1)}, bf16[128,768]{1,0:T(8,128)(2,1)S(1)}, u32[]{:S(2)}, u32[]{:S(2)}) %collective-permute-start) | collective-permute-done | bytes 196640 | tf_op jit(solution)/shard_map/ppermute | solution.py:224
  26.5 2.8 %collective-permute-start.9 = (s16[520,128]{1,0:T(8,128)(2,1)S(1)}, s16[520,128]{1,0:T(8,128)(2,1)S(1)}, u32[]{:S(2)}, u32[]{:S(2)}) collective-permute-start(s16[520,128]{1,0:T(8,128)(2,1)S(1)} %get-tuple-element.44), channel_id=1, source_target_pairs={{0,3},{1,2},{2,1},{3,0},{4,7},{5,6},{6,5},{7,4},{8,11},{9,10},{10,... | collective-permute-start | bytes 399368 | tf_op jit(solution)/shard_map/ppermute | solution.py:224
  29.3 4.4 %collective-permute-done.1.refs_2_ = bf16[128,768]{1,0:T(8,128)(2,1)S(1)} collective-permute-done((bf16[128,768]{1,0:T(8,128)(2,1)S(1)}, bf16[128,768]{1,0:T(8,128)(2,1)S(1)}, u32[]{:S(2)}, u32[]{:S(2)}) %collective-permute-start.1) | collective-permute-done | bytes 196640 | tf_op jit(solution)/shard_map/ppermute | solution.py:224
  33.7 11.5 %collective-permute-start.18 = (bf16[128,256]{1,0:T(8,128)(2,1)S(1)}, bf16[128,256]{1,0:T(8,128)(2,1)S(1)}, u32[]{:S(2)}, u32[]{:S(2)}) collective-permute-start(bf16[128,256]{1,0:T(8,128)(2,1)S(1)} %get-tuple-element.57), channel_id=1, source_target_pairs={{0,2},{1,3},{2,0},{3,1},{4,6},{5,7},{6,4},{7,5},{8,10},{9,11},{10,... | collective-permute-start | bytes 196616 | tf_op jit(solution)/shard_map/ppermute | solution.py:224
  45.2 1.3 %collective-permute-start.19 = (bf16[128,256]{1,0:T(8,128)(2,1)S(1)}, bf16[128,256]{1,0:T(8,128)(2,1)S(1)}, u32[]{:S(2)}, u32[]{:S(2)}) collective-permute-start(bf16[128,256]{1,0:T(8,128)(2,1)S(1)} %get-tuple-element.58), channel_id=1, source_target_pairs={{0,3},{1,2},{2,1},{3,0},{4,7},{5,6},{6,5},{7,4},{8,11},{9,10},{10,... | collective-permute-start | bytes 196616 | tf_op jit(solution)/shard_map/ppermute | solution.py:224
  46.6 0.6 collective-permute-done.8.refs_6_
  47.2 1.6 %shard_map.68 = (f32[128,256]{1,0:T(8,128)S(1)}, s16[264,128]{1,0:T(8,128)(2,1)S(1)}, s16[264,128]{1,0:T(8,128)(2,1)S(1)}, s16[264,128]{1,0:T(8,128)(2,1)S(1)}) custom-call(bf16[128,768]{1,0:T(8,128)(2,1)S(1)} %get-tuple-element.37.refs_0_, bf16[128,768]{1,0:T(8,128)(2,1)S(1)} %collective-permute-done.refs_1_, ...), custom_call_target="tpu_custom_call" | custom-call | flops 536870912 | bytes 1 | tf_op jit(solution)/shard_map/pallas_call | solution.py:268
  48.8 5.6 %collective-permute-start.10 = (s16[264,128]{1,0:T(8,128)(2,1)S(1)}, s16[264,128]{1,0:T(8,128)(2,1)S(1)}, u32[]{:S(2)}, u32[]{:S(2)}) collective-permute-start(s16[264,128]{1,0:T(8,128)(2,1)S(1)} %get-tuple-element.46), channel_id=1, source_target_pairs={{0,1},{1,0},{2,3},{3,2},{4,5},{5,4},{6,7},{7,6},{8,9},{9,8},{10,11... | collective-permute-start | bytes 202760 | tf_op jit(solution)/shard_map/ppermute | solution.py:224
  54.4 1.1 %collective-permute-start.11 = (s16[264,128]{1,0:T(8,128)(2,1)S(1)}, s16[264,128]{1,0:T(8,128)(2,1)S(1)}, u32[]{:S(2)}, u32[]{:S(2)}) collective-permute-start(s16[264,128]{1,0:T(8,128)(2,1)S(1)} %get-tuple-element.47), channel_id=1, source_target_pairs={{0,2},{1,3},{2,0},{3,1},{4,6},{5,7},{6,4},{7,5},{8,10},{9,11},{10,... | collective-permute-start | bytes 202760 | tf_op jit(solution)/shard_map/ppermute | solution.py:224
  55.5 1.4 %collective-permute-start.12 = (s16[264,128]{1,0:T(8,128)(2,1)S(1)}, s16[264,128]{1,0:T(8,128)(2,1)S(1)}, u32[]{:S(2)}, u32[]{:S(2)}) collective-permute-start(s16[264,128]{1,0:T(8,128)(2,1)S(1)} %get-tuple-element.48), channel_id=1, source_target_pairs={{0,3},{1,2},{2,1},{3,0},{4,7},{5,6},{6,5},{7,4},{8,11},{9,10},{10,... | collective-permute-start | bytes 202760 | tf_op jit(solution)/shard_map/ppermute | solution.py:224
  56.9 1.6 %shard_map.71 = (f32[128,256]{1,0:T(8,128)S(1)}, s16[264,128]{1,0:T(8,128)(2,1)S(1)}, s16[264,128]{1,0:T(8,128)(2,1)S(1)}, s16[264,128]{1,0:T(8,128)(2,1)S(1)}) custom-call(bf16[128,768]{1,0:T(8,128)(2,1)S(1)} %get-tuple-element.37.refs_0_, bf16[128,768]{1,0:T(8,128)(2,1)S(1)} %collective-permute-done.refs_1_, ...), custom_call_target="tpu_custom_call" | custom-call | flops 536870912 | bytes 1 | tf_op jit(solution)/shard_map/pallas_call | solution.py:268
  58.5 1.1 %collective-permute-start.20 = (s16[264,128]{1,0:T(8,128)(2,1)S(1)}, s16[264,128]{1,0:T(8,128)(2,1)S(1)}, u32[]{:S(2)}, u32[]{:S(2)}) collective-permute-start(s16[264,128]{1,0:T(8,128)(2,1)S(1)} %get-tuple-element.60), channel_id=1, source_target_pairs={{0,1},{1,0},{2,3},{3,2},{4,5},{5,4},{6,7},{7,6},{8,9},{9,8},{10,11... | collective-permute-start | bytes 202760 | tf_op jit(solution)/shard_map/ppermute | solution.py:224
  59.6 2.0 %collective-permute-start.21 = (s16[264,128]{1,0:T(8,128)(2,1)S(1)}, s16[264,128]{1,0:T(8,128)(2,1)S(1)}, u32[]{:S(2)}, u32[]{:S(2)}) collective-permute-start(s16[264,128]{1,0:T(8,128)(2,1)S(1)} %get-tuple-element.61), channel_id=1, source_target_pairs={{0,2},{1,3},{2,0},{3,1},{4,6},{5,7},{6,4},{7,5},{8,10},{9,11},{10,... | collective-permute-start | bytes 202760 | tf_op jit(solution)/shard_map/ppermute | solution.py:224
  61.6 1.4 %collective-permute-start.22 = (s16[264,128]{1,0:T(8,128)(2,1)S(1)}, s16[264,128]{1,0:T(8,128)(2,1)S(1)}, u32[]{:S(2)}, u32[]{:S(2)}) collective-permute-start(s16[264,128]{1,0:T(8,128)(2,1)S(1)} %get-tuple-element.62), channel_id=1, source_target_pairs={{0,3},{1,2},{2,1},{3,0},{4,7},{5,6},{6,5},{7,4},{8,11},{9,10},{10,... | collective-permute-start | bytes 202760 | tf_op jit(solution)/shard_map/ppermute | solution.py:224
  63.0 0.3 shard_map.69
  63.3 3.1 %collective-permute-done.21.rest_2_ = s16[264,128]{1,0:T(8,128)(2,1)S(1)} collective-permute-done((s16[264,128]{1,0:T(8,128)(2,1)S(1)}, s16[264,128]{1,0:T(8,128)(2,1)S(1)}, u32[]{:S(2)}, u32[]{:S(2)}) %collective-permute-start.21) | collective-permute-done | bytes 67616 | tf_op jit(solution)/shard_map/ppermute | solution.py:224
  66.4 1.4 %collective-permute-done.22.rest_3_ = s16[264,128]{1,0:T(8,128)(2,1)S(1)} collective-permute-done((s16[264,128]{1,0:T(8,128)(2,1)S(1)}, s16[264,128]{1,0:T(8,128)(2,1)S(1)}, u32[]{:S(2)}, u32[]{:S(2)}) %collective-permute-start.22) | collective-permute-done | bytes 67616 | tf_op jit(solution)/shard_map/ppermute | solution.py:224
  67.7 0.3 shard_map.72
  68.1 0.2 shard_map.70
  68.3 1.6 %collective-permute-start.14 = (s16[264,128]{1,0:T(8,128)(2,1)S(1)}, s16[264,128]{1,0:T(8,128)(2,1)S(1)}, u32[]{:S(2)}, u32[]{:S(2)}) collective-permute-start(s16[264,128]{1,0:T(8,128)(2,1)S(1)} %get-tuple-element.52), channel_id=1, source_target_pairs={{0,8},{4,12},{8,0},{12,4},{16,24},{20,28},{24,16},{28,20},{1,9},{5... | collective-permute-start | bytes 202760 | tf_op jit(solution)/shard_map/ppermute | solution.py:292
  69.9 0.7 collective-permute-start.15
  70.6 1.2 %collective-permute-start.16 = (s16[264,128]{1,0:T(8,128)(2,1)S(1)}, s16[264,128]{1,0:T(8,128)(2,1)S(1)}, u32[]{:S(2)}, u32[]{:S(2)}) collective-permute-start(s16[264,128]{1,0:T(8,128)(2,1)S(1)} %get-tuple-element.54), channel_id=1, source_target_pairs={{0,24},{4,28},{8,16},{12,20},{16,8},{20,12},{24,0},{28,4},{1,25},{... | collective-permute-start | bytes 202760 | tf_op jit(solution)/shard_map/ppermute | solution.py:292
  71.9 0.2 shard_map.73
  72.1 1.6 %collective-permute-start.24 = (s16[264,128]{1,0:T(8,128)(2,1)S(1)}, s16[264,128]{1,0:T(8,128)(2,1)S(1)}, u32[]{:S(2)}, u32[]{:S(2)}) collective-permute-start(s16[264,128]{1,0:T(8,128)(2,1)S(1)} %get-tuple-element.66), channel_id=1, source_target_pairs={{0,8},{4,12},{8,0},{12,4},{16,24},{20,28},{24,16},{28,20},{1,9},{5... | collective-permute-start | bytes 202760 | tf_op jit(solution)/shard_map/ppermute | solution.py:292
  73.7 0.7 collective-permute-start.25
  74.4 1.2 %collective-permute-start.26 = (s16[264,128]{1,0:T(8,128)(2,1)S(1)}, s16[264,128]{1,0:T(8,128)(2,1)S(1)}, u32[]{:S(2)}, u32[]{:S(2)}) collective-permute-start(s16[264,128]{1,0:T(8,128)(2,1)S(1)} %get-tuple-element.68), channel_id=1, source_target_pairs={{0,24},{4,28},{8,16},{12,20},{16,8},{20,12},{24,0},{28,4},{1,25},{... | collective-permute-start | bytes 202760 | tf_op jit(solution)/shard_map/ppermute | solution.py:292
  75.6 0.7 collective-permute-done.16.refs_3_
  76.3 0.5 collective-permute-done.24.refs_5_
  76.8 1.8 %collective-permute-done.25.refs_6_ = s16[264,128]{1,0:T(8,128)(2,1)S(1)} collective-permute-done((s16[264,128]{1,0:T(8,128)(2,1)S(1)}, s16[264,128]{1,0:T(8,128)(2,1)S(1)}, u32[]{:S(2)}, u32[]{:S(2)}) %collective-permute-start.25) | collective-permute-done | bytes 67616 | tf_op jit(solution)/shard_map/ppermute | solution.py:292
  78.6 1.0 %collective-permute-done.26.refs_7_ = s16[264,128]{1,0:T(8,128)(2,1)S(1)} collective-permute-done((s16[264,128]{1,0:T(8,128)(2,1)S(1)}, s16[264,128]{1,0:T(8,128)(2,1)S(1)}, u32[]{:S(2)}, u32[]{:S(2)}) %collective-permute-start.26) | collective-permute-done | bytes 67616 | tf_op jit(solution)/shard_map/ppermute | solution.py:292
  79.6 0.9 %shard_map.74 = f32[128,512]{1,0:T(8,128)} custom-call(f32[128,256]{1,0:T(8,128)S(1)} %get-tuple-element.51.refs_0_, s16[264,128]{1,0:T(8,128)(2,1)S(1)} %collective-permute-done.14.refs_1_, s16[264,128]{1,0:T(8,128)(2,1)S(1)} %collective-permute-done.15.refs_2_, s16[264,128]{1,0:T(8,128)(2,1)S(1)} %collective-permute-done.16.refs_3_, ...), custom_call_target="tpu_custom_call" | custom-call | flops 1 | bytes 1 | tf_op jit(solution)/shard_map/pallas_call | solution.py:293
  (27 shorter events, 0.4 us)
Async XLA Ops:
  0.0 0.9 %copy-start = (f32[1,128,512]{2,1,0:T(8,128)S(1)}, f32[1,128,512]{2,1,0:T(8,128)}, u32[]{:S(2)}) copy-start(f32[1,128,512]{2,1,0:T(8,128)} %param.6) | copy-start | bytes 786436
  1.1 7.9 %collective-permute-start.5 = (s16[520,128]{1,0:T(8,128)(2,1)S(1)}, s16[520,128]{1,0:T(8,128)(2,1)S(1)}, u32[]{:S(2)}, u32[]{:S(2)}) collective-permute-start(s16[520,128]{1,0:T(8,128)(2,1)S(1)} %shard_map.65.rest_0_), channel_id=1, source_target_pairs={{0,24},{4,28},{8,16},{12,20},{16,8},{20,12},{24,0},{28,4},{1,25},{... | collective-permute-start | bytes 399368 | tf_op jit(solution)/shard_map/ppermute | solution.py:250
  5.1 6.4 %collective-permute-start.4 = (s16[520,128]{1,0:T(8,128)(2,1)S(1)}, s16[520,128]{1,0:T(8,128)(2,1)S(1)}, u32[]{:S(2)}, u32[]{:S(2)}) collective-permute-start(s16[520,128]{1,0:T(8,128)(2,1)S(1)} %shard_map.65.rest_0_), channel_id=1, source_target_pairs={{0,16},{4,20},{8,24},{12,28},{16,0},{20,4},{24,8},{28,12},{1,17},{... | collective-permute-start | bytes 399368 | tf_op jit(solution)/shard_map/ppermute | solution.py:250
  5.6 6.1 %collective-permute-start.3 = (s16[520,128]{1,0:T(8,128)(2,1)S(1)}, s16[520,128]{1,0:T(8,128)(2,1)S(1)}, u32[]{:S(2)}, u32[]{:S(2)}) collective-permute-start(s16[520,128]{1,0:T(8,128)(2,1)S(1)} %shard_map.65.rest_0_), channel_id=1, source_target_pairs={{0,8},{4,12},{8,0},{12,4},{16,24},{20,28},{24,16},{28,20},{1,9},{5... | collective-permute-start | bytes 399368 | tf_op jit(solution)/shard_map/ppermute | solution.py:250
  11.7 0.7 copy-start.1
  12.6 6.7 %collective-permute-start.6 = (s16[4,520,128]{2,1,0:T(8,128)(2,1)S(1)}, s16[4,520,128]{2,1,0:T(8,128)(2,1)S(1)}, u32[]{:S(2)}, u32[]{:S(2)}) collective-permute-start(s16[4,520,128]{2,1,0:T(8,128)(2,1)S(1)} %shard_map.66), channel_id=1, source_target_pairs={{0,4},{4,0},{8,12},{12,8},{16,20},{20,16},{24,28},{28,24},{1,5},{5... | collective-permute-start | bytes 1597448 | tf_op jit(solution)/shard_map/ppermute | solution.py:256
  12.7 0.7 copy-start.4
  13.4 6.0 %copy-start.2 = (s32[32]{0:T(128)S(1)}, s32[32]{0:T(128)}, u32[]{:S(2)}) copy-start(s32[32]{0:T(128)} %param.9) | copy-start | bytes 388
  14.9 48.1 %copy-start.3 = (s32[32,1]{0,1:T(1,128)S(1)}, s32[32,1]{0,1:T(1,128)}, u32[]{:S(2)}) copy-start(s32[32,1]{0,1:T(1,128)} %param.10) | copy-start | bytes 388
  14.9 11.6 %collective-permute-start = (bf16[128,768]{1,0:T(8,128)(2,1)S(1)}, bf16[128,768]{1,0:T(8,128)(2,1)S(1)}, u32[]{:S(2)}, u32[]{:S(2)}) collective-permute-start(bf16[128,768]{1,0:T(8,128)(2,1)S(1)} %get-tuple-element.38), channel_id=1, source_target_pairs={{0,1},{1,0},{2,3},{3,2},{4,5},{5,4},{6,7},{7,6},{8,9},{9,8},{10,11... | collective-permute-start | bytes 589832 | tf_op jit(solution)/shard_map/ppermute | solution.py:224
  16.5 17.2 %collective-permute-start.1 = (bf16[128,768]{1,0:T(8,128)(2,1)S(1)}, bf16[128,768]{1,0:T(8,128)(2,1)S(1)}, u32[]{:S(2)}, u32[]{:S(2)}) collective-permute-start(bf16[128,768]{1,0:T(8,128)(2,1)S(1)} %get-tuple-element.39), channel_id=1, source_target_pairs={{0,2},{1,3},{2,0},{3,1},{4,6},{5,7},{6,4},{7,5},{8,10},{9,11},{10,... | collective-permute-start | bytes 589832 | tf_op jit(solution)/shard_map/ppermute | solution.py:224
  19.1 14.6 %collective-permute-start.2 = (bf16[128,768]{1,0:T(8,128)(2,1)S(1)}, bf16[128,768]{1,0:T(8,128)(2,1)S(1)}, u32[]{:S(2)}, u32[]{:S(2)}) collective-permute-start(bf16[128,768]{1,0:T(8,128)(2,1)S(1)} %get-tuple-element.40), channel_id=1, source_target_pairs={{0,3},{1,2},{2,1},{3,0},{4,7},{5,6},{6,5},{7,4},{8,11},{9,10},{10,... | collective-permute-start | bytes 589832 | tf_op jit(solution)/shard_map/ppermute | solution.py:224
  19.6 25.6 %collective-permute-start.7 = (s16[520,128]{1,0:T(8,128)(2,1)S(1)}, s16[520,128]{1,0:T(8,128)(2,1)S(1)}, u32[]{:S(2)}, u32[]{:S(2)}) collective-permute-start(s16[520,128]{1,0:T(8,128)(2,1)S(1)} %get-tuple-element.42), channel_id=1, source_target_pairs={{0,1},{1,0},{2,3},{3,2},{4,5},{5,4},{6,7},{7,6},{8,9},{9,8},{10,11... | collective-permute-start | bytes 399368 | tf_op jit(solution)/shard_map/ppermute | solution.py:224
  20.4 26.8 %collective-permute-start.8 = (s16[520,128]{1,0:T(8,128)(2,1)S(1)}, s16[520,128]{1,0:T(8,128)(2,1)S(1)}, u32[]{:S(2)}, u32[]{:S(2)}) collective-permute-start(s16[520,128]{1,0:T(8,128)(2,1)S(1)} %get-tuple-element.43), channel_id=1, source_target_pairs={{0,2},{1,3},{2,0},{3,1},{4,6},{5,7},{6,4},{7,5},{8,10},{9,11},{10,... | collective-permute-start | bytes 399368 | tf_op jit(solution)/shard_map/ppermute | solution.py:224
  26.5 20.7 %collective-permute-start.9 = (s16[520,128]{1,0:T(8,128)(2,1)S(1)}, s16[520,128]{1,0:T(8,128)(2,1)S(1)}, u32[]{:S(2)}, u32[]{:S(2)}) collective-permute-start(s16[520,128]{1,0:T(8,128)(2,1)S(1)} %get-tuple-element.44), channel_id=1, source_target_pairs={{0,3},{1,2},{2,1},{3,0},{4,7},{5,6},{6,5},{7,4},{8,11},{9,10},{10,... | collective-permute-start | bytes 399368 | tf_op jit(solution)/shard_map/ppermute | solution.py:224
  33.7 21.8 %collective-permute-start.17 = (bf16[128,256]{1,0:T(8,128)(2,1)S(1)}, bf16[128,256]{1,0:T(8,128)(2,1)S(1)}, u32[]{:S(2)}, u32[]{:S(2)}) collective-permute-start(bf16[128,256]{1,0:T(8,128)(2,1)S(1)} %get-tuple-element.56), channel_id=1, source_target_pairs={{0,1},{1,0},{2,3},{3,2},{4,5},{5,4},{6,7},{7,6},{8,9},{9,8},{10,11... | collective-permute-start | bytes 196616 | tf_op jit(solution)/shard_map/ppermute | solution.py:224
  33.7 23.2 %collective-permute-start.18 = (bf16[128,256]{1,0:T(8,128)(2,1)S(1)}, bf16[128,256]{1,0:T(8,128)(2,1)S(1)}, u32[]{:S(2)}, u32[]{:S(2)}) collective-permute-start(bf16[128,256]{1,0:T(8,128)(2,1)S(1)} %get-tuple-element.57), channel_id=1, source_target_pairs={{0,2},{1,3},{2,0},{3,1},{4,6},{5,7},{6,4},{7,5},{8,10},{9,11},{10,... | collective-permute-start | bytes 196616 | tf_op jit(solution)/shard_map/ppermute | solution.py:224
  45.2 11.7 %collective-permute-start.19 = (bf16[128,256]{1,0:T(8,128)(2,1)S(1)}, bf16[128,256]{1,0:T(8,128)(2,1)S(1)}, u32[]{:S(2)}, u32[]{:S(2)}) collective-permute-start(bf16[128,256]{1,0:T(8,128)(2,1)S(1)} %get-tuple-element.58), channel_id=1, source_target_pairs={{0,3},{1,2},{2,1},{3,0},{4,7},{5,6},{6,5},{7,4},{8,11},{9,10},{10,... | collective-permute-start | bytes 196616 | tf_op jit(solution)/shard_map/ppermute | solution.py:224
  48.8 12.8 %collective-permute-start.10 = (s16[264,128]{1,0:T(8,128)(2,1)S(1)}, s16[264,128]{1,0:T(8,128)(2,1)S(1)}, u32[]{:S(2)}, u32[]{:S(2)}) collective-permute-start(s16[264,128]{1,0:T(8,128)(2,1)S(1)} %get-tuple-element.46), channel_id=1, source_target_pairs={{0,1},{1,0},{2,3},{3,2},{4,5},{5,4},{6,7},{7,6},{8,9},{9,8},{10,11... | collective-permute-start | bytes 202760 | tf_op jit(solution)/shard_map/ppermute | solution.py:224
  54.4 8.6 %collective-permute-start.11 = (s16[264,128]{1,0:T(8,128)(2,1)S(1)}, s16[264,128]{1,0:T(8,128)(2,1)S(1)}, u32[]{:S(2)}, u32[]{:S(2)}) collective-permute-start(s16[264,128]{1,0:T(8,128)(2,1)S(1)} %get-tuple-element.47), channel_id=1, source_target_pairs={{0,2},{1,3},{2,0},{3,1},{4,6},{5,7},{6,4},{7,5},{8,10},{9,11},{10,... | collective-permute-start | bytes 202760 | tf_op jit(solution)/shard_map/ppermute | solution.py:224
  55.5 7.5 %collective-permute-start.12 = (s16[264,128]{1,0:T(8,128)(2,1)S(1)}, s16[264,128]{1,0:T(8,128)(2,1)S(1)}, u32[]{:S(2)}, u32[]{:S(2)}) collective-permute-start(s16[264,128]{1,0:T(8,128)(2,1)S(1)} %get-tuple-element.48), channel_id=1, source_target_pairs={{0,3},{1,2},{2,1},{3,0},{4,7},{5,6},{6,5},{7,4},{8,11},{9,10},{10,... | collective-permute-start | bytes 202760 | tf_op jit(solution)/shard_map/ppermute | solution.py:224
  58.5 4.8 %collective-permute-start.20 = (s16[264,128]{1,0:T(8,128)(2,1)S(1)}, s16[264,128]{1,0:T(8,128)(2,1)S(1)}, u32[]{:S(2)}, u32[]{:S(2)}) collective-permute-start(s16[264,128]{1,0:T(8,128)(2,1)S(1)} %get-tuple-element.60), channel_id=1, source_target_pairs={{0,1},{1,0},{2,3},{3,2},{4,5},{5,4},{6,7},{7,6},{8,9},{9,8},{10,11... | collective-permute-start | bytes 202760 | tf_op jit(solution)/shard_map/ppermute | solution.py:224
  59.6 6.8 %collective-permute-start.21 = (s16[264,128]{1,0:T(8,128)(2,1)S(1)}, s16[264,128]{1,0:T(8,128)(2,1)S(1)}, u32[]{:S(2)}, u32[]{:S(2)}) collective-permute-start(s16[264,128]{1,0:T(8,128)(2,1)S(1)} %get-tuple-element.61), channel_id=1, source_target_pairs={{0,2},{1,3},{2,0},{3,1},{4,6},{5,7},{6,4},{7,5},{8,10},{9,11},{10,... | collective-permute-start | bytes 202760 | tf_op jit(solution)/shard_map/ppermute | solution.py:224
  61.6 6.2 %collective-permute-start.22 = (s16[264,128]{1,0:T(8,128)(2,1)S(1)}, s16[264,128]{1,0:T(8,128)(2,1)S(1)}, u32[]{:S(2)}, u32[]{:S(2)}) collective-permute-start(s16[264,128]{1,0:T(8,128)(2,1)S(1)} %get-tuple-element.62), channel_id=1, source_target_pairs={{0,3},{1,2},{2,1},{3,0},{4,7},{5,6},{6,5},{7,4},{8,11},{9,10},{10,... | collective-permute-start | bytes 202760 | tf_op jit(solution)/shard_map/ppermute | solution.py:224
  63.2 4.9 %collective-permute-start.13 = (f32[4,128,256]{2,1,0:T(8,128)S(1)}, f32[4,128,256]{2,1,0:T(8,128)S(1)}, u32[]{:S(2)}, u32[]{:S(2)}) collective-permute-start(f32[4,128,256]{2,1,0:T(8,128)S(1)} %get-tuple-element.50), channel_id=1, source_target_pairs={{0,4},{4,0},{8,12},{12,8},{16,20},{20,16},{24,28},{28,24},{1,5},{5... | collective-permute-start | bytes 1572872 | tf_op jit(solution)/shard_map/ppermute | solution.py:287
  68.0 3.9 %collective-permute-start.23 = (f32[4,128,256]{2,1,0:T(8,128)S(1)}, f32[4,128,256]{2,1,0:T(8,128)S(1)}, u32[]{:S(2)}, u32[]{:S(2)}) collective-permute-start(f32[4,128,256]{2,1,0:T(8,128)S(1)} %get-tuple-element.64), channel_id=1, source_target_pairs={{0,4},{4,0},{8,12},{12,8},{16,20},{20,16},{24,28},{28,24},{1,5},{5... | collective-permute-start | bytes 1572872 | tf_op jit(solution)/shard_map/ppermute | solution.py:287
  68.3 6.1 %collective-permute-start.14 = (s16[264,128]{1,0:T(8,128)(2,1)S(1)}, s16[264,128]{1,0:T(8,128)(2,1)S(1)}, u32[]{:S(2)}, u32[]{:S(2)}) collective-permute-start(s16[264,128]{1,0:T(8,128)(2,1)S(1)} %get-tuple-element.52), channel_id=1, source_target_pairs={{0,8},{4,12},{8,0},{12,4},{16,24},{20,28},{24,16},{28,20},{1,9},{5... | collective-permute-start | bytes 202760 | tf_op jit(solution)/shard_map/ppermute | solution.py:292
  69.9 5.7 %collective-permute-start.15 = (s16[264,128]{1,0:T(8,128)(2,1)S(1)}, s16[264,128]{1,0:T(8,128)(2,1)S(1)}, u32[]{:S(2)}, u32[]{:S(2)}) collective-permute-start(s16[264,128]{1,0:T(8,128)(2,1)S(1)} %get-tuple-element.53), channel_id=1, source_target_pairs={{0,16},{4,20},{8,24},{12,28},{16,0},{20,4},{24,8},{28,12},{1,17},{... | collective-permute-start | bytes 202760 | tf_op jit(solution)/shard_map/ppermute | solution.py:292
  70.6 5.7 %collective-permute-start.16 = (s16[264,128]{1,0:T(8,128)(2,1)S(1)}, s16[264,128]{1,0:T(8,128)(2,1)S(1)}, u32[]{:S(2)}, u32[]{:S(2)}) collective-permute-start(s16[264,128]{1,0:T(8,128)(2,1)S(1)} %get-tuple-element.54), channel_id=1, source_target_pairs={{0,24},{4,28},{8,16},{12,20},{16,8},{20,12},{24,0},{28,4},{1,25},{... | collective-permute-start | bytes 202760 | tf_op jit(solution)/shard_map/ppermute | solution.py:292
  72.1 4.7 %collective-permute-start.24 = (s16[264,128]{1,0:T(8,128)(2,1)S(1)}, s16[264,128]{1,0:T(8,128)(2,1)S(1)}, u32[]{:S(2)}, u32[]{:S(2)}) collective-permute-start(s16[264,128]{1,0:T(8,128)(2,1)S(1)} %get-tuple-element.66), channel_id=1, source_target_pairs={{0,8},{4,12},{8,0},{12,4},{16,24},{20,28},{24,16},{28,20},{1,9},{5... | collective-permute-start | bytes 202760 | tf_op jit(solution)/shard_map/ppermute | solution.py:292
  73.7 4.9 %collective-permute-start.25 = (s16[264,128]{1,0:T(8,128)(2,1)S(1)}, s16[264,128]{1,0:T(8,128)(2,1)S(1)}, u32[]{:S(2)}, u32[]{:S(2)}) collective-permute-start(s16[264,128]{1,0:T(8,128)(2,1)S(1)} %get-tuple-element.67), channel_id=1, source_target_pairs={{0,16},{4,20},{8,24},{12,28},{16,0},{20,4},{24,8},{28,12},{1,17},{... | collective-permute-start | bytes 202760 | tf_op jit(solution)/shard_map/ppermute | solution.py:292
  74.4 5.2 %collective-permute-start.26 = (s16[264,128]{1,0:T(8,128)(2,1)S(1)}, s16[264,128]{1,0:T(8,128)(2,1)S(1)}, u32[]{:S(2)}, u32[]{:S(2)}) collective-permute-start(s16[264,128]{1,0:T(8,128)(2,1)S(1)} %get-tuple-element.68), channel_id=1, source_target_pairs={{0,24},{4,28},{8,16},{12,20},{16,8},{20,12},{24,0},{28,4},{1,25},{... | collective-permute-start | bytes 202760 | tf_op jit(solution)/shard_map/ppermute | solution.py:292

commit v7 on v6

--- a/solution.py
+++ b/solution.py
@@ -102,38 +102,47 @@
     encode(psi_ref[...], code, True)
 
 
-def partner_psi_kernel(base, sec, count, chips, in_ref, *rest):
-    held, out = rest[:chips], rest[chips]
-    start = base()
+def partner_psi_kernel(base, sec, me, count, chips, in_ref, *rest):
+    held, out = rest[: 2 * chips], rest[2 * chips]
+    start, mine, near = base(), me(), count // 2
     chip, core = sec() // 2, lax.rem(sec(), 2)
-    sources = [entry(in_ref, start + slot) for slot in range(count)]
-    for slot, source in enumerate(sources):
-        for step in range(chips):
-            @pl.when((source // 2 == chip ^ step) & (lax.rem(source, 2) == core))
+    sources = [entry(in_ref, start + (mine ^ step)) for step in range(near)]
+    for step, source in enumerate(sources):
+        for hop in range(chips):
+            @pl.when((source // 2 == chip ^ hop) & (lax.rem(source, 2) == core))
             def _():
-                out[slot] = held[step][...]
+                out[step] = held[hop][...]
+                out[near + step] = held[chips + hop][...]
 
 
 def own_psi_kernel(base, sec, me, count, chips, in_ref, *rest):
-    held, paired, outs = rest[:chips], rest[chips], rest[chips + 1 :]
-    start, mine = base(), me()
+    held, paired, outs = rest[: 2 * chips], rest[2 * chips], rest[2 * chips + 1 :]
+    start, mine, near = base(), me(), count // 2
     chip, core = sec() // 2, lax.rem(sec(), 2)
-    slots = [mine ^ step for step in range(count)]
-    sources = [entry(in_ref, start + slot) for slot in slots]
-    for step, (slot, source) in enumerate(zip(slots, sources)):
+    sources = [entry(in_ref, start + (mine ^ step)) for step in range(near)]
+    for step, source in enumerate(sources):
         same = lax.rem(source, 2) == core
         for hop in range(chips):
             @pl.when((source // 2 == chip ^ hop) & same)
             def _():
-                outs[step][...] = held[hop][...]
+                outs[step][0] = held[hop][...]
+                outs[step][1] = held[chips + hop][...]
 
         @pl.when(jnp.logical_not(same))
         def _():
-            outs[step][...] = paired[slot]
+            outs[step][0] = paired[step]
+            outs[step][1] = paired[near + step]
 
 
 def task_kernel(me, count, half, *refs):
-    envs, psis, lates, outs = refs[:count], refs[count : 2 * count], refs[2 * count : -3 - count], refs[-3 - count : -3]
+    near = count // 2
+    envs, psis, lates, outs = (
+        refs[:count],
+        refs[count : count + near],
+        refs[count + near : -3 - count],
+        refs[-3 - count : -3],
+    )
+    psis = [both.at[0] for both in psis] + [both.at[1] for both in psis]
     high, low, right = refs[-3:]
     rows, width = outs[0].shape
     cols = high.shape[1]
@@ -161,8 +170,8 @@
             encode(part, outs[step], False)
 
 
-def combine_kernel(base, sec, me, count, target_ref, *rest):
-    parts, keep, send = rest[:count], rest[count], rest[count + 1]
+def combine_kernel(base, sec, me, count, chips, target_ref, *rest):
+    parts, (keep, code, send) = rest[:count], rest[count:]
     start, mine = base(), me()
     chip, core = sec() // 2, lax.rem(sec(), 2)
     keep[...] = jnp.zeros(keep.shape, jnp.float32)
@@ -181,24 +190,43 @@
         def _():
             send[hop] = send[hop] + part
 
+    for hop in range(chips):
+        encode(send[hop], code.at[hop], False)
+
 
 def join_kernel(chips, keep, other, *outs):
     for hop in range(chips):
-        total = keep[hop] + other[hop]
+        total = keep[hop] + decode(other.at[hop], *keep.shape[1:])
         if hop == 0:
             outs[0][...] = total
         else:
             encode(total, outs[hop], False)
 
 
-def finish_kernel(chips, *refs):
-    width = refs[0].shape[1]
-    for half in range(HALVES):
-        mine = refs[half * chips : (half + 1) * chips]
-        total = mine[0][...]
-        for hop in range(1, chips):
-            total = total + decode(mine[hop], *mine[0].shape)
-        refs[-1][:, half * width : (half + 1) * width] = total
+def halve_kernel(first, second, keep, send):
+    left = keep.shape[0]
+    for slot in range(2 * left):
+        if len(second.shape) == len(first.shape) and second.dtype == first.dtype:
+            total = first[slot] + second[slot]
+        else:
+            total = first[slot] + decode(second.at[slot], *first.shape[1:])
+        if slot < left:
+            keep[slot] = total
+        else:
+            encode(total, send.at[slot - left], False)
+
+
+def finish_kernel(counts, *refs):
+    refs, out = list(refs[:-1]), refs[-1]
+    place = 0
+    for many in counts:
+        mine, refs = refs[:many], refs[many:]
+        rows, width = mine[0].shape[-2:]
+        total = mine[0][...].reshape(rows, width)
+        for code in mine[1:]:
+            total = total + decode(code.at[0] if len(code.shape) > 2 else code, rows, width)
+        out[:, place : place + width] = total
+        place += width
 
 
 def body(wavefunction, left_env, right_env, task_in, task_out, task_term):
@@ -247,19 +275,24 @@
         envs = exchange(picked[:count])
         if held is None:
             psi = call(encode_kernel, code, [VMEM])(wavefunction[0])
-            held = [psi] + [lax.ppermute(psi, "sec", across(hop)) for hop in range(1, chips)]
+            far = lax.ppermute(psi, "env", along(count // 2))
+            held = []
+            for rows_of in (psi, far):
+                held += [rows_of] + [
+                    lax.ppermute(rows_of, "sec", across(hop)) for hop in range(1, chips)
+                ]
         sent = call(
-            functools.partial(partner_psi_kernel, partner_base, sec, count, chips),
+            functools.partial(partner_psi_kernel, partner_base, sec, me, count, chips),
             jax.ShapeDtypeStruct((count, *code.shape), code.dtype),
-            [VMEM] * (chips + 1),
+            [VMEM] * (2 * chips + 1),
         )(task_in[None], *held)
         paired = lax.ppermute(sent, "sec", pair)
         psis = call(
             functools.partial(own_psi_kernel, base, sec, me, count, chips),
-            [code] * count,
-            [VMEM] * (chips + 2),
+            [jax.ShapeDtypeStruct((2, *code.shape), code.dtype)] * (count // 2),
+            [VMEM] * (2 * chips + 2),
         )(task_in[None], *held, paired)
-        psis = exchange(psis)
+        psis = [psis[0]] + [lax.ppermute(psis[s], "env", along(s)) for s in range(1, count // 2)]
         lates = [exchange(picked[half * count : (half + 1) * count]) for half in range(1, HALVES)]
         full = count * rows
         halves = []
@@ -268,29 +301,50 @@
             parts = call(
                 functools.partial(task_kernel, me, count, half),
                 [part] + [piece] * (count - 1),
-                [VMEM] * (2 * count + len(extra)),
+                [VMEM] * (count + count // 2 + len(extra)),
                 [pltpu.VMEM((full, cols), bf16)] * 2 + [pltpu.VMEM((full, width), bf16)],
                 flops=8 * full * full * width,
             )(*envs, *psis, *extra)
             halves.append(exchange(parts))
         for half, mine in enumerate(halves):
             kept, sent = call(
-                functools.partial(combine_kernel, base, sec, me, count),
-                [stack, stack],
+                functools.partial(combine_kernel, base, sec, me, count, chips),
+                [stack, jax.ShapeDtypeStruct((chips, *piece.shape), piece.dtype)],
                 [VMEM] * (count + 1),
+                [pltpu.VMEM(stack.shape, f32)],
             )(targets, *mine)
             if turn:
-                kept, sent = keeps[half] + kept, sends[half] + sent
+                raise NotImplementedError
             keeps[half], sends[half] = kept, sent
-    sums = []
+    waves = []
     for half in range(HALVES):
         other = lax.ppermute(sends[half], "sec", pair)
+        if half < HALVES - 1:
+            bit, kept = chips // 2, keeps[half]
+            while bit:
+                kept, sent = call(
+                    halve_kernel,
+                    [
+                        jax.ShapeDtypeStruct((bit, rows, width), f32),
+                        jax.ShapeDtypeStruct((bit, *piece.shape), piece.dtype),
+                    ],
+                    [VMEM] * 2,
+                )(kept, other)
+                other = lax.ppermute(sent, "sec", across(bit))
+                bit //= 2
+            waves.append([kept, other])
+            continue
         mine = call(
             functools.partial(join_kernel, chips), [part] + [piece] * (chips - 1), [VMEM] * 2
         )(keeps[half], other)
-        sums += [mine[0]]
-        sums += [lax.ppermute(mine[hop], "sec", across(hop)) for hop in range(1, chips)]
-    total = call(functools.partial(finish_kernel, chips), block, [VMEM] * (chips * HALVES))(*sums)
+        waves.append(
+            [mine[0]]
+            + [lax.ppermute(mine[hop], "sec", across(hop)) for hop in range(1, chips)]
+        )
+    inputs = [value for wave in waves for value in wave]
+    total = call(
+        functools.partial(finish_kernel, [len(wave) for wave in waves]), block, [VMEM] * len(inputs)
+    )(*inputs)
     return total[None]
 
 

time: 80.6 us -> 87.7 us (1.088)
  waiting for transfers between devices: 22.1 us -> 38.7 us
  starting transfers between devices: 48.8 us -> 38.8 us
    ppermute x15 -> x12, starting transfers between devices: 36.8 us -> 19.2 us  [exchange(): got[s] = lax.ppermute(blocks[s], 'env', along(s))]
    ppermute x15 -> x12, waiting for transfers between devices: 12.1 us -> 25.1 us  [exchange(): got[s] = lax.ppermute(blocks[s], 'env', along(s))]
    ppermute x3 -> x10, starting transfers between devices: 4.63 us -> 15.9 us  [the longest x6 6.98 us: body(): lax.ppermute(rows_of, 'sec', across(hop))]
    ppermute x3 -> x10, waiting for transfers between devices: 6 us -> 10.9 us  [the longest x6 4.97 us: body(): lax.ppermute(rows_of, 'sec', across(hop))]
    ppermute x6 -> x3, starting transfers between devices: 7.11 us -> 3.55 us  [body(): lax.ppermute(mine[hop], 'sec', across(hop))]
    ppermute x6 -> x3, waiting for transfers between devices: 3.95 us -> 0.88 us  [body(): lax.ppermute(mine[hop], 'sec', across(hop))]
    ppermute x1, waiting for transfers between devices: 0.01 us -> 1.91 us  [body(): paired = lax.ppermute(sent, 'sec', pair)]
    pallas_call x5 -> x7, Pallas kernels: 1.88 us -> 2.49 us  [the longest x2 0.96 us: body(): call(functools.partial(combine_kernel, base, sec, me, count, chips), [sta...]
  transfers between devices with their start and end apart: 27 -> 28, of which waited for: 12 -> 14; matrix products, arithmetic and copies ran while one was open for 0% -> 0% of each run, Pallas kernels for 7% -> 5%
where the time goes in v7:
time: 87.7 us; the launch traced here: 87.6 us
  starting transfers between devices  38.8 us (44%)
  waiting for transfers between devices  38.7 us (44%)
  Pallas kernels  7.6 us (9%)
  local copies, waits for them, and re-layouts  2.26 us (3%)
    ppermute x12, waiting for transfers between devices, exchange(): got[s] = lax.ppermute(blocks[s], 'env', along(s))  25.1 us
    ppermute x12, starting transfers between devices, exchange(): got[s] = lax.ppermute(blocks[s], 'env', along(s))  19.2 us
    ppermute x6, starting transfers between devices, body(): lax.ppermute(rows_of, 'sec', across(hop))  6.98 us
    ppermute x6, waiting for transfers between devices, body(): lax.ppermute(rows_of, 'sec', across(hop))  4.97 us
    ppermute x1, starting transfers between devices, body(): far = lax.ppermute(psi, 'env', along(count // 2))  4.13 us
    ppermute x3, starting transfers between devices, body(): lax.ppermute(mine[hop], 'sec', across(hop))  3.55 us
    pallas_call x2, Pallas kernels, body(): call(functools.partial(task_kernel, me, count, half), [part] + [piece] *...  3.23 us
    ppermute x2, starting transfers between devices, body(): other = lax.ppermute(sent, 'sec', across(bit))  3.15 us
  transfers between devices with their start and end apart: 28, of which 14 were waited for; matrix products, arithmetic and copies ran while one was open for 0% of the time, Pallas kernels for 5%

profile of v7, /device:TPU:0, one launch (start us, length us, event | category | flops | bytes accessed | tf_op | source)
XLA Modules:
  0.0 87.6 jit_solution(2598816230923156497)
XLA Ops:
  0.0 0.9 %copy-done = f32[1,128,512]{2,1,0:T(8,128)S(1)} copy-done((f32[1,128,512]{2,1,0:T(8,128)S(1)}, f32[1,128,512]{2,1,0:T(8,128)}, u32[]{:S(2)}) %copy-start) | copy-done | bytes 262168
  1.1 4.1 %collective-permute-start.6 = (s16[520,128]{1,0:T(8,128)(2,1)S(1)}, s16[520,128]{1,0:T(8,128)(2,1)S(1)}, u32[]{:S(2)}, u32[]{:S(2)}) collective-permute-start(s16[520,128]{1,0:T(8,128)(2,1)S(1)} %shard_map.65.rest_0_), channel_id=1, source_target_pairs={{0,2},{1,3},{2,0},{3,1},{4,6},{5,7},{6,4},{7,5},{8,10},{9,11},{10,... | collective-permute-start | bytes 399368 | tf_op jit(solution)/shard_map/ppermute | solution.py:278
  5.2 2.4 %collective-permute-start.5 = (s16[520,128]{1,0:T(8,128)(2,1)S(1)}, s16[520,128]{1,0:T(8,128)(2,1)S(1)}, u32[]{:S(2)}, u32[]{:S(2)}) collective-permute-start(s16[520,128]{1,0:T(8,128)(2,1)S(1)} %shard_map.65.rest_0_), channel_id=1, source_target_pairs={{0,24},{4,28},{8,16},{12,20},{16,8},{20,12},{24,0},{28,4},{1,25},{... | collective-permute-start | bytes 399368 | tf_op jit(solution)/shard_map/ppermute | solution.py:282
  7.7 0.5 collective-permute-start.4
  8.2 0.5 collective-permute-start.3
  8.7 2.9 %collective-permute-done.6.rest_4_ = s16[520,128]{1,0:T(8,128)(2,1)S(1)} collective-permute-done((s16[520,128]{1,0:T(8,128)(2,1)S(1)}, s16[520,128]{1,0:T(8,128)(2,1)S(1)}, u32[]{:S(2)}, u32[]{:S(2)}) %collective-permute-start.6) | collective-permute-done | bytes 133152 | tf_op jit(solution)/shard_map/ppermute | solution.py:278
  11.6 2.5 %collective-permute-start.9 = (s16[520,128]{1,0:T(8,128)(2,1)S(1)}, s16[520,128]{1,0:T(8,128)(2,1)S(1)}, u32[]{:S(2)}, u32[]{:S(2)}) collective-permute-start(s16[520,128]{1,0:T(8,128)(2,1)S(1)} %collective-permute-done.6.rest_4_), channel_id=1, source_target_pairs={{0,24},{4,28},{8,16},{12,20},{16,8},{20,12},{24,0},{28,4},{1,25},{... | collective-permute-start | bytes 399368 | tf_op jit(solution)/shard_map/ppermute | solution.py:282
  14.1 0.5 collective-permute-start.8
  14.6 0.5 collective-permute-start.7
  15.1 3.3 %collective-permute-done.9.rest_7_ = s16[520,128]{1,0:T(8,128)(2,1)S(1)} collective-permute-done((s16[520,128]{1,0:T(8,128)(2,1)S(1)}, s16[520,128]{1,0:T(8,128)(2,1)S(1)}, u32[]{:S(2)}, u32[]{:S(2)}) %collective-permute-start.9) | collective-permute-done | bytes 133152 | tf_op jit(solution)/shard_map/ppermute | solution.py:282
  18.4 1.7 %collective-permute-done.8.rest_6_ = s16[520,128]{1,0:T(8,128)(2,1)S(1)} collective-permute-done((s16[520,128]{1,0:T(8,128)(2,1)S(1)}, s16[520,128]{1,0:T(8,128)(2,1)S(1)}, u32[]{:S(2)}, u32[]{:S(2)}) %collective-permute-start.8) | collective-permute-done | bytes 133152 | tf_op jit(solution)/shard_map/ppermute | solution.py:282
  20.1 0.7 copy-done.1
  21.0 1.9 %collective-permute-done.10.rest_8_ = s16[4,520,128]{2,1,0:T(8,128)(2,1)S(1)} collective-permute-done((s16[4,520,128]{2,1,0:T(8,128)(2,1)S(1)}, s16[4,520,128]{2,1,0:T(8,128)(2,1)S(1)}, u32[]{:S(2)}, u32[]{:S(2)}) %collective-permute-start.10) | collective-permute-done | bytes 532512 | tf_op jit(solution)/shard_map/ppermute | solution.py:289
  23.2 1.6 %collective-permute-start.11 = (s16[2,520,128]{2,1,0:T(8,128)(2,1)S(1)}, s16[2,520,128]{2,1,0:T(8,128)(2,1)S(1)}, u32[]{:S(2)}, u32[]{:S(2)}) collective-permute-start(s16[2,520,128]{2,1,0:T(8,128)(2,1)S(1)} %get-tuple-element.40), channel_id=1, source_target_pairs={{0,1},{1,0},{2,3},{3,2},{4,5},{5,4},{6,7},{7,6},{8,9},{9,8},{10,11... | collective-permute-start | bytes 798728 | tf_op jit(solution)/shard_map/ppermute | solution.py:295
  24.8 0.7 copy-done.3
  25.4 1.5 %shard_map.64 = (bf16[128,768]{1,0:T(8,128)(2,1)S(1)}, bf16[128,768]{1,0:T(8,128)(2,1)S(1)}, bf16[128,768]{1,0:T(8,128)(2,1)S(1)}, bf16[128,768]{1,0:T(8,128)(2,...) custom-call(s32[1,32]{1,0:T(1,128)S(1)} %bitcast.10, ...), custom_call_target="tpu_custom_call" | custom-call | flops 1 | bytes 1 | tf_op jit(solution)/shard_map/pallas_call | solution.py:268
  26.9 0.5 collective-permute-start
  27.5 3.0 %collective-permute-start.1 = (bf16[128,768]{1,0:T(8,128)(2,1)S(1)}, bf16[128,768]{1,0:T(8,128)(2,1)S(1)}, u32[]{:S(2)}, u32[]{:S(2)}) collective-permute-start(bf16[128,768]{1,0:T(8,128)(2,1)S(1)} %get-tuple-element.37), channel_id=1, source_target_pairs={{0,2},{1,3},{2,0},{3,1},{4,6},{5,7},{6,4},{7,5},{8,10},{9,11},{10,... | collective-permute-start | bytes 589832 | tf_op jit(solution)/shard_map/ppermute | solution.py:252
  30.5 1.4 %collective-permute-start.2 = (bf16[128,768]{1,0:T(8,128)(2,1)S(1)}, bf16[128,768]{1,0:T(8,128)(2,1)S(1)}, u32[]{:S(2)}, u32[]{:S(2)}) collective-permute-start(bf16[128,768]{1,0:T(8,128)(2,1)S(1)} %get-tuple-element.38), channel_id=1, source_target_pairs={{0,3},{1,2},{2,1},{3,0},{4,7},{5,6},{6,5},{7,4},{8,11},{9,10},{10,... | collective-permute-start | bytes 589832 | tf_op jit(solution)/shard_map/ppermute | solution.py:252
  31.8 8.2 %collective-permute-done.refs_1_ = bf16[128,768]{1,0:T(8,128)(2,1)S(1)} collective-permute-done((bf16[128,768]{1,0:T(8,128)(2,1)S(1)}, bf16[128,768]{1,0:T(8,128)(2,1)S(1)}, u32[]{:S(2)}, u32[]{:S(2)}) %collective-permute-start) | collective-permute-done | bytes 196640 | tf_op jit(solution)/shard_map/ppermute | solution.py:252
  40.1 6.9 %collective-permute-done.2.refs_3_ = bf16[128,768]{1,0:T(8,128)(2,1)S(1)} collective-permute-done((bf16[128,768]{1,0:T(8,128)(2,1)S(1)}, bf16[128,768]{1,0:T(8,128)(2,1)S(1)}, u32[]{:S(2)}, u32[]{:S(2)}) %collective-permute-start.2) | collective-permute-done | bytes 196640 | tf_op jit(solution)/shard_map/ppermute | solution.py:252
  47.0 1.6 %shard_map.68 = (f32[128,256]{1,0:T(8,128)S(1)}, s16[264,128]{1,0:T(8,128)(2,1)S(1)}, s16[264,128]{1,0:T(8,128)(2,1)S(1)}, s16[264,128]{1,0:T(8,128)(2,1)S(1)}) custom-call(bf16[128,768]{1,0:T(8,128)(2,1)S(1)} %get-tuple-element.35.refs_0_, bf16[128,768]{1,0:T(8,128)(2,1)S(1)} %collective-permute-done.refs_1_, ...), custom_call_target="tpu_custom_call" | custom-call | flops 536870912 | bytes 1 | tf_op jit(solution)/shard_map/pallas_call | solution.py:301
  48.7 2.1 %collective-permute-start.12 = (s16[264,128]{1,0:T(8,128)(2,1)S(1)}, s16[264,128]{1,0:T(8,128)(2,1)S(1)}, u32[]{:S(2)}, u32[]{:S(2)}) collective-permute-start(s16[264,128]{1,0:T(8,128)(2,1)S(1)} %get-tuple-element.42), channel_id=1, source_target_pairs={{0,1},{1,0},{2,3},{3,2},{4,5},{5,4},{6,7},{7,6},{8,9},{9,8},{10,11... | collective-permute-start | bytes 202760 | tf_op jit(solution)/shard_map/ppermute | solution.py:252
  50.7 2.0 %collective-permute-start.13 = (s16[264,128]{1,0:T(8,128)(2,1)S(1)}, s16[264,128]{1,0:T(8,128)(2,1)S(1)}, u32[]{:S(2)}, u32[]{:S(2)}) collective-permute-start(s16[264,128]{1,0:T(8,128)(2,1)S(1)} %get-tuple-element.43), channel_id=1, source_target_pairs={{0,2},{1,3},{2,0},{3,1},{4,6},{5,7},{6,4},{7,5},{8,10},{9,11},{10,... | collective-permute-start | bytes 202760 | tf_op jit(solution)/shard_map/ppermute | solution.py:252
  52.7 1.4 %collective-permute-start.14 = (s16[264,128]{1,0:T(8,128)(2,1)S(1)}, s16[264,128]{1,0:T(8,128)(2,1)S(1)}, u32[]{:S(2)}, u32[]{:S(2)}) collective-permute-start(s16[264,128]{1,0:T(8,128)(2,1)S(1)} %get-tuple-element.44), channel_id=1, source_target_pairs={{0,3},{1,2},{2,1},{3,0},{4,7},{5,6},{6,5},{7,4},{8,11},{9,10},{10,... | collective-permute-start | bytes 202760 | tf_op jit(solution)/shard_map/ppermute | solution.py:252
  54.1 0.6 collective-permute-start.18
  54.7 2.4 %collective-permute-start.19 = (bf16[128,256]{1,0:T(8,128)(2,1)S(1)}, bf16[128,256]{1,0:T(8,128)(2,1)S(1)}, u32[]{:S(2)}, u32[]{:S(2)}) collective-permute-start(bf16[128,256]{1,0:T(8,128)(2,1)S(1)} %get-tuple-element.53), channel_id=1, source_target_pairs={{0,2},{1,3},{2,0},{3,1},{4,6},{5,7},{6,4},{7,5},{8,10},{9,11},{10,... | collective-permute-start | bytes 196616 | tf_op jit(solution)/shard_map/ppermute | solution.py:252
  57.1 1.4 %collective-permute-start.20 = (bf16[128,256]{1,0:T(8,128)(2,1)S(1)}, bf16[128,256]{1,0:T(8,128)(2,1)S(1)}, u32[]{:S(2)}, u32[]{:S(2)}) collective-permute-start(bf16[128,256]{1,0:T(8,128)(2,1)S(1)} %get-tuple-element.54), channel_id=1, source_target_pairs={{0,3},{1,2},{2,1},{3,0},{4,7},{5,6},{6,5},{7,4},{8,11},{9,10},{10,... | collective-permute-start | bytes 196616 | tf_op jit(solution)/shard_map/ppermute | solution.py:252
  58.5 1.5 %collective-permute-done.14.rest_3_ = s16[264,128]{1,0:T(8,128)(2,1)S(1)} collective-permute-done((s16[264,128]{1,0:T(8,128)(2,1)S(1)}, s16[264,128]{1,0:T(8,128)(2,1)S(1)}, u32[]{:S(2)}, u32[]{:S(2)}) %collective-permute-start.14) | collective-permute-done | bytes 67616 | tf_op jit(solution)/shard_map/ppermute | solution.py:252
  60.0 0.5 shard_map.69
  60.5 3.6 %collective-permute-done.19.refs_8_ = bf16[128,256]{1,0:T(8,128)(2,1)S(1)} collective-permute-done((bf16[128,256]{1,0:T(8,128)(2,1)S(1)}, bf16[128,256]{1,0:T(8,128)(2,1)S(1)}, u32[]{:S(2)}, u32[]{:S(2)}) %collective-permute-start.19) | collective-permute-done | bytes 65568 | tf_op jit(solution)/shard_map/ppermute | solution.py:252
  64.2 1.6 %shard_map.72 = (f32[128,256]{1,0:T(8,128)S(1)}, s16[264,128]{1,0:T(8,128)(2,1)S(1)}, s16[264,128]{1,0:T(8,128)(2,1)S(1)}, s16[264,128]{1,0:T(8,128)(2,1)S(1)}) custom-call(bf16[128,768]{1,0:T(8,128)(2,1)S(1)} %get-tuple-element.35.refs_0_, bf16[128,768]{1,0:T(8,128)(2,1)S(1)} %collective-permute-done.refs_1_, ...), custom_call_target="tpu_custom_call" | custom-call | flops 536870912 | bytes 1 | tf_op jit(solution)/shard_map/pallas_call | solution.py:301
  65.8 1.3 %collective-permute-start.21 = (s16[264,128]{1,0:T(8,128)(2,1)S(1)}, s16[264,128]{1,0:T(8,128)(2,1)S(1)}, u32[]{:S(2)}, u32[]{:S(2)}) collective-permute-start(s16[264,128]{1,0:T(8,128)(2,1)S(1)} %get-tuple-element.56), channel_id=1, source_target_pairs={{0,1},{1,0},{2,3},{3,2},{4,5},{5,4},{6,7},{7,6},{8,9},{9,8},{10,11... | collective-permute-start | bytes 202760 | tf_op jit(solution)/shard_map/ppermute | solution.py:252
  67.1 1.7 %collective-permute-start.22 = (s16[264,128]{1,0:T(8,128)(2,1)S(1)}, s16[264,128]{1,0:T(8,128)(2,1)S(1)}, u32[]{:S(2)}, u32[]{:S(2)}) collective-permute-start(s16[264,128]{1,0:T(8,128)(2,1)S(1)} %get-tuple-element.57), channel_id=1, source_target_pairs={{0,2},{1,3},{2,0},{3,1},{4,6},{5,7},{6,4},{7,5},{8,10},{9,11},{10,... | collective-permute-start | bytes 202760 | tf_op jit(solution)/shard_map/ppermute | solution.py:252
  68.8 1.4 %collective-permute-start.23 = (s16[264,128]{1,0:T(8,128)(2,1)S(1)}, s16[264,128]{1,0:T(8,128)(2,1)S(1)}, u32[]{:S(2)}, u32[]{:S(2)}) collective-permute-start(s16[264,128]{1,0:T(8,128)(2,1)S(1)} %get-tuple-element.58), channel_id=1, source_target_pairs={{0,3},{1,2},{2,1},{3,0},{4,7},{5,6},{6,5},{7,4},{8,11},{9,10},{10,... | collective-permute-start | bytes 202760 | tf_op jit(solution)/shard_map/ppermute | solution.py:252
  70.2 0.3 collective-permute-done.21.rest_1_
  70.6 3.2 %collective-permute-done.22.rest_2_ = s16[264,128]{1,0:T(8,128)(2,1)S(1)} collective-permute-done((s16[264,128]{1,0:T(8,128)(2,1)S(1)}, s16[264,128]{1,0:T(8,128)(2,1)S(1)}, u32[]{:S(2)}, u32[]{:S(2)}) %collective-permute-start.22) | collective-permute-done | bytes 67616 | tf_op jit(solution)/shard_map/ppermute | solution.py:252
  73.7 1.3 %collective-permute-done.23.rest_3_ = s16[264,128]{1,0:T(8,128)(2,1)S(1)} collective-permute-done((s16[264,128]{1,0:T(8,128)(2,1)S(1)}, s16[264,128]{1,0:T(8,128)(2,1)S(1)}, u32[]{:S(2)}, u32[]{:S(2)}) %collective-permute-start.23) | collective-permute-done | bytes 67616 | tf_op jit(solution)/shard_map/ppermute | solution.py:252
  75.0 0.5 shard_map.73
  75.8 1.5 %collective-permute-start.16 = (s16[2,264,128]{2,1,0:T(8,128)(2,1)S(1)}, s16[2,264,128]{2,1,0:T(8,128)(2,1)S(1)}, u32[]{:S(2)}, u32[]{:S(2)}) collective-permute-start(s16[2,264,128]{2,1,0:T(8,128)(2,1)S(1)} %get-tuple-element.48), channel_id=1, source_target_pairs={{0,16},{4,20},{8,24},{12,28},{16,0},{20,4},{24,8},{28,12},{1,17},{... | collective-permute-start | bytes 405512 | tf_op jit(solution)/shard_map/ppermute | solution.py:333
  77.6 1.4 %collective-permute-start.25 = (s16[264,128]{1,0:T(8,128)(2,1)S(1)}, s16[264,128]{1,0:T(8,128)(2,1)S(1)}, u32[]{:S(2)}, u32[]{:S(2)}) collective-permute-start(s16[264,128]{1,0:T(8,128)(2,1)S(1)} %get-tuple-element.62), channel_id=1, source_target_pairs={{0,8},{4,12},{8,0},{12,4},{16,24},{20,28},{24,16},{28,20},{1,9},{5... | collective-permute-start | bytes 202760 | tf_op jit(solution)/shard_map/ppermute | solution.py:342
  79.0 0.8 collective-permute-start.26
  79.7 1.4 %collective-permute-start.27 = (s16[264,128]{1,0:T(8,128)(2,1)S(1)}, s16[264,128]{1,0:T(8,128)(2,1)S(1)}, u32[]{:S(2)}, u32[]{:S(2)}) collective-permute-start(s16[264,128]{1,0:T(8,128)(2,1)S(1)} %get-tuple-element.64), channel_id=1, source_target_pairs={{0,24},{4,28},{8,16},{12,20},{16,8},{20,12},{24,0},{28,4},{1,25},{... | collective-permute-start | bytes 202760 | tf_op jit(solution)/shard_map/ppermute | solution.py:342
  81.1 1.2 %collective-permute-done.16.second = s16[2,264,128]{2,1,0:T(8,128)(2,1)S(1)} collective-permute-done((s16[2,264,128]{2,1,0:T(8,128)(2,1)S(1)}, s16[2,264,128]{2,1,0:T(8,128)(2,1)S(1)}, u32[]{:S(2)}, u32[]{:S(2)}) %collective-permute-start.16) | collective-permute-done | bytes 135200 | tf_op jit(solution)/shard_map/ppermute | solution.py:333
  82.4 1.6 %collective-permute-start.17 = (s16[1,264,128]{2,1,0:T(8,128)(2,1)S(1)}, s16[1,264,128]{2,1,0:T(8,128)(2,1)S(1)}, u32[]{:S(2)}, u32[]{:S(2)}) collective-permute-start(s16[1,264,128]{2,1,0:T(8,128)(2,1)S(1)} %get-tuple-element.50), channel_id=1, source_target_pairs={{0,8},{4,12},{8,0},{12,4},{16,24},{20,28},{24,16},{28,20},{1,9},{5... | collective-permute-start | bytes 202760 | tf_op jit(solution)/shard_map/ppermute | solution.py:333
  84.0 0.9 %collective-permute-done.27.refs_5_ = s16[264,128]{1,0:T(8,128)(2,1)S(1)} collective-permute-done((s16[264,128]{1,0:T(8,128)(2,1)S(1)}, s16[264,128]{1,0:T(8,128)(2,1)S(1)}, u32[]{:S(2)}, u32[]{:S(2)}) %collective-permute-start.27) | collective-permute-done | bytes 67616 | tf_op jit(solution)/shard_map/ppermute | solution.py:342
  84.9 1.8 %collective-permute-done.17.refs_1_ = s16[1,264,128]{2,1,0:T(8,128)(2,1)S(1)} collective-permute-done((s16[1,264,128]{2,1,0:T(8,128)(2,1)S(1)}, s16[1,264,128]{2,1,0:T(8,128)(2,1)S(1)}, u32[]{:S(2)}, u32[]{:S(2)}) %collective-permute-start.17) | collective-permute-done | bytes 67616 | tf_op jit(solution)/shard_map/ppermute | solution.py:333
  86.8 0.8 shard_map.75
  (28 shorter events, 1.4 us)
Async XLA Ops:
  0.0 0.9 %copy-start = (f32[1,128,512]{2,1,0:T(8,128)S(1)}, f32[1,128,512]{2,1,0:T(8,128)}, u32[]{:S(2)}) copy-start(f32[1,128,512]{2,1,0:T(8,128)} %param.6) | copy-start | bytes 786436
  1.1 10.5 %collective-permute-start.6 = (s16[520,128]{1,0:T(8,128)(2,1)S(1)}, s16[520,128]{1,0:T(8,128)(2,1)S(1)}, u32[]{:S(2)}, u32[]{:S(2)}) collective-permute-start(s16[520,128]{1,0:T(8,128)(2,1)S(1)} %shard_map.65.rest_0_), channel_id=1, source_target_pairs={{0,2},{1,3},{2,0},{3,1},{4,6},{5,7},{6,4},{7,5},{8,10},{9,11},{10,... | collective-permute-start | bytes 399368 | tf_op jit(solution)/shard_map/ppermute | solution.py:278
  5.2 9.4 %collective-permute-start.5 = (s16[520,128]{1,0:T(8,128)(2,1)S(1)}, s16[520,128]{1,0:T(8,128)(2,1)S(1)}, u32[]{:S(2)}, u32[]{:S(2)}) collective-permute-start(s16[520,128]{1,0:T(8,128)(2,1)S(1)} %shard_map.65.rest_0_), channel_id=1, source_target_pairs={{0,24},{4,28},{8,16},{12,20},{16,8},{20,12},{24,0},{28,4},{1,25},{... | collective-permute-start | bytes 399368 | tf_op jit(solution)/shard_map/ppermute | solution.py:282
  7.7 7.4 %collective-permute-start.4 = (s16[520,128]{1,0:T(8,128)(2,1)S(1)}, s16[520,128]{1,0:T(8,128)(2,1)S(1)}, u32[]{:S(2)}, u32[]{:S(2)}) collective-permute-start(s16[520,128]{1,0:T(8,128)(2,1)S(1)} %shard_map.65.rest_0_), channel_id=1, source_target_pairs={{0,16},{4,20},{8,24},{12,28},{16,0},{20,4},{24,8},{28,12},{1,17},{... | collective-permute-start | bytes 399368 | tf_op jit(solution)/shard_map/ppermute | solution.py:282
  8.2 6.9 %collective-permute-start.3 = (s16[520,128]{1,0:T(8,128)(2,1)S(1)}, s16[520,128]{1,0:T(8,128)(2,1)S(1)}, u32[]{:S(2)}, u32[]{:S(2)}) collective-permute-start(s16[520,128]{1,0:T(8,128)(2,1)S(1)} %shard_map.65.rest_0_), channel_id=1, source_target_pairs={{0,8},{4,12},{8,0},{12,4},{16,24},{20,28},{24,16},{28,20},{1,9},{5... | collective-permute-start | bytes 399368 | tf_op jit(solution)/shard_map/ppermute | solution.py:282
  11.6 6.8 %collective-permute-start.9 = (s16[520,128]{1,0:T(8,128)(2,1)S(1)}, s16[520,128]{1,0:T(8,128)(2,1)S(1)}, u32[]{:S(2)}, u32[]{:S(2)}) collective-permute-start(s16[520,128]{1,0:T(8,128)(2,1)S(1)} %collective-permute-done.6.rest_4_), channel_id=1, source_target_pairs={{0,24},{4,28},{8,16},{12,20},{16,8},{20,12},{24,0},{28,4},{1,25},{... | collective-permute-start | bytes 399368 | tf_op jit(solution)/shard_map/ppermute | solution.py:282
  14.1 6.0 %collective-permute-start.8 = (s16[520,128]{1,0:T(8,128)(2,1)S(1)}, s16[520,128]{1,0:T(8,128)(2,1)S(1)}, u32[]{:S(2)}, u32[]{:S(2)}) collective-permute-start(s16[520,128]{1,0:T(8,128)(2,1)S(1)} %collective-permute-done.6.rest_4_), channel_id=1, source_target_pairs={{0,16},{4,20},{8,24},{12,28},{16,0},{20,4},{24,8},{28,12},{1,17},{... | collective-permute-start | bytes 399368 | tf_op jit(solution)/shard_map/ppermute | solution.py:282
  14.6 5.5 %collective-permute-start.7 = (s16[520,128]{1,0:T(8,128)(2,1)S(1)}, s16[520,128]{1,0:T(8,128)(2,1)S(1)}, u32[]{:S(2)}, u32[]{:S(2)}) collective-permute-start(s16[520,128]{1,0:T(8,128)(2,1)S(1)} %collective-permute-done.6.rest_4_), channel_id=1, source_target_pairs={{0,8},{4,12},{8,0},{12,4},{16,24},{20,28},{24,16},{28,20},{1,9},{5... | collective-permute-start | bytes 399368 | tf_op jit(solution)/shard_map/ppermute | solution.py:282
  20.1 0.7 copy-start.1
  20.9 2.0 %collective-permute-start.10 = (s16[4,520,128]{2,1,0:T(8,128)(2,1)S(1)}, s16[4,520,128]{2,1,0:T(8,128)(2,1)S(1)}, u32[]{:S(2)}, u32[]{:S(2)}) collective-permute-start(s16[4,520,128]{2,1,0:T(8,128)(2,1)S(1)} %shard_map.66), channel_id=1, source_target_pairs={{0,4},{4,0},{8,12},{12,8},{16,20},{20,16},{24,28},{28,24},{1,5},{5... | collective-permute-start | bytes 1597448 | tf_op jit(solution)/shard_map/ppermute | solution.py:289
  23.2 23.9 %collective-permute-start.11 = (s16[2,520,128]{2,1,0:T(8,128)(2,1)S(1)}, s16[2,520,128]{2,1,0:T(8,128)(2,1)S(1)}, u32[]{:S(2)}, u32[]{:S(2)}) collective-permute-start(s16[2,520,128]{2,1,0:T(8,128)(2,1)S(1)} %get-tuple-element.40), channel_id=1, source_target_pairs={{0,1},{1,0},{2,3},{3,2},{4,5},{5,4},{6,7},{7,6},{8,9},{9,8},{10,11... | collective-permute-start | bytes 798728 | tf_op jit(solution)/shard_map/ppermute | solution.py:295
  24.8 0.7 copy-start.3
  25.4 34.5 %copy-start.2 = (s32[32,1]{0,1:T(1,128)S(1)}, s32[32,1]{0,1:T(1,128)}, u32[]{:S(2)}) copy-start(s32[32,1]{0,1:T(1,128)} %param.10) | copy-start | bytes 388
  26.9 13.2 %collective-permute-start = (bf16[128,768]{1,0:T(8,128)(2,1)S(1)}, bf16[128,768]{1,0:T(8,128)(2,1)S(1)}, u32[]{:S(2)}, u32[]{:S(2)}) collective-permute-start(bf16[128,768]{1,0:T(8,128)(2,1)S(1)} %get-tuple-element.36), channel_id=1, source_target_pairs={{0,1},{1,0},{2,3},{3,2},{4,5},{5,4},{6,7},{7,6},{8,9},{9,8},{10,11... | collective-permute-start | bytes 589832 | tf_op jit(solution)/shard_map/ppermute | solution.py:252
  27.5 12.6 %collective-permute-start.1 = (bf16[128,768]{1,0:T(8,128)(2,1)S(1)}, bf16[128,768]{1,0:T(8,128)(2,1)S(1)}, u32[]{:S(2)}, u32[]{:S(2)}) collective-permute-start(bf16[128,768]{1,0:T(8,128)(2,1)S(1)} %get-tuple-element.37), channel_id=1, source_target_pairs={{0,2},{1,3},{2,0},{3,1},{4,6},{5,7},{6,4},{7,5},{8,10},{9,11},{10,... | collective-permute-start | bytes 589832 | tf_op jit(solution)/shard_map/ppermute | solution.py:252
  30.5 16.6 %collective-permute-start.2 = (bf16[128,768]{1,0:T(8,128)(2,1)S(1)}, bf16[128,768]{1,0:T(8,128)(2,1)S(1)}, u32[]{:S(2)}, u32[]{:S(2)}) collective-permute-start(bf16[128,768]{1,0:T(8,128)(2,1)S(1)} %get-tuple-element.38), channel_id=1, source_target_pairs={{0,3},{1,2},{2,1},{3,0},{4,7},{5,6},{6,5},{7,4},{8,11},{9,10},{10,... | collective-permute-start | bytes 589832 | tf_op jit(solution)/shard_map/ppermute | solution.py:252
  48.7 8.4 %collective-permute-start.12 = (s16[264,128]{1,0:T(8,128)(2,1)S(1)}, s16[264,128]{1,0:T(8,128)(2,1)S(1)}, u32[]{:S(2)}, u32[]{:S(2)}) collective-permute-start(s16[264,128]{1,0:T(8,128)(2,1)S(1)} %get-tuple-element.42), channel_id=1, source_target_pairs={{0,1},{1,0},{2,3},{3,2},{4,5},{5,4},{6,7},{7,6},{8,9},{9,8},{10,11... | collective-permute-start | bytes 202760 | tf_op jit(solution)/shard_map/ppermute | solution.py:252
  50.7 7.8 %collective-permute-start.13 = (s16[264,128]{1,0:T(8,128)(2,1)S(1)}, s16[264,128]{1,0:T(8,128)(2,1)S(1)}, u32[]{:S(2)}, u32[]{:S(2)}) collective-permute-start(s16[264,128]{1,0:T(8,128)(2,1)S(1)} %get-tuple-element.43), channel_id=1, source_target_pairs={{0,2},{1,3},{2,0},{3,1},{4,6},{5,7},{6,4},{7,5},{8,10},{9,11},{10,... | collective-permute-start | bytes 202760 | tf_op jit(solution)/shard_map/ppermute | solution.py:252
  52.7 7.3 %collective-permute-start.14 = (s16[264,128]{1,0:T(8,128)(2,1)S(1)}, s16[264,128]{1,0:T(8,128)(2,1)S(1)}, u32[]{:S(2)}, u32[]{:S(2)}) collective-permute-start(s16[264,128]{1,0:T(8,128)(2,1)S(1)} %get-tuple-element.44), channel_id=1, source_target_pairs={{0,3},{1,2},{2,1},{3,0},{4,7},{5,6},{6,5},{7,4},{8,11},{9,10},{10,... | collective-permute-start | bytes 202760 | tf_op jit(solution)/shard_map/ppermute | solution.py:252
  54.1 6.4 %collective-permute-start.18 = (bf16[128,256]{1,0:T(8,128)(2,1)S(1)}, bf16[128,256]{1,0:T(8,128)(2,1)S(1)}, u32[]{:S(2)}, u32[]{:S(2)}) collective-permute-start(bf16[128,256]{1,0:T(8,128)(2,1)S(1)} %get-tuple-element.52), channel_id=1, source_target_pairs={{0,1},{1,0},{2,3},{3,2},{4,5},{5,4},{6,7},{7,6},{8,9},{9,8},{10,11... | collective-permute-start | bytes 196616 | tf_op jit(solution)/shard_map/ppermute | solution.py:252
  54.7 9.5 %collective-permute-start.19 = (bf16[128,256]{1,0:T(8,128)(2,1)S(1)}, bf16[128,256]{1,0:T(8,128)(2,1)S(1)}, u32[]{:S(2)}, u32[]{:S(2)}) collective-permute-start(bf16[128,256]{1,0:T(8,128)(2,1)S(1)} %get-tuple-element.53), channel_id=1, source_target_pairs={{0,2},{1,3},{2,0},{3,1},{4,6},{5,7},{6,4},{7,5},{8,10},{9,11},{10,... | collective-permute-start | bytes 196616 | tf_op jit(solution)/shard_map/ppermute | solution.py:252
  57.1 7.1 %collective-permute-start.20 = (bf16[128,256]{1,0:T(8,128)(2,1)S(1)}, bf16[128,256]{1,0:T(8,128)(2,1)S(1)}, u32[]{:S(2)}, u32[]{:S(2)}) collective-permute-start(bf16[128,256]{1,0:T(8,128)(2,1)S(1)} %get-tuple-element.54), channel_id=1, source_target_pairs={{0,3},{1,2},{2,1},{3,0},{4,7},{5,6},{6,5},{7,4},{8,11},{9,10},{10,... | collective-permute-start | bytes 196616 | tf_op jit(solution)/shard_map/ppermute | solution.py:252
  60.5 15.1 %collective-permute-start.15 = (s16[4,264,128]{2,1,0:T(8,128)(2,1)S(1)}, s16[4,264,128]{2,1,0:T(8,128)(2,1)S(1)}, u32[]{:S(2)}, u32[]{:S(2)}) collective-permute-start(s16[4,264,128]{2,1,0:T(8,128)(2,1)S(1)} %get-tuple-element.46), channel_id=1, source_target_pairs={{0,4},{4,0},{8,12},{12,8},{16,20},{20,16},{24,28},{28,24},{1,5},{5... | collective-permute-start | bytes 811016 | tf_op jit(solution)/shard_map/ppermute | solution.py:321
  65.8 4.8 %collective-permute-start.21 = (s16[264,128]{1,0:T(8,128)(2,1)S(1)}, s16[264,128]{1,0:T(8,128)(2,1)S(1)}, u32[]{:S(2)}, u32[]{:S(2)}) collective-permute-start(s16[264,128]{1,0:T(8,128)(2,1)S(1)} %get-tuple-element.56), channel_id=1, source_target_pairs={{0,1},{1,0},{2,3},{3,2},{4,5},{5,4},{6,7},{7,6},{8,9},{9,8},{10,11... | collective-permute-start | bytes 202760 | tf_op jit(solution)/shard_map/ppermute | solution.py:252
  67.1 6.6 %collective-permute-start.22 = (s16[264,128]{1,0:T(8,128)(2,1)S(1)}, s16[264,128]{1,0:T(8,128)(2,1)S(1)}, u32[]{:S(2)}, u32[]{:S(2)}) collective-permute-start(s16[264,128]{1,0:T(8,128)(2,1)S(1)} %get-tuple-element.57), channel_id=1, source_target_pairs={{0,2},{1,3},{2,0},{3,1},{4,6},{5,7},{6,4},{7,5},{8,10},{9,11},{10,... | collective-permute-start | bytes 202760 | tf_op jit(solution)/shard_map/ppermute | solution.py:252
  68.8 6.2 %collective-permute-start.23 = (s16[264,128]{1,0:T(8,128)(2,1)S(1)}, s16[264,128]{1,0:T(8,128)(2,1)S(1)}, u32[]{:S(2)}, u32[]{:S(2)}) collective-permute-start(s16[264,128]{1,0:T(8,128)(2,1)S(1)} %get-tuple-element.58), channel_id=1, source_target_pairs={{0,3},{1,2},{2,1},{3,0},{4,7},{5,6},{6,5},{7,4},{8,11},{9,10},{10,... | collective-permute-start | bytes 202760 | tf_op jit(solution)/shard_map/ppermute | solution.py:252
  75.5 1.8 %collective-permute-start.24 = (s16[4,264,128]{2,1,0:T(8,128)(2,1)S(1)}, s16[4,264,128]{2,1,0:T(8,128)(2,1)S(1)}, u32[]{:S(2)}, u32[]{:S(2)}) collective-permute-start(s16[4,264,128]{2,1,0:T(8,128)(2,1)S(1)} %get-tuple-element.60), channel_id=1, source_target_pairs={{0,4},{4,0},{8,12},{12,8},{16,20},{20,16},{24,28},{28,24},{1,5},{5... | collective-permute-start | bytes 811016 | tf_op jit(solution)/shard_map/ppermute | solution.py:321
  75.8 6.5 %collective-permute-start.16 = (s16[2,264,128]{2,1,0:T(8,128)(2,1)S(1)}, s16[2,264,128]{2,1,0:T(8,128)(2,1)S(1)}, u32[]{:S(2)}, u32[]{:S(2)}) collective-permute-start(s16[2,264,128]{2,1,0:T(8,128)(2,1)S(1)} %get-tuple-element.48), channel_id=1, source_target_pairs={{0,16},{4,20},{8,24},{12,28},{16,0},{20,4},{24,8},{28,12},{1,17},{... | collective-permute-start | bytes 405512 | tf_op jit(solution)/shard_map/ppermute | solution.py:333
  77.6 6.5 %collective-permute-start.25 = (s16[264,128]{1,0:T(8,128)(2,1)S(1)}, s16[264,128]{1,0:T(8,128)(2,1)S(1)}, u32[]{:S(2)}, u32[]{:S(2)}) collective-permute-start(s16[264,128]{1,0:T(8,128)(2,1)S(1)} %get-tuple-element.62), channel_id=1, source_target_pairs={{0,8},{4,12},{8,0},{12,4},{16,24},{20,28},{24,16},{28,20},{1,9},{5... | collective-permute-start | bytes 202760 | tf_op jit(solution)/shard_map/ppermute | solution.py:342
  79.0 5.1 %collective-permute-start.26 = (s16[264,128]{1,0:T(8,128)(2,1)S(1)}, s16[264,128]{1,0:T(8,128)(2,1)S(1)}, u32[]{:S(2)}, u32[]{:S(2)}) collective-permute-start(s16[264,128]{1,0:T(8,128)(2,1)S(1)} %get-tuple-element.63), channel_id=1, source_target_pairs={{0,16},{4,20},{8,24},{12,28},{16,0},{20,4},{24,8},{28,12},{1,17},{... | collective-permute-start | bytes 202760 | tf_op jit(solution)/shard_map/ppermute | solution.py:342
  79.7 5.2 %collective-permute-start.27 = (s16[264,128]{1,0:T(8,128)(2,1)S(1)}, s16[264,128]{1,0:T(8,128)(2,1)S(1)}, u32[]{:S(2)}, u32[]{:S(2)}) collective-permute-start(s16[264,128]{1,0:T(8,128)(2,1)S(1)} %get-tuple-element.64), channel_id=1, source_target_pairs={{0,24},{4,28},{8,16},{12,20},{16,8},{20,12},{24,0},{28,4},{1,25},{... | collective-permute-start | bytes 202760 | tf_op jit(solution)/shard_map/ppermute | solution.py:342
  82.4 4.4 %collective-permute-start.17 = (s16[1,264,128]{2,1,0:T(8,128)(2,1)S(1)}, s16[1,264,128]{2,1,0:T(8,128)(2,1)S(1)}, u32[]{:S(2)}, u32[]{:S(2)}) collective-permute-start(s16[1,264,128]{2,1,0:T(8,128)(2,1)S(1)} %get-tuple-element.50), channel_id=1, source_target_pairs={{0,8},{4,12},{8,0},{12,4},{16,24},{20,28},{24,16},{28,20},{1,9},{5... | collective-permute-start | bytes 202760 | tf_op jit(solution)/shard_map/ppermute | solution.py:333

commit v8 on v7

--- a/solution.py
+++ b/solution.py
@@ -170,8 +170,8 @@
             encode(part, outs[step], False)
 
 
-def combine_kernel(base, sec, me, count, chips, target_ref, *rest):
-    parts, (keep, code, send) = rest[:count], rest[count:]
+def combine_kernel(base, sec, me, count, target_ref, *rest):
+    parts, keep, send = rest[:count], rest[count], rest[count + 1]
     start, mine = base(), me()
     chip, core = sec() // 2, lax.rem(sec(), 2)
     keep[...] = jnp.zeros(keep.shape, jnp.float32)
@@ -190,13 +190,10 @@
         def _():
             send[hop] = send[hop] + part
 
-    for hop in range(chips):
-        encode(send[hop], code.at[hop], False)
-
 
 def join_kernel(chips, keep, other, *outs):
     for hop in range(chips):
-        total = keep[hop] + decode(other.at[hop], *keep.shape[1:])
+        total = keep[hop] + other[hop]
         if hop == 0:
             outs[0][...] = total
         else:
@@ -308,13 +305,12 @@
             halves.append(exchange(parts))
         for half, mine in enumerate(halves):
             kept, sent = call(
-                functools.partial(combine_kernel, base, sec, me, count, chips),
-                [stack, jax.ShapeDtypeStruct((chips, *piece.shape), piece.dtype)],
+                functools.partial(combine_kernel, base, sec, me, count),
+                [stack, stack],
                 [VMEM] * (count + 1),
-                [pltpu.VMEM(stack.shape, f32)],
             )(targets, *mine)
             if turn:
-                raise NotImplementedError
+                kept, sent = keeps[half] + kept, sends[half] + sent
             keeps[half], sends[half] = kept, sent
     waves = []
     for half in range(HALVES):

time: 87.7 us -> 87.1 us (level)
    ppermute x2, waiting for transfers between devices: 2.98 us -> 1.79 us  [body(): other = lax.ppermute(sent, 'sec', across(bit))]
  transfers between devices with their start and end apart: 28 -> 28, of which waited for: 14 -> 16; matrix products, arithmetic and copies ran while one was open for 0% -> 0% of each run, Pallas kernels for 5% -> 5%
where the time goes in v8:
time: 87.1 us; the launch traced here: 87 us
  starting transfers between devices  39.2 us (45%)
  waiting for transfers between devices  38.3 us (44%)
  Pallas kernels  7.06 us (8%)
  local copies, waits for them, and re-layouts  2.26 us (3%)
    ppermute x12, waiting for transfers between devices, exchange(): got[s] = lax.ppermute(blocks[s], 'env', along(s))  25.3 us
    ppermute x12, starting transfers between devices, exchange(): got[s] = lax.ppermute(blocks[s], 'env', along(s))  19.2 us
    ppermute x6, starting transfers between devices, body(): lax.ppermute(rows_of, 'sec', across(hop))  6.98 us
    ppermute x6, waiting for transfers between devices, body(): lax.ppermute(rows_of, 'sec', across(hop))  4.97 us
    ppermute x1, starting transfers between devices, body(): far = lax.ppermute(psi, 'env', along(count // 2))  4.13 us
    ppermute x3, starting transfers between devices, body(): lax.ppermute(mine[hop], 'sec', across(hop))  3.55 us
    ppermute x2, starting transfers between devices, body(): other = lax.ppermute(sent, 'sec', across(bit))  3.52 us
    pallas_call x2, Pallas kernels, body(): call(functools.partial(task_kernel, me, count, half), [part] + [piece] *...  3.23 us
  transfers between devices with their start and end apart: 28, of which 16 were waited for; matrix products, arithmetic and copies ran while one was open for 0% of the time, Pallas kernels for 5%

profile of v8, /device:TPU:0, one launch (start us, length us, event | category | flops | bytes accessed | tf_op | source)
XLA Modules:
  0.0 87.0 jit_solution(4130624186933516476)
XLA Ops:
  0.0 0.9 %copy-done = f32[1,128,512]{2,1,0:T(8,128)S(1)} copy-done((f32[1,128,512]{2,1,0:T(8,128)S(1)}, f32[1,128,512]{2,1,0:T(8,128)}, u32[]{:S(2)}) %copy-start) | copy-done | bytes 262168
  1.1 4.1 %collective-permute-start.6 = (s16[520,128]{1,0:T(8,128)(2,1)S(1)}, s16[520,128]{1,0:T(8,128)(2,1)S(1)}, u32[]{:S(2)}, u32[]{:S(2)}) collective-permute-start(s16[520,128]{1,0:T(8,128)(2,1)S(1)} %shard_map.65.rest_0_), channel_id=1, source_target_pairs={{0,2},{1,3},{2,0},{3,1},{4,6},{5,7},{6,4},{7,5},{8,10},{9,11},{10,... | collective-permute-start | bytes 399368 | tf_op jit(solution)/shard_map/ppermute | solution.py:275
  5.2 2.4 %collective-permute-start.5 = (s16[520,128]{1,0:T(8,128)(2,1)S(1)}, s16[520,128]{1,0:T(8,128)(2,1)S(1)}, u32[]{:S(2)}, u32[]{:S(2)}) collective-permute-start(s16[520,128]{1,0:T(8,128)(2,1)S(1)} %shard_map.65.rest_0_), channel_id=1, source_target_pairs={{0,24},{4,28},{8,16},{12,20},{16,8},{20,12},{24,0},{28,4},{1,25},{... | collective-permute-start | bytes 399368 | tf_op jit(solution)/shard_map/ppermute | solution.py:279
  7.7 0.5 collective-permute-start.4
  8.2 0.5 collective-permute-start.3
  8.7 2.9 %collective-permute-done.6.rest_4_ = s16[520,128]{1,0:T(8,128)(2,1)S(1)} collective-permute-done((s16[520,128]{1,0:T(8,128)(2,1)S(1)}, s16[520,128]{1,0:T(8,128)(2,1)S(1)}, u32[]{:S(2)}, u32[]{:S(2)}) %collective-permute-start.6) | collective-permute-done | bytes 133152 | tf_op jit(solution)/shard_map/ppermute | solution.py:275
  11.6 2.5 %collective-permute-start.9 = (s16[520,128]{1,0:T(8,128)(2,1)S(1)}, s16[520,128]{1,0:T(8,128)(2,1)S(1)}, u32[]{:S(2)}, u32[]{:S(2)}) collective-permute-start(s16[520,128]{1,0:T(8,128)(2,1)S(1)} %collective-permute-done.6.rest_4_), channel_id=1, source_target_pairs={{0,24},{4,28},{8,16},{12,20},{16,8},{20,12},{24,0},{28,4},{1,25},{... | collective-permute-start | bytes 399368 | tf_op jit(solution)/shard_map/ppermute | solution.py:279
  14.1 0.5 collective-permute-start.8
  14.6 0.5 collective-permute-start.7
  15.1 3.3 %collective-permute-done.9.rest_7_ = s16[520,128]{1,0:T(8,128)(2,1)S(1)} collective-permute-done((s16[520,128]{1,0:T(8,128)(2,1)S(1)}, s16[520,128]{1,0:T(8,128)(2,1)S(1)}, u32[]{:S(2)}, u32[]{:S(2)}) %collective-permute-start.9) | collective-permute-done | bytes 133152 | tf_op jit(solution)/shard_map/ppermute | solution.py:279
  18.4 1.7 %collective-permute-done.8.rest_6_ = s16[520,128]{1,0:T(8,128)(2,1)S(1)} collective-permute-done((s16[520,128]{1,0:T(8,128)(2,1)S(1)}, s16[520,128]{1,0:T(8,128)(2,1)S(1)}, u32[]{:S(2)}, u32[]{:S(2)}) %collective-permute-start.8) | collective-permute-done | bytes 133152 | tf_op jit(solution)/shard_map/ppermute | solution.py:279
  20.1 0.7 copy-done.1
  21.0 1.9 %collective-permute-done.10.rest_8_ = s16[4,520,128]{2,1,0:T(8,128)(2,1)S(1)} collective-permute-done((s16[4,520,128]{2,1,0:T(8,128)(2,1)S(1)}, s16[4,520,128]{2,1,0:T(8,128)(2,1)S(1)}, u32[]{:S(2)}, u32[]{:S(2)}) %collective-permute-start.10) | collective-permute-done | bytes 532512 | tf_op jit(solution)/shard_map/ppermute | solution.py:286
  23.2 1.6 %collective-permute-start.11 = (s16[2,520,128]{2,1,0:T(8,128)(2,1)S(1)}, s16[2,520,128]{2,1,0:T(8,128)(2,1)S(1)}, u32[]{:S(2)}, u32[]{:S(2)}) collective-permute-start(s16[2,520,128]{2,1,0:T(8,128)(2,1)S(1)} %get-tuple-element.40), channel_id=1, source_target_pairs={{0,1},{1,0},{2,3},{3,2},{4,5},{5,4},{6,7},{7,6},{8,9},{9,8},{10,11... | collective-permute-start | bytes 798728 | tf_op jit(solution)/shard_map/ppermute | solution.py:292
  24.8 0.7 copy-done.3
  25.4 1.5 %shard_map.64 = (bf16[128,768]{1,0:T(8,128)(2,1)S(1)}, bf16[128,768]{1,0:T(8,128)(2,1)S(1)}, bf16[128,768]{1,0:T(8,128)(2,1)S(1)}, bf16[128,768]{1,0:T(8,128)(2,...) custom-call(s32[1,32]{1,0:T(1,128)S(1)} %bitcast.10, ...), custom_call_target="tpu_custom_call" | custom-call | flops 1 | bytes 1 | tf_op jit(solution)/shard_map/pallas_call | solution.py:265
  26.9 0.5 collective-permute-start
  27.5 3.0 %collective-permute-start.1 = (bf16[128,768]{1,0:T(8,128)(2,1)S(1)}, bf16[128,768]{1,0:T(8,128)(2,1)S(1)}, u32[]{:S(2)}, u32[]{:S(2)}) collective-permute-start(bf16[128,768]{1,0:T(8,128)(2,1)S(1)} %get-tuple-element.37), channel_id=1, source_target_pairs={{0,2},{1,3},{2,0},{3,1},{4,6},{5,7},{6,4},{7,5},{8,10},{9,11},{10,... | collective-permute-start | bytes 589832 | tf_op jit(solution)/shard_map/ppermute | solution.py:249
  30.5 1.4 %collective-permute-start.2 = (bf16[128,768]{1,0:T(8,128)(2,1)S(1)}, bf16[128,768]{1,0:T(8,128)(2,1)S(1)}, u32[]{:S(2)}, u32[]{:S(2)}) collective-permute-start(bf16[128,768]{1,0:T(8,128)(2,1)S(1)} %get-tuple-element.38), channel_id=1, source_target_pairs={{0,3},{1,2},{2,1},{3,0},{4,7},{5,6},{6,5},{7,4},{8,11},{9,10},{10,... | collective-permute-start | bytes 589832 | tf_op jit(solution)/shard_map/ppermute | solution.py:249
  31.8 8.2 %collective-permute-done.refs_1_ = bf16[128,768]{1,0:T(8,128)(2,1)S(1)} collective-permute-done((bf16[128,768]{1,0:T(8,128)(2,1)S(1)}, bf16[128,768]{1,0:T(8,128)(2,1)S(1)}, u32[]{:S(2)}, u32[]{:S(2)}) %collective-permute-start) | collective-permute-done | bytes 196640 | tf_op jit(solution)/shard_map/ppermute | solution.py:249
  40.1 6.9 %collective-permute-done.2.refs_3_ = bf16[128,768]{1,0:T(8,128)(2,1)S(1)} collective-permute-done((bf16[128,768]{1,0:T(8,128)(2,1)S(1)}, bf16[128,768]{1,0:T(8,128)(2,1)S(1)}, u32[]{:S(2)}, u32[]{:S(2)}) %collective-permute-start.2) | collective-permute-done | bytes 196640 | tf_op jit(solution)/shard_map/ppermute | solution.py:249
  47.0 1.6 %shard_map.68 = (f32[128,256]{1,0:T(8,128)S(1)}, s16[264,128]{1,0:T(8,128)(2,1)S(1)}, s16[264,128]{1,0:T(8,128)(2,1)S(1)}, s16[264,128]{1,0:T(8,128)(2,1)S(1)}) custom-call(bf16[128,768]{1,0:T(8,128)(2,1)S(1)} %get-tuple-element.35.refs_0_, bf16[128,768]{1,0:T(8,128)(2,1)S(1)} %collective-permute-done.refs_1_, ...), custom_call_target="tpu_custom_call" | custom-call | flops 536870912 | bytes 1 | tf_op jit(solution)/shard_map/pallas_call | solution.py:298
  48.7 2.1 %collective-permute-start.12 = (s16[264,128]{1,0:T(8,128)(2,1)S(1)}, s16[264,128]{1,0:T(8,128)(2,1)S(1)}, u32[]{:S(2)}, u32[]{:S(2)}) collective-permute-start(s16[264,128]{1,0:T(8,128)(2,1)S(1)} %get-tuple-element.42), channel_id=1, source_target_pairs={{0,1},{1,0},{2,3},{3,2},{4,5},{5,4},{6,7},{7,6},{8,9},{9,8},{10,11... | collective-permute-start | bytes 202760 | tf_op jit(solution)/shard_map/ppermute | solution.py:249
  50.7 2.0 %collective-permute-start.13 = (s16[264,128]{1,0:T(8,128)(2,1)S(1)}, s16[264,128]{1,0:T(8,128)(2,1)S(1)}, u32[]{:S(2)}, u32[]{:S(2)}) collective-permute-start(s16[264,128]{1,0:T(8,128)(2,1)S(1)} %get-tuple-element.43), channel_id=1, source_target_pairs={{0,2},{1,3},{2,0},{3,1},{4,6},{5,7},{6,4},{7,5},{8,10},{9,11},{10,... | collective-permute-start | bytes 202760 | tf_op jit(solution)/shard_map/ppermute | solution.py:249
  52.7 1.4 %collective-permute-start.14 = (s16[264,128]{1,0:T(8,128)(2,1)S(1)}, s16[264,128]{1,0:T(8,128)(2,1)S(1)}, u32[]{:S(2)}, u32[]{:S(2)}) collective-permute-start(s16[264,128]{1,0:T(8,128)(2,1)S(1)} %get-tuple-element.44), channel_id=1, source_target_pairs={{0,3},{1,2},{2,1},{3,0},{4,7},{5,6},{6,5},{7,4},{8,11},{9,10},{10,... | collective-permute-start | bytes 202760 | tf_op jit(solution)/shard_map/ppermute | solution.py:249
  54.1 0.6 collective-permute-start.18
  54.7 2.4 %collective-permute-start.19 = (bf16[128,256]{1,0:T(8,128)(2,1)S(1)}, bf16[128,256]{1,0:T(8,128)(2,1)S(1)}, u32[]{:S(2)}, u32[]{:S(2)}) collective-permute-start(bf16[128,256]{1,0:T(8,128)(2,1)S(1)} %get-tuple-element.53), channel_id=1, source_target_pairs={{0,2},{1,3},{2,0},{3,1},{4,6},{5,7},{6,4},{7,5},{8,10},{9,11},{10,... | collective-permute-start | bytes 196616 | tf_op jit(solution)/shard_map/ppermute | solution.py:249
  57.1 1.4 %collective-permute-start.20 = (bf16[128,256]{1,0:T(8,128)(2,1)S(1)}, bf16[128,256]{1,0:T(8,128)(2,1)S(1)}, u32[]{:S(2)}, u32[]{:S(2)}) collective-permute-start(bf16[128,256]{1,0:T(8,128)(2,1)S(1)} %get-tuple-element.54), channel_id=1, source_target_pairs={{0,3},{1,2},{2,1},{3,0},{4,7},{5,6},{6,5},{7,4},{8,11},{9,10},{10,... | collective-permute-start | bytes 196616 | tf_op jit(solution)/shard_map/ppermute | solution.py:249
  58.5 1.5 %collective-permute-done.14.rest_3_ = s16[264,128]{1,0:T(8,128)(2,1)S(1)} collective-permute-done((s16[264,128]{1,0:T(8,128)(2,1)S(1)}, s16[264,128]{1,0:T(8,128)(2,1)S(1)}, u32[]{:S(2)}, u32[]{:S(2)}) %collective-permute-start.14) | collective-permute-done | bytes 67616 | tf_op jit(solution)/shard_map/ppermute | solution.py:249
  60.0 0.3 shard_map.69
  60.3 3.8 %collective-permute-done.19.refs_8_ = bf16[128,256]{1,0:T(8,128)(2,1)S(1)} collective-permute-done((bf16[128,256]{1,0:T(8,128)(2,1)S(1)}, bf16[128,256]{1,0:T(8,128)(2,1)S(1)}, u32[]{:S(2)}, u32[]{:S(2)}) %collective-permute-start.19) | collective-permute-done | bytes 65568 | tf_op jit(solution)/shard_map/ppermute | solution.py:249
  64.2 1.6 %shard_map.72 = (f32[128,256]{1,0:T(8,128)S(1)}, s16[264,128]{1,0:T(8,128)(2,1)S(1)}, s16[264,128]{1,0:T(8,128)(2,1)S(1)}, s16[264,128]{1,0:T(8,128)(2,1)S(1)}) custom-call(bf16[128,768]{1,0:T(8,128)(2,1)S(1)} %get-tuple-element.35.refs_0_, bf16[128,768]{1,0:T(8,128)(2,1)S(1)} %collective-permute-done.refs_1_, ...), custom_call_target="tpu_custom_call" | custom-call | flops 536870912 | bytes 1 | tf_op jit(solution)/shard_map/pallas_call | solution.py:298
  65.8 1.3 %collective-permute-start.21 = (s16[264,128]{1,0:T(8,128)(2,1)S(1)}, s16[264,128]{1,0:T(8,128)(2,1)S(1)}, u32[]{:S(2)}, u32[]{:S(2)}) collective-permute-start(s16[264,128]{1,0:T(8,128)(2,1)S(1)} %get-tuple-element.56), channel_id=1, source_target_pairs={{0,1},{1,0},{2,3},{3,2},{4,5},{5,4},{6,7},{7,6},{8,9},{9,8},{10,11... | collective-permute-start | bytes 202760 | tf_op jit(solution)/shard_map/ppermute | solution.py:249
  67.1 1.7 %collective-permute-start.22 = (s16[264,128]{1,0:T(8,128)(2,1)S(1)}, s16[264,128]{1,0:T(8,128)(2,1)S(1)}, u32[]{:S(2)}, u32[]{:S(2)}) collective-permute-start(s16[264,128]{1,0:T(8,128)(2,1)S(1)} %get-tuple-element.57), channel_id=1, source_target_pairs={{0,2},{1,3},{2,0},{3,1},{4,6},{5,7},{6,4},{7,5},{8,10},{9,11},{10,... | collective-permute-start | bytes 202760 | tf_op jit(solution)/shard_map/ppermute | solution.py:249
  68.8 1.4 %collective-permute-start.23 = (s16[264,128]{1,0:T(8,128)(2,1)S(1)}, s16[264,128]{1,0:T(8,128)(2,1)S(1)}, u32[]{:S(2)}, u32[]{:S(2)}) collective-permute-start(s16[264,128]{1,0:T(8,128)(2,1)S(1)} %get-tuple-element.58), channel_id=1, source_target_pairs={{0,3},{1,2},{2,1},{3,0},{4,7},{5,6},{6,5},{7,4},{8,11},{9,10},{10,... | collective-permute-start | bytes 202760 | tf_op jit(solution)/shard_map/ppermute | solution.py:249
  70.2 0.3 collective-permute-done.21.rest_1_
  70.6 3.0 %collective-permute-done.22.rest_2_ = s16[264,128]{1,0:T(8,128)(2,1)S(1)} collective-permute-done((s16[264,128]{1,0:T(8,128)(2,1)S(1)}, s16[264,128]{1,0:T(8,128)(2,1)S(1)}, u32[]{:S(2)}, u32[]{:S(2)}) %collective-permute-start.22) | collective-permute-done | bytes 67616 | tf_op jit(solution)/shard_map/ppermute | solution.py:249
  73.6 1.4 %collective-permute-done.23.rest_3_ = s16[264,128]{1,0:T(8,128)(2,1)S(1)} collective-permute-done((s16[264,128]{1,0:T(8,128)(2,1)S(1)}, s16[264,128]{1,0:T(8,128)(2,1)S(1)}, u32[]{:S(2)}, u32[]{:S(2)}) %collective-permute-start.23) | collective-permute-done | bytes 67616 | tf_op jit(solution)/shard_map/ppermute | solution.py:249
  75.5 1.5 %collective-permute-start.16 = (s16[2,264,128]{2,1,0:T(8,128)(2,1)S(1)}, s16[2,264,128]{2,1,0:T(8,128)(2,1)S(1)}, u32[]{:S(2)}, u32[]{:S(2)}) collective-permute-start(s16[2,264,128]{2,1,0:T(8,128)(2,1)S(1)} %get-tuple-element.48), channel_id=1, source_target_pairs={{0,16},{4,20},{8,24},{12,28},{16,0},{20,4},{24,8},{28,12},{1,17},{... | collective-permute-start | bytes 405512 | tf_op jit(solution)/shard_map/ppermute | solution.py:329
  77.5 1.6 %collective-permute-start.25 = (s16[264,128]{1,0:T(8,128)(2,1)S(1)}, s16[264,128]{1,0:T(8,128)(2,1)S(1)}, u32[]{:S(2)}, u32[]{:S(2)}) collective-permute-start(s16[264,128]{1,0:T(8,128)(2,1)S(1)} %get-tuple-element.62), channel_id=1, source_target_pairs={{0,8},{4,12},{8,0},{12,4},{16,24},{20,28},{24,16},{28,20},{1,9},{5... | collective-permute-start | bytes 202760 | tf_op jit(solution)/shard_map/ppermute | solution.py:338
  79.1 0.7 collective-permute-start.26
  79.7 1.3 %collective-permute-start.27 = (s16[264,128]{1,0:T(8,128)(2,1)S(1)}, s16[264,128]{1,0:T(8,128)(2,1)S(1)}, u32[]{:S(2)}, u32[]{:S(2)}) collective-permute-start(s16[264,128]{1,0:T(8,128)(2,1)S(1)} %get-tuple-element.64), channel_id=1, source_target_pairs={{0,24},{4,28},{8,16},{12,20},{16,8},{20,12},{24,0},{28,4},{1,25},{... | collective-permute-start | bytes 202760 | tf_op jit(solution)/shard_map/ppermute | solution.py:338
  81.0 0.6 collective-permute-done.16.second
  81.8 2.0 %collective-permute-start.17 = (s16[1,264,128]{2,1,0:T(8,128)(2,1)S(1)}, s16[1,264,128]{2,1,0:T(8,128)(2,1)S(1)}, u32[]{:S(2)}, u32[]{:S(2)}) collective-permute-start(s16[1,264,128]{2,1,0:T(8,128)(2,1)S(1)} %get-tuple-element.50), channel_id=1, source_target_pairs={{0,8},{4,12},{8,0},{12,4},{16,24},{20,28},{24,16},{28,20},{1,9},{5... | collective-permute-start | bytes 202760 | tf_op jit(solution)/shard_map/ppermute | solution.py:329
  83.8 0.3 collective-permute-done.26.refs_4_
  84.1 0.9 %collective-permute-done.27.refs_5_ = s16[264,128]{1,0:T(8,128)(2,1)S(1)} collective-permute-done((s16[264,128]{1,0:T(8,128)(2,1)S(1)}, s16[264,128]{1,0:T(8,128)(2,1)S(1)}, u32[]{:S(2)}, u32[]{:S(2)}) %collective-permute-start.27) | collective-permute-done | bytes 67616 | tf_op jit(solution)/shard_map/ppermute | solution.py:338
  85.0 1.2 %collective-permute-done.17.refs_1_ = s16[1,264,128]{2,1,0:T(8,128)(2,1)S(1)} collective-permute-done((s16[1,264,128]{2,1,0:T(8,128)(2,1)S(1)}, s16[1,264,128]{2,1,0:T(8,128)(2,1)S(1)}, u32[]{:S(2)}, u32[]{:S(2)}) %collective-permute-start.17) | collective-permute-done | bytes 67616 | tf_op jit(solution)/shard_map/ppermute | solution.py:329
  86.2 0.8 shard_map.75
  (28 shorter events, 1.8 us)
Async XLA Ops:
  0.0 0.9 %copy-start = (f32[1,128,512]{2,1,0:T(8,128)S(1)}, f32[1,128,512]{2,1,0:T(8,128)}, u32[]{:S(2)}) copy-start(f32[1,128,512]{2,1,0:T(8,128)} %param.6) | copy-start | bytes 786436
  1.1 10.5 %collective-permute-start.6 = (s16[520,128]{1,0:T(8,128)(2,1)S(1)}, s16[520,128]{1,0:T(8,128)(2,1)S(1)}, u32[]{:S(2)}, u32[]{:S(2)}) collective-permute-start(s16[520,128]{1,0:T(8,128)(2,1)S(1)} %shard_map.65.rest_0_), channel_id=1, source_target_pairs={{0,2},{1,3},{2,0},{3,1},{4,6},{5,7},{6,4},{7,5},{8,10},{9,11},{10,... | collective-permute-start | bytes 399368 | tf_op jit(solution)/shard_map/ppermute | solution.py:275
  5.2 9.4 %collective-permute-start.5 = (s16[520,128]{1,0:T(8,128)(2,1)S(1)}, s16[520,128]{1,0:T(8,128)(2,1)S(1)}, u32[]{:S(2)}, u32[]{:S(2)}) collective-permute-start(s16[520,128]{1,0:T(8,128)(2,1)S(1)} %shard_map.65.rest_0_), channel_id=1, source_target_pairs={{0,24},{4,28},{8,16},{12,20},{16,8},{20,12},{24,0},{28,4},{1,25},{... | collective-permute-start | bytes 399368 | tf_op jit(solution)/shard_map/ppermute | solution.py:279
  7.7 7.4 %collective-permute-start.4 = (s16[520,128]{1,0:T(8,128)(2,1)S(1)}, s16[520,128]{1,0:T(8,128)(2,1)S(1)}, u32[]{:S(2)}, u32[]{:S(2)}) collective-permute-start(s16[520,128]{1,0:T(8,128)(2,1)S(1)} %shard_map.65.rest_0_), channel_id=1, source_target_pairs={{0,16},{4,20},{8,24},{12,28},{16,0},{20,4},{24,8},{28,12},{1,17},{... | collective-permute-start | bytes 399368 | tf_op jit(solution)/shard_map/ppermute | solution.py:279
  8.2 6.9 %collective-permute-start.3 = (s16[520,128]{1,0:T(8,128)(2,1)S(1)}, s16[520,128]{1,0:T(8,128)(2,1)S(1)}, u32[]{:S(2)}, u32[]{:S(2)}) collective-permute-start(s16[520,128]{1,0:T(8,128)(2,1)S(1)} %shard_map.65.rest_0_), channel_id=1, source_target_pairs={{0,8},{4,12},{8,0},{12,4},{16,24},{20,28},{24,16},{28,20},{1,9},{5... | collective-permute-start | bytes 399368 | tf_op jit(solution)/shard_map/ppermute | solution.py:279
  11.6 6.8 %collective-permute-start.9 = (s16[520,128]{1,0:T(8,128)(2,1)S(1)}, s16[520,128]{1,0:T(8,128)(2,1)S(1)}, u32[]{:S(2)}, u32[]{:S(2)}) collective-permute-start(s16[520,128]{1,0:T(8,128)(2,1)S(1)} %collective-permute-done.6.rest_4_), channel_id=1, source_target_pairs={{0,24},{4,28},{8,16},{12,20},{16,8},{20,12},{24,0},{28,4},{1,25},{... | collective-permute-start | bytes 399368 | tf_op jit(solution)/shard_map/ppermute | solution.py:279
  14.1 6.0 %collective-permute-start.8 = (s16[520,128]{1,0:T(8,128)(2,1)S(1)}, s16[520,128]{1,0:T(8,128)(2,1)S(1)}, u32[]{:S(2)}, u32[]{:S(2)}) collective-permute-start(s16[520,128]{1,0:T(8,128)(2,1)S(1)} %collective-permute-done.6.rest_4_), channel_id=1, source_target_pairs={{0,16},{4,20},{8,24},{12,28},{16,0},{20,4},{24,8},{28,12},{1,17},{... | collective-permute-start | bytes 399368 | tf_op jit(solution)/shard_map/ppermute | solution.py:279
  14.6 5.5 %collective-permute-start.7 = (s16[520,128]{1,0:T(8,128)(2,1)S(1)}, s16[520,128]{1,0:T(8,128)(2,1)S(1)}, u32[]{:S(2)}, u32[]{:S(2)}) collective-permute-start(s16[520,128]{1,0:T(8,128)(2,1)S(1)} %collective-permute-done.6.rest_4_), channel_id=1, source_target_pairs={{0,8},{4,12},{8,0},{12,4},{16,24},{20,28},{24,16},{28,20},{1,9},{5... | collective-permute-start | bytes 399368 | tf_op jit(solution)/shard_map/ppermute | solution.py:279
  20.1 0.7 copy-start.1
  20.9 2.0 %collective-permute-start.10 = (s16[4,520,128]{2,1,0:T(8,128)(2,1)S(1)}, s16[4,520,128]{2,1,0:T(8,128)(2,1)S(1)}, u32[]{:S(2)}, u32[]{:S(2)}) collective-permute-start(s16[4,520,128]{2,1,0:T(8,128)(2,1)S(1)} %shard_map.66), channel_id=1, source_target_pairs={{0,4},{4,0},{8,12},{12,8},{16,20},{20,16},{24,28},{28,24},{1,5},{5... | collective-permute-start | bytes 1597448 | tf_op jit(solution)/shard_map/ppermute | solution.py:286
  23.2 23.9 %collective-permute-start.11 = (s16[2,520,128]{2,1,0:T(8,128)(2,1)S(1)}, s16[2,520,128]{2,1,0:T(8,128)(2,1)S(1)}, u32[]{:S(2)}, u32[]{:S(2)}) collective-permute-start(s16[2,520,128]{2,1,0:T(8,128)(2,1)S(1)} %get-tuple-element.40), channel_id=1, source_target_pairs={{0,1},{1,0},{2,3},{3,2},{4,5},{5,4},{6,7},{7,6},{8,9},{9,8},{10,11... | collective-permute-start | bytes 798728 | tf_op jit(solution)/shard_map/ppermute | solution.py:292
  24.8 0.7 copy-start.3
  25.4 34.5 %copy-start.2 = (s32[32,1]{0,1:T(1,128)S(1)}, s32[32,1]{0,1:T(1,128)}, u32[]{:S(2)}) copy-start(s32[32,1]{0,1:T(1,128)} %param.10) | copy-start | bytes 388
  26.9 13.2 %collective-permute-start = (bf16[128,768]{1,0:T(8,128)(2,1)S(1)}, bf16[128,768]{1,0:T(8,128)(2,1)S(1)}, u32[]{:S(2)}, u32[]{:S(2)}) collective-permute-start(bf16[128,768]{1,0:T(8,128)(2,1)S(1)} %get-tuple-element.36), channel_id=1, source_target_pairs={{0,1},{1,0},{2,3},{3,2},{4,5},{5,4},{6,7},{7,6},{8,9},{9,8},{10,11... | collective-permute-start | bytes 589832 | tf_op jit(solution)/shard_map/ppermute | solution.py:249
  27.5 12.6 %collective-permute-start.1 = (bf16[128,768]{1,0:T(8,128)(2,1)S(1)}, bf16[128,768]{1,0:T(8,128)(2,1)S(1)}, u32[]{:S(2)}, u32[]{:S(2)}) collective-permute-start(bf16[128,768]{1,0:T(8,128)(2,1)S(1)} %get-tuple-element.37), channel_id=1, source_target_pairs={{0,2},{1,3},{2,0},{3,1},{4,6},{5,7},{6,4},{7,5},{8,10},{9,11},{10,... | collective-permute-start | bytes 589832 | tf_op jit(solution)/shard_map/ppermute | solution.py:249
  30.5 16.6 %collective-permute-start.2 = (bf16[128,768]{1,0:T(8,128)(2,1)S(1)}, bf16[128,768]{1,0:T(8,128)(2,1)S(1)}, u32[]{:S(2)}, u32[]{:S(2)}) collective-permute-start(bf16[128,768]{1,0:T(8,128)(2,1)S(1)} %get-tuple-element.38), channel_id=1, source_target_pairs={{0,3},{1,2},{2,1},{3,0},{4,7},{5,6},{6,5},{7,4},{8,11},{9,10},{10,... | collective-permute-start | bytes 589832 | tf_op jit(solution)/shard_map/ppermute | solution.py:249
  48.7 8.4 %collective-permute-start.12 = (s16[264,128]{1,0:T(8,128)(2,1)S(1)}, s16[264,128]{1,0:T(8,128)(2,1)S(1)}, u32[]{:S(2)}, u32[]{:S(2)}) collective-permute-start(s16[264,128]{1,0:T(8,128)(2,1)S(1)} %get-tuple-element.42), channel_id=1, source_target_pairs={{0,1},{1,0},{2,3},{3,2},{4,5},{5,4},{6,7},{7,6},{8,9},{9,8},{10,11... | collective-permute-start | bytes 202760 | tf_op jit(solution)/shard_map/ppermute | solution.py:249
  50.7 7.8 %collective-permute-start.13 = (s16[264,128]{1,0:T(8,128)(2,1)S(1)}, s16[264,128]{1,0:T(8,128)(2,1)S(1)}, u32[]{:S(2)}, u32[]{:S(2)}) collective-permute-start(s16[264,128]{1,0:T(8,128)(2,1)S(1)} %get-tuple-element.43), channel_id=1, source_target_pairs={{0,2},{1,3},{2,0},{3,1},{4,6},{5,7},{6,4},{7,5},{8,10},{9,11},{10,... | collective-permute-start | bytes 202760 | tf_op jit(solution)/shard_map/ppermute | solution.py:249
  52.7 7.3 %collective-permute-start.14 = (s16[264,128]{1,0:T(8,128)(2,1)S(1)}, s16[264,128]{1,0:T(8,128)(2,1)S(1)}, u32[]{:S(2)}, u32[]{:S(2)}) collective-permute-start(s16[264,128]{1,0:T(8,128)(2,1)S(1)} %get-tuple-element.44), channel_id=1, source_target_pairs={{0,3},{1,2},{2,1},{3,0},{4,7},{5,6},{6,5},{7,4},{8,11},{9,10},{10,... | collective-permute-start | bytes 202760 | tf_op jit(solution)/shard_map/ppermute | solution.py:249
  54.1 6.2 %collective-permute-start.18 = (bf16[128,256]{1,0:T(8,128)(2,1)S(1)}, bf16[128,256]{1,0:T(8,128)(2,1)S(1)}, u32[]{:S(2)}, u32[]{:S(2)}) collective-permute-start(bf16[128,256]{1,0:T(8,128)(2,1)S(1)} %get-tuple-element.52), channel_id=1, source_target_pairs={{0,1},{1,0},{2,3},{3,2},{4,5},{5,4},{6,7},{7,6},{8,9},{9,8},{10,11... | collective-permute-start | bytes 196616 | tf_op jit(solution)/shard_map/ppermute | solution.py:249
  54.7 9.5 %collective-permute-start.19 = (bf16[128,256]{1,0:T(8,128)(2,1)S(1)}, bf16[128,256]{1,0:T(8,128)(2,1)S(1)}, u32[]{:S(2)}, u32[]{:S(2)}) collective-permute-start(bf16[128,256]{1,0:T(8,128)(2,1)S(1)} %get-tuple-element.53), channel_id=1, source_target_pairs={{0,2},{1,3},{2,0},{3,1},{4,6},{5,7},{6,4},{7,5},{8,10},{9,11},{10,... | collective-permute-start | bytes 196616 | tf_op jit(solution)/shard_map/ppermute | solution.py:249
  57.1 7.1 %collective-permute-start.20 = (bf16[128,256]{1,0:T(8,128)(2,1)S(1)}, bf16[128,256]{1,0:T(8,128)(2,1)S(1)}, u32[]{:S(2)}, u32[]{:S(2)}) collective-permute-start(bf16[128,256]{1,0:T(8,128)(2,1)S(1)} %get-tuple-element.54), channel_id=1, source_target_pairs={{0,3},{1,2},{2,1},{3,0},{4,7},{5,6},{6,5},{7,4},{8,11},{9,10},{10,... | collective-permute-start | bytes 196616 | tf_op jit(solution)/shard_map/ppermute | solution.py:249
  60.2 15.1 %collective-permute-start.15 = (f32[4,128,256]{2,1,0:T(8,128)S(1)}, f32[4,128,256]{2,1,0:T(8,128)S(1)}, u32[]{:S(2)}, u32[]{:S(2)}) collective-permute-start(f32[4,128,256]{2,1,0:T(8,128)S(1)} %get-tuple-element.46), channel_id=1, source_target_pairs={{0,4},{4,0},{8,12},{12,8},{16,20},{20,16},{24,28},{28,24},{1,5},{5... | collective-permute-start | bytes 1572872 | tf_op jit(solution)/shard_map/ppermute | solution.py:317
  65.8 4.8 %collective-permute-start.21 = (s16[264,128]{1,0:T(8,128)(2,1)S(1)}, s16[264,128]{1,0:T(8,128)(2,1)S(1)}, u32[]{:S(2)}, u32[]{:S(2)}) collective-permute-start(s16[264,128]{1,0:T(8,128)(2,1)S(1)} %get-tuple-element.56), channel_id=1, source_target_pairs={{0,1},{1,0},{2,3},{3,2},{4,5},{5,4},{6,7},{7,6},{8,9},{9,8},{10,11... | collective-permute-start | bytes 202760 | tf_op jit(solution)/shard_map/ppermute | solution.py:249
  67.1 6.5 %collective-permute-start.22 = (s16[264,128]{1,0:T(8,128)(2,1)S(1)}, s16[264,128]{1,0:T(8,128)(2,1)S(1)}, u32[]{:S(2)}, u32[]{:S(2)}) collective-permute-start(s16[264,128]{1,0:T(8,128)(2,1)S(1)} %get-tuple-element.57), channel_id=1, source_target_pairs={{0,2},{1,3},{2,0},{3,1},{4,6},{5,7},{6,4},{7,5},{8,10},{9,11},{10,... | collective-permute-start | bytes 202760 | tf_op jit(solution)/shard_map/ppermute | solution.py:249
  68.8 6.2 %collective-permute-start.23 = (s16[264,128]{1,0:T(8,128)(2,1)S(1)}, s16[264,128]{1,0:T(8,128)(2,1)S(1)}, u32[]{:S(2)}, u32[]{:S(2)}) collective-permute-start(s16[264,128]{1,0:T(8,128)(2,1)S(1)} %get-tuple-element.58), channel_id=1, source_target_pairs={{0,3},{1,2},{2,1},{3,0},{4,7},{5,6},{6,5},{7,4},{8,11},{9,10},{10,... | collective-permute-start | bytes 202760 | tf_op jit(solution)/shard_map/ppermute | solution.py:249
  75.3 2.0 %collective-permute-start.24 = (f32[4,128,256]{2,1,0:T(8,128)S(1)}, f32[4,128,256]{2,1,0:T(8,128)S(1)}, u32[]{:S(2)}, u32[]{:S(2)}) collective-permute-start(f32[4,128,256]{2,1,0:T(8,128)S(1)} %get-tuple-element.60), channel_id=1, source_target_pairs={{0,4},{4,0},{8,12},{12,8},{16,20},{20,16},{24,28},{28,24},{1,5},{5... | collective-permute-start | bytes 1572872 | tf_op jit(solution)/shard_map/ppermute | solution.py:317
  75.5 6.1 %collective-permute-start.16 = (s16[2,264,128]{2,1,0:T(8,128)(2,1)S(1)}, s16[2,264,128]{2,1,0:T(8,128)(2,1)S(1)}, u32[]{:S(2)}, u32[]{:S(2)}) collective-permute-start(s16[2,264,128]{2,1,0:T(8,128)(2,1)S(1)} %get-tuple-element.48), channel_id=1, source_target_pairs={{0,16},{4,20},{8,24},{12,28},{16,0},{20,4},{24,8},{28,12},{1,17},{... | collective-permute-start | bytes 405512 | tf_op jit(solution)/shard_map/ppermute | solution.py:329
  77.5 6.3 %collective-permute-start.25 = (s16[264,128]{1,0:T(8,128)(2,1)S(1)}, s16[264,128]{1,0:T(8,128)(2,1)S(1)}, u32[]{:S(2)}, u32[]{:S(2)}) collective-permute-start(s16[264,128]{1,0:T(8,128)(2,1)S(1)} %get-tuple-element.62), channel_id=1, source_target_pairs={{0,8},{4,12},{8,0},{12,4},{16,24},{20,28},{24,16},{28,20},{1,9},{5... | collective-permute-start | bytes 202760 | tf_op jit(solution)/shard_map/ppermute | solution.py:338
  79.1 5.0 %collective-permute-start.26 = (s16[264,128]{1,0:T(8,128)(2,1)S(1)}, s16[264,128]{1,0:T(8,128)(2,1)S(1)}, u32[]{:S(2)}, u32[]{:S(2)}) collective-permute-start(s16[264,128]{1,0:T(8,128)(2,1)S(1)} %get-tuple-element.63), channel_id=1, source_target_pairs={{0,16},{4,20},{8,24},{12,28},{16,0},{20,4},{24,8},{28,12},{1,17},{... | collective-permute-start | bytes 202760 | tf_op jit(solution)/shard_map/ppermute | solution.py:338
  79.7 5.2 %collective-permute-start.27 = (s16[264,128]{1,0:T(8,128)(2,1)S(1)}, s16[264,128]{1,0:T(8,128)(2,1)S(1)}, u32[]{:S(2)}, u32[]{:S(2)}) collective-permute-start(s16[264,128]{1,0:T(8,128)(2,1)S(1)} %get-tuple-element.64), channel_id=1, source_target_pairs={{0,24},{4,28},{8,16},{12,20},{16,8},{20,12},{24,0},{28,4},{1,25},{... | collective-permute-start | bytes 202760 | tf_op jit(solution)/shard_map/ppermute | solution.py:338
  81.8 4.4 %collective-permute-start.17 = (s16[1,264,128]{2,1,0:T(8,128)(2,1)S(1)}, s16[1,264,128]{2,1,0:T(8,128)(2,1)S(1)}, u32[]{:S(2)}, u32[]{:S(2)}) collective-permute-start(s16[1,264,128]{2,1,0:T(8,128)(2,1)S(1)} %get-tuple-element.50), channel_id=1, source_target_pairs={{0,8},{4,12},{8,0},{12,4},{16,24},{20,28},{24,16},{28,20},{1,9},{5... | collective-permute-start | bytes 202760 | tf_op jit(solution)/shard_map/ppermute | solution.py:329
